TPU v7x, 16 devices: a whole 2x2x2 slice. The times are simulated.
16 devices in a mesh: dp: 4 (over z, y), tp: 4 (over x, core).
Axes of the slice: x: 2, y: 2, z: 2, core: 2. Of those that a mesh axis runs over, the one named last changes fastest.
Arguments:
- x_in: bfloat16 [32, 1024, 768], P('dp', 'tp'), parts along dimension 0
- cond_vec: bfloat16 [32, 768], P('dp'), parts along dimension 0
- rope_cos: float32 [1024, 32], P('tp')
- rope_sin: float32 [1024, 32], P('tp')
- w_mod: bfloat16 [2, 768, 2304], replicated
- b_mod: bfloat16 [2, 2304], replicated
- w_in: bfloat16 [2, 768, 12, 448], P(None, None, 'tp')
- b_in: bfloat16 [2, 12, 448], P(None, 'tp')
- q_scale: bfloat16 [2, 64], replicated
- k_scale: bfloat16 [2, 64], replicated
- w_out: bfloat16 [2, 12, 320, 768], P(None, 'tp')
- b_out: bfloat16 [2, 768], replicated
- d_out: bfloat16 [32, 1024, 768], P('dp', 'tp'), parts along dimension 0
Outputs:
- output 1: bfloat16 [32, 1024, 768], P('dp', 'tp'), parts along dimension 0
- output 2: bfloat16 [32, 1024, 768], P('dp', 'tp'), parts along dimension 0
- output 3: float32 [8, 768, 2304], P('dp'), parts along dimension 0
- output 4: float32 [8, 2304], P('dp'), parts along dimension 0
- output 5: bfloat16 [8, 768, 12, 448], P('dp', None, 'tp'), parts along dimension 0
- output 6: float32 [8, 12, 448], P('dp', 'tp'), parts along dimension 0
- output 7: float32 [8, 64], P('dp'), parts along dimension 0
- output 8: float32 [8, 64], P('dp'), parts along dimension 0
- output 9: bfloat16 [8, 12, 320, 768], P('dp', 'tp'), parts along dimension 0
- output 10: float32 [8, 768], P('dp'), parts along dimension 0
There are 4 independent parts. A program takes and returns all parts, laid end to end along the dimension named above; an argument that names none is the same for every part.
All inputs are finite; a program needn't handle non-finite values.
Results may differ from a plain program's by a relative error of at most 0.02.
Values are sent between devices in bfloat16 or wider.
A program may use at most 1 GiB of HBM per device.

v0:
```python
import functools
import jax
import jax.numpy as jnp
from jax import lax
from jax.sharding import PartitionSpec as P

NORM_EPS = 1e-6


def rms_norm(tensor):
    return tensor * lax.rsqrt(jnp.mean(tensor * tensor, axis=-1, keepdims=True) + NORM_EPS)


def apply_rope(tensor, rope_cos, rope_sin):
    pair_view = tensor.reshape(tensor.shape[:-1] + (tensor.shape[-1] // 2, 2))
    even_part = pair_view[..., 0]
    odd_part = pair_view[..., 1]
    cos_wide = rope_cos[None, :, None, :]
    sin_wide = rope_sin[None, :, None, :]
    rotated = jnp.stack([even_part * cos_wide - odd_part * sin_wide, even_part * sin_wide + odd_part * cos_wide], axis=-1)
    return rotated.reshape(tensor.shape)


def layer_modulate(x_f32, mod_shift, mod_scale):
    row_mean = jnp.mean(x_f32, axis=-1, keepdims=True)
    centered = x_f32 - row_mean
    row_var = jnp.mean(centered * centered, axis=-1, keepdims=True)
    normed = centered * lax.rsqrt(row_var + NORM_EPS)
    return (normed * (1.0 + mod_scale[:, None, :]) + mod_shift[:, None, :]).astype(jnp.bfloat16)


def mix_heads(projected, q_scale, k_scale, rope_cos, rope_sin):
    head_dim = q_scale.shape[-1]
    q_rot = apply_rope(rms_norm(projected[..., :head_dim]) * q_scale, rope_cos, rope_sin).astype(jnp.bfloat16)
    k_rot = apply_rope(rms_norm(projected[..., head_dim:2 * head_dim]) * k_scale, rope_cos, rope_sin).astype(jnp.bfloat16)
    v_part = projected[..., 2 * head_dim:3 * head_dim].astype(jnp.bfloat16)
    scores = jnp.einsum("bqhe,bkhe->bhqk", q_rot, k_rot, preferred_element_type=jnp.float32) * (head_dim ** -0.5)
    attn_probs = jax.nn.softmax(scores, axis=-1).astype(jnp.bfloat16)
    attn_out = jnp.einsum("bhqk,bkhe->bqhe", attn_probs, v_part, preferred_element_type=jnp.float32).astype(jnp.bfloat16)
    mlp_act = jax.nn.gelu(projected[..., 3 * head_dim:], approximate=True).astype(jnp.bfloat16)
    return jnp.concatenate([attn_out, mlp_act], axis=-1)


def solution(mesh):
    act_spec = P("dp", "tp", None)
    in_specs = (act_spec, P("dp", None), P("tp", None), P("tp", None), P(None, None, None), P(None, None), P(None, None, "tp", None), P(None, "tp", None), P(None, None), P(None, None), P(None, "tp", None, None), P(None, None), act_spec)
    out_specs = (act_spec, act_spec, P("dp", None, None), P("dp", None), P("dp", None, "tp", None), P("dp", "tp", None), P("dp", None), P("dp", None), P("dp", "tp", None, None), P("dp", None))

    def device_fn(x_in, cond_vec, rope_cos, rope_sin, w_mod, b_mod, w_in, b_in, q_scale, k_scale, w_out, b_out, d_out):
        num_blocks = w_in.shape[0]
        cos_full = lax.all_gather(rope_cos, "tp", axis=0, tiled=True)
        sin_full = lax.all_gather(rope_sin, "tp", axis=0, tiled=True)
        core_fn = functools.partial(mix_heads, rope_cos=cos_full, rope_sin=sin_full)
        silu_vec = jax.nn.silu(cond_vec.astype(jnp.float32)).astype(jnp.bfloat16)
        saved_acts = []
        x_cur = x_in
        for block_idx in range(num_blocks):
            mod_vec = jnp.dot(silu_vec, w_mod[block_idx], preferred_element_type=jnp.float32) + b_mod[block_idx].astype(jnp.float32)
            mod_shift, mod_scale, mod_gate = jnp.split(mod_vec, 3, axis=-1)
            x_f32 = x_cur.astype(jnp.float32)
            normed = layer_modulate(x_f32, mod_shift, mod_scale)
            normed_full = lax.all_gather(normed, "tp", axis=1, tiled=True)
            projected = jnp.einsum("bsd,dhc->bshc", normed_full, w_in[block_idx], preferred_element_type=jnp.float32) + b_in[block_idx].astype(jnp.float32)
            joined = core_fn(projected, q_scale[block_idx].astype(jnp.float32), k_scale[block_idx].astype(jnp.float32))
            part_out = jnp.einsum("bshc,hcd->bsd", joined, w_out[block_idx], preferred_element_type=jnp.float32)
            mixed_out = lax.psum_scatter(part_out.astype(jnp.bfloat16), "tp", scatter_dimension=1, tiled=True)
            branch = mixed_out.astype(jnp.float32) + b_out[block_idx].astype(jnp.float32)
            saved_acts.append((x_f32, mod_vec, normed_full, projected, joined, branch))
            x_cur = (x_f32 + mod_gate[:, None, :] * branch).astype(jnp.bfloat16)
        x_out = x_cur

        silu_f32 = silu_vec.astype(jnp.float32)
        grad_cur = d_out
        block_grads = {}
        for block_idx in reversed(range(num_blocks)):
            x_f32, mod_vec, normed_full, projected, joined, branch = saved_acts[block_idx]
            mod_shift, mod_scale, mod_gate = jnp.split(mod_vec, 3, axis=-1)
            qs_f32 = q_scale[block_idx].astype(jnp.float32)
            ks_f32 = k_scale[block_idx].astype(jnp.float32)
            grad_f32 = grad_cur.astype(jnp.float32)
            d_gate = jnp.sum(grad_f32 * branch, axis=1)
            gated_grad = grad_f32 * mod_gate[:, None, :]
            d_bout = lax.psum(jnp.sum(gated_grad, axis=(0, 1)), "tp")
            d_branch = lax.all_gather(gated_grad.astype(jnp.bfloat16), "tp", axis=1, tiled=True)
            g_wout = jnp.einsum("bshc,bsd->hcd", joined, d_branch, preferred_element_type=jnp.float32).astype(jnp.bfloat16)
            d_joined = jnp.einsum("bsd,hcd->bshc", d_branch, w_out[block_idx], preferred_element_type=jnp.float32).astype(jnp.bfloat16)
            unused_out, core_pull = jax.vjp(core_fn, projected, qs_f32, ks_f32)
            d_proj, d_qs, d_ks = core_pull(d_joined)
            g_bin = jnp.sum(d_proj, axis=(0, 1))
            d_proj16 = d_proj.astype(jnp.bfloat16)
            g_win = jnp.einsum("bsd,bshc->dhc", normed_full, d_proj16, preferred_element_type=jnp.float32).astype(jnp.bfloat16)
            d_norm_part = jnp.einsum("bshc,dhc->bsd", d_proj16, w_in[block_idx], preferred_element_type=jnp.float32)
            d_normed = lax.psum_scatter(d_norm_part.astype(jnp.bfloat16), "tp", scatter_dimension=1, tiled=True)
            unused_norm, norm_pull = jax.vjp(layer_modulate, x_f32, mod_shift, mod_scale)
            d_xnorm, d_shift, d_scale = norm_pull(d_normed)
            d_mod = lax.psum(jnp.concatenate([d_shift, d_scale, d_gate], axis=-1), "tp")
            g_wmod = jnp.einsum("bd,bm->dm", silu_f32, d_mod, preferred_element_type=jnp.float32)
            block_grads[block_idx] = (g_wmod, jnp.sum(d_mod, axis=0), g_win, g_bin, lax.psum(d_qs, "tp"), lax.psum(d_ks, "tp"), g_wout, d_bout)
            grad_cur = (grad_f32 + d_xnorm).astype(jnp.bfloat16)
        stacked = tuple(jnp.stack([block_grads[block_idx][entry_idx] for block_idx in range(num_blocks)]) for entry_idx in range(8))
        return (x_out, grad_cur) + stacked

    return jax.shard_map(device_fn, mesh=mesh, in_specs=in_specs, out_specs=out_specs, check_vma=False)
```

profile of v0, /device:TPU:0, one launch (start us, length us, event | category | flops | bytes accessed | tf_op | source)
XLA Modules:
  0.0 1946.2 jit_solution(1262558229248344001)
XLA Ops:
  34.5 69.2 %all-gather.5.cloned.1.call-done = bf16[8,1024,768]{2,1,0:T(8,128)(2,1)} async-done(((bf16[8,256,768]{2,1,0:T(8,128)(2,1)}), bf16[8,1024,768]{2,1,0:T(8,128)(2,1)}) %all-gather.5.cloned.1.call-update) | async-done | bytes 12582928 | tf_op jit(solution)/shard_map/all_gather | solution.py:62
  103.8 28.0 %broadcast_add_fusion.1 = f32[8,1024,3,448]{1,3,2,0:T(8,128)} fusion(f32[3,448]{1,0:T(4,128)S(1)} %bitcast.264, bf16[8,1024,768]{2,1,0:T(8,128)(2,1)} %all-gather.5.cloned.1.call-done, bf16[2,768,3,448]{1,3,2,0:T(8,128)(2,1)} %param.19), kind=kOutput, calls=%fused_computation.69 | convolution fusion | flops 16922443776 | bytes 58692864 | tf_op jit(solution)/shard_map/bsd,dhc->bshc/dot_general | solution.py:63
  137.5 16.2 multiply_convert_fusion.1
  179.2 19.3 subtract_convert_fusion.2
  226.7 39.9 %fusion.184 = (f32[8,3,1024]{2,1,0:T(4,128)S(1)}, f32[8,3,1024,1024]{2,3,1,0:T(8,128)}) fusion(bf16[8,1024,3,64]{1,3,2,0:T(8,128)(2,1)} %convert_element_type.305, bf16[8,1024,3,64]{1,3,2,0:T(8,128)(2,1)S(1)} %copy-done.22), kind=kOutput, calls=%fused_computation.300 | convolution fusion | flops 3296723968 | bytes 107053056 | tf_op jit(solution)/shard_map/sub | solution.py:38
  266.6 48.3 %divide_convert_fusion.1 = bf16[8,3,1024,1024]{2,3,1,0:T(8,128)(2,1)} fusion(f32[8,3,1024,1024]{2,3,1,0:T(8,128)} %get-tuple-element.126, f32[8,3,1024]{2,1,0:T(4,128)S(1)} %get-tuple-element.125), kind=kLoop, calls=%fused_computation.18 | loop fusion | flops 50331648 | bytes 151093248 | tf_op jit(solution)/shard_map/convert_element_type | solution.py:38
  315.0 19.5 %convert_bitcast_fusion.7 = bf16[8,1024,3,64]{1,3,2,0:T(8,128)(2,1)S(1)} fusion(bf16[8,3,1024,1024]{2,3,1,0:T(8,128)(2,1)} %divide_convert_fusion.1, f32[8,1024,3,448]{1,3,2,0:T(8,128)} %broadcast_add_fusion.1), kind=kOutput, calls=%fused_computation.211 | convolution fusion | flops 3222798336 | bytes 56623104 | tf_op jit(solution)/shard_map/bhqk,bkhe->bqhe/dot_general | solution.py:39
  334.5 20.6 %bitcast_convert_fusion.3 = bf16[8,1024,768]{2,1,0:T(8,128)(2,1)} fusion(bf16[8,1024,3,256]{1,3,2,0:T(8,128)(2,1)} %multiply_convert_fusion.1, bf16[8,1024,3,64]{1,3,2,0:T(8,128)(2,1)S(1)} %convert_bitcast_fusion.7, bf16[2,3,320,768]{3,2,1,0:T(8,128)(2,1)} %param.23), kind=kOutput, calls=%fused_computation.61 | convolution fusion | flops 12117344256 | bytes 29786112 | tf_op jit(solution)/shard_map/bshc,hcd->bsd/dot_general | solution.py:65
  364.0 83.6 %reduce-scatter.5.cloned.1.call-done = bf16[8,256,768]{2,1,0:T(8,128)(2,1)} async-done(((bf16[8,1024,768]{2,1,0:T(8,128)(2,1)}), bf16[8,256,768]{2,1,0:T(8,128)(2,1)}) %reduce-scatter.5.cloned.1.call-update) | async-done | bytes 3145744 | tf_op jit(solution)/shard_map/reduce_scatter | solution.py:66
  455.4 74.7 %all-gather.9.cloned.1.call-done = bf16[8,1024,768]{2,1,0:T(8,128)(2,1)} async-done(((bf16[8,256,768]{2,1,0:T(8,128)(2,1)}), bf16[8,1024,768]{2,1,0:T(8,128)(2,1)}) %all-gather.9.cloned.1.call-update) | async-done | bytes 12582928 | tf_op jit(solution)/shard_map/all_gather | solution.py:84
  530.1 20.1 %fusion.65 = bf16[8,1024,3,320]{1,3,2,0:T(8,128)(2,1)} fusion(bf16[8,1024,768]{2,1,0:T(8,128)(2,1)} %all-gather.9.cloned.1.call-done, bf16[2,3,320,768]{3,2,1,0:T(8,128)(2,1)S(1)} %copy-done.100), kind=kOutput, calls=%fused_computation.90 | convolution fusion | flops 12087459840 | bytes 29786112 | tf_op jit(solution)/shard_map/bsd,hcd->bshc/dot_general | solution.py:86
  550.2 62.8 %all-gather.7.cloned.1.call-done = bf16[8,1024,768]{2,1,0:T(8,128)(2,1)} async-done(((bf16[8,256,768]{2,1,0:T(8,128)(2,1)}), bf16[8,1024,768]{2,1,0:T(8,128)(2,1)}) %all-gather.7.cloned.1.call-update) | async-done | bytes 12582928 | tf_op jit(solution)/shard_map/all_gather | solution.py:62
  613.0 28.1 %broadcast_add_fusion = f32[8,1024,3,448]{1,3,2,0:T(8,128)} fusion(f32[3,448]{1,0:T(4,128)S(1)} %bitcast.265, bf16[8,1024,768]{2,1,0:T(8,128)(2,1)} %all-gather.7.cloned.1.call-done, bf16[2,768,3,448]{1,3,2,0:T(8,128)(2,1)} %param.19), kind=kOutput, calls=%fused_computation.68 | convolution fusion | flops 16922443776 | bytes 58692864 | tf_op jit(solution)/shard_map/bsd,dhc->bshc/dot_general | solution.py:63
  673.2 19.5 %subtract_convert_fusion = (bf16[8,1024,3,32,1]{1,4,3,2,0:T(2,128)(2,1)S(1)}, bf16[8,1024,3,32,1]{1,4,3,2,0:T(2,128)(2,1)S(1)}, bf16[8,1024,3,32,1]{1,4,3,2,0:T(2,128)(2,1)S(1)}, bf16[8,1024,3,32,1]{1,4,3,2,0:T(2,128)(2,1)}) fusion(f32[8,1024,3,32,2]{1,4,3,2,0:T(2,128)} %reshape.313, f32[1024,32]{0,1:T(8,128)S(1)} %copy-done.17, ...), kind=kLoop, calls=%fused_computation.208 | loop fusion | flops 12582912 | bytes 19136512 | tf_op jit(solution)/shard_map/convert.24
  721.0 40.0 %fusion.185 = (f32[8,3,1024]{2,1,0:T(4,128)S(1)}, f32[8,3,1024,1024]{2,3,1,0:T(8,128)}) fusion(bf16[8,1024,3,64]{1,3,2,0:T(8,128)(2,1)} %convert_element_type.324, bf16[8,1024,3,64]{1,3,2,0:T(8,128)(2,1)S(1)} %copy-done.24), kind=kOutput, calls=%fused_computation.301 | convolution fusion | flops 3296723968 | bytes 107053056 | tf_op jit(solution)/shard_map/sub | solution.py:38
  761.0 70.0 %fusion.6 = (f32[8,3,1024]{2,1,0:T(4,128)S(1)}, bf16[8,3,1024,1024]{2,3,1,0:T(8,128)(2,1)}, bf16[8,3,1024,1024]{2,3,1,0:T(8,128)(2,1)}) fusion(f32[8,3,1024,1024]{2,3,1,0:T(8,128)} %get-tuple-element.128, f32[8,3,1024]{2,1,0:T(4,128)S(1)} %multiply_divide_fusion.1, f32[8,3,1024]{2,1,0:T(4,128)S(1)} %get-tuple-element.127, ...), kind=kOutput, calls=%fused_computation.10 | convolution fusion | flops 3397361664 | bytes 207912960 | tf_op jit(solution)/shard_map/transpose(jvp(bhqk,bkhe->bqhe))/dot_general | solution.py:39
  831.1 50.9 %convert_bitcast_fusion.2 = f32[8,1024,3,64]{1,3,2,0:T(8,128)} fusion(bf16[8,1024,3,64]{1,3,2,0:T(8,128)(2,1)S(1)} %copy-done.25, f32[8,3,1024,1024]{2,3,1,0:T(8,128)} %get-tuple-element.128, bf16[8,3,1024,1024]{2,3,1,0:T(8,128)(2,1)} %get-tuple-element.129, f32[8,3,1024]{2,1,0:T(4,128)S(1)} %neg.39, f32[8,3,1024]{2,1,0:T(4,128)S(1)} %get-tuple-element.127), kind=kOutput, calls=%fused_computation.151 | convolution fusion | flops 3350200320 | bytes 160628736 | tf_op jit(solution)/shard_map/transpose(jvp(bqhe,bkhe->bhqk))/dot_general | solution.py:37
  882.0 50.9 %convert_bitcast_fusion.3 = f32[8,1024,3,64]{1,3,2,0:T(8,128)} fusion(bf16[8,1024,3,64]{1,3,2,0:T(8,128)(2,1)} %convert_element_type.324, f32[8,3,1024,1024]{2,3,1,0:T(8,128)} %get-tuple-element.128, bf16[8,3,1024,1024]{2,3,1,0:T(8,128)(2,1)} %get-tuple-element.129, f32[8,3,1024]{2,1,0:T(4,128)S(1)} %neg.39, f32[8,3,1024]{2,1,0:T(4,128)S(1)} %get-tuple-element.127), kind=kOutput, calls=%fused_computation.152 | convolution fusion | flops 3350200320 | bytes 160628736 | tf_op jit(solution)/shard_map/transpose(jvp(bqhe,bkhe->bhqk))/dot_general | solution.py:37
  932.9 32.6 %fusion.25 = (f32[8,1024,3,256]{1,3,2,0:T(8,128)}, bf16[8,1024,3,256]{1,3,2,0:T(8,128)(2,1)}) fusion(f32[8,1024,3,448]{1,3,2,0:T(8,128)} %broadcast_add_fusion, bf16[8,1024,3,320]{1,3,2,0:T(8,128)(2,1)} %fusion.65), kind=kLoop, calls=%fused_computation.41 | loop fusion | flops 138412032 | bytes 75497472 | tf_op jit(solution)/shard_map/transpose(jvp())/add_any | solution.py:40
  982.3 18.3 multiply_add_fusion.7
  1037.8 11.1 multiply_reduce_fusion.2
  1049.8 22.1 %convert_bitcast_fusion.5 = bf16[8,1024,3,64]{1,3,2,0:T(8,128)(2,1)S(1)} fusion(bf16[8,3,1024,1024]{2,3,1,0:T(8,128)(2,1)} %get-tuple-element.74, bf16[8,1024,3,320]{1,3,2,0:T(8,128)(2,1)} %fusion.65), kind=kOutput, calls=%fused_computation.205 | convolution fusion | flops 3222798336 | bytes 56623104 | tf_op jit(solution)/shard_map/transpose(jvp(bhqk,bkhe->bqhe))/dot_general | solution.py:39
  1071.9 14.9 add_add_fusion.5
  1086.9 26.9 %bitcast_convert_fusion.1 = bf16[8,1024,768]{2,1,0:T(8,128)(2,1)} fusion(bf16[2,768,3,448]{1,3,2,0:T(8,128)(2,1)} %param.19, f32[8,1024,3,64]{1,3,2,0:T(8,128)} %get-tuple-element.80, f32[8,1024,3,64]{1,3,2,0:T(8,128)} %get-tuple-element.79, bf16[8,1024,3,64]{1,3,2,0:T(8,128)(2,1)S(1)} %convert_bitcast_fusion.5, f32[8,1024,3,256]{1,3,2,0:T(8,128)} %get-tuple-element.77), kind=kOutput, calls=%fused_computation.59 | convolution fusion | flops 16972775424 | bytes 55541760 | tf_op jit(solution)/shard_map/bshc,dhc->bsd/dot_general | solution.py:92
  1113.8 19.8 %convert_bitcast_fusion.6 = bf16[8,1024,3,64]{1,3,2,0:T(8,128)(2,1)S(1)} fusion(bf16[8,3,1024,1024]{2,3,1,0:T(8,128)(2,1)} %get-tuple-element.74, f32[8,1024,3,448]{1,3,2,0:T(8,128)} %broadcast_add_fusion), kind=kOutput, calls=%fused_computation.206 | convolution fusion | flops 3222798336 | bytes 56623104 | tf_op jit(solution)/shard_map/bhqk,bkhe->bqhe/dot_general | solution.py:39
  1133.6 20.7 %bitcast_convert_fusion.2 = bf16[8,1024,768]{2,1,0:T(8,128)(2,1)} fusion(bf16[8,1024,3,256]{1,3,2,0:T(8,128)(2,1)} %get-tuple-element.78, bf16[8,1024,3,64]{1,3,2,0:T(8,128)(2,1)S(1)} %convert_bitcast_fusion.6, bf16[2,3,320,768]{3,2,1,0:T(8,128)(2,1)} %param.23), kind=kOutput, calls=%fused_computation.60 | convolution fusion | flops 12117344256 | bytes 29786112 | tf_op jit(solution)/shard_map/bshc,hcd->bsd/dot_general | solution.py:65
  1154.5 51.8 %reduce-scatter.9.cloned.1.call-done = bf16[8,256,768]{2,1,0:T(8,128)(2,1)} async-done(((bf16[8,1024,768]{2,1,0:T(8,128)(2,1)}), bf16[8,256,768]{2,1,0:T(8,128)(2,1)}) %reduce-scatter.9.cloned.1.call-update) | async-done | bytes 3145744 | tf_op jit(solution)/shard_map/reduce_scatter | solution.py:93
  1215.7 85.5 %reduce-scatter.7.cloned.1.call-done = bf16[8,256,768]{2,1,0:T(8,128)(2,1)} async-done(((bf16[8,1024,768]{2,1,0:T(8,128)(2,1)}), bf16[8,256,768]{2,1,0:T(8,128)(2,1)}) %reduce-scatter.7.cloned.1.call-update) | async-done | bytes 3145744 | tf_op jit(solution)/shard_map/reduce_scatter | solution.py:66
  1301.2 10.5 fusion.76
  1315.9 80.9 %all-gather.11.cloned.1.call-done = bf16[8,1024,768]{2,1,0:T(8,128)(2,1)} async-done(((bf16[8,256,768]{2,1,0:T(8,128)(2,1)}), bf16[8,1024,768]{2,1,0:T(8,128)(2,1)}) %all-gather.11.cloned.1.call-update) | async-done | bytes 12582928 | tf_op jit(solution)/shard_map/all_gather | solution.py:84
  1396.8 19.9 %fusion.62 = bf16[8,1024,3,320]{1,3,2,0:T(8,128)(2,1)} fusion(bf16[8,1024,768]{2,1,0:T(8,128)(2,1)} %all-gather.11.cloned.1.call-done, bf16[2,3,320,768]{3,2,1,0:T(8,128)(2,1)S(1)} %copy-done.101), kind=kOutput, calls=%fused_computation.89 | convolution fusion | flops 12087459840 | bytes 29786112 | tf_op jit(solution)/shard_map/bsd,hcd->bshc/dot_general | solution.py:86
  1416.7 52.3 %fusion.11 = (f32[8,3,1024]{2,1,0:T(4,128)S(1)}, bf16[8,3,1024,1024]{2,3,1,0:T(8,128)(2,1)}) fusion(f32[8,3,1024,1024]{2,3,1,0:T(8,128)} %get-tuple-element.126, f32[8,3,1024]{2,1,0:T(4,128)S(1)} %multiply_divide_fusion, f32[8,1024,3,448]{1,3,2,0:T(8,128)} %broadcast_add_fusion.1, bf16[8,1024,3,320]{1,3,2,0:T(8,128)(2,1)} %fusion.62), kind=kOutput, calls=%fused_computation.15 | convolution fusion | flops 3347030016 | bytes 157483008 | tf_op jit(solution)/shard_map/transpose(jvp(bhqk,bkhe->bqhe))/dot_general | solution.py:39
  1469.0 50.9 %convert_bitcast_fusion = f32[8,1024,3,64]{1,3,2,0:T(8,128)} fusion(bf16[8,1024,3,64]{1,3,2,0:T(8,128)(2,1)S(1)} %copy-done.23, f32[8,3,1024,1024]{2,3,1,0:T(8,128)} %get-tuple-element.126, bf16[8,3,1024,1024]{2,3,1,0:T(8,128)(2,1)} %get-tuple-element.131, f32[8,3,1024]{2,1,0:T(4,128)S(1)} %neg.43, f32[8,3,1024]{2,1,0:T(4,128)S(1)} %copy-done.48), kind=kOutput, calls=%fused_computation.149 | convolution fusion | flops 3350200320 | bytes 160628736 | tf_op jit(solution)/shard_map/transpose(jvp(bqhe,bkhe->bhqk))/dot_general | solution.py:37
  1519.9 50.9 %convert_bitcast_fusion.1 = f32[8,1024,3,64]{1,3,2,0:T(8,128)} fusion(bf16[8,1024,3,64]{1,3,2,0:T(8,128)(2,1)} %convert_element_type.305, f32[8,3,1024,1024]{2,3,1,0:T(8,128)} %get-tuple-element.126, bf16[8,3,1024,1024]{2,3,1,0:T(8,128)(2,1)} %get-tuple-element.131, f32[8,3,1024]{2,1,0:T(4,128)S(1)} %neg.43, f32[8,3,1024]{2,1,0:T(4,128)S(1)} %copy-done.48), kind=kOutput, calls=%fused_computation.150 | convolution fusion | flops 3350200320 | bytes 160628736 | tf_op jit(solution)/shard_map/transpose(jvp(bqhe,bkhe->bhqk))/dot_general | solution.py:37
  1570.8 23.6 %convert_bitcast_fusion.4 = bf16[8,1024,3,64]{1,3,2,0:T(8,128)(2,1)} fusion(bf16[8,3,1024,1024]{2,3,1,0:T(8,128)(2,1)} %divide_convert_fusion.1, bf16[8,1024,3,320]{1,3,2,0:T(8,128)(2,1)} %fusion.62), kind=kOutput, calls=%fused_computation.200 | convolution fusion | flops 3222798336 | bytes 56623104 | tf_op jit(solution)/shard_map/transpose(jvp(bhqk,bkhe->bqhe))/dot_general | solution.py:39
  1594.4 27.7 %fusion.29 = f32[8,1024,3,256]{1,3,2,0:T(8,128)} fusion(f32[8,1024,3,448]{1,3,2,0:T(8,128)} %broadcast_add_fusion.1, bf16[8,1024,3,320]{1,3,2,0:T(8,128)(2,1)} %fusion.62), kind=kLoop, calls=%fused_computation.45 | loop fusion | flops 125829120 | bytes 62914560 | tf_op jit(solution)/shard_map/transpose(jvp())/add_any | solution.py:40
  1638.5 18.8 multiply_add_fusion.3
  1657.3 10.0 pad_add_fusion.2
  1694.5 13.0 multiply_reduce_fusion.3
  1717.0 27.4 %bitcast_convert_fusion = bf16[8,1024,768]{2,1,0:T(8,128)(2,1)} fusion(bf16[2,768,3,448]{1,3,2,0:T(8,128)(2,1)} %param.19, f32[8,1024,3,64]{1,3,2,0:T(8,128)} %get-tuple-element.76, f32[8,1024,3,64]{1,3,2,0:T(8,128)} %get-tuple-element.75, bf16[8,1024,3,64]{1,3,2,0:T(8,128)(2,1)} %convert_bitcast_fusion.4, f32[8,1024,3,256]{1,3,2,0:T(8,128)} %fusion.29), kind=kOutput, calls=%fused_computation.58 | convolution fusion | flops 16972775424 | bytes 55541760 | tf_op jit(solution)/shard_map/bshc,dhc->bsd/dot_general | solution.py:92
  1746.2 15.0 fusion.44
  1761.2 19.6 %fusion.145 = bf16[1,3,320,768]{3,2,1,0:T(8,128)(2,1)} fusion(bf16[8,1024,768]{2,1,0:T(8,128)(2,1)} %all-gather.9.cloned.1.call-done, bf16[8,1024,3,256]{1,3,2,0:T(8,128)(2,1)} %get-tuple-element.78, bf16[8,1024,3,64]{1,3,2,0:T(8,128)(2,1)} %copy-done.21), kind=kOutput, calls=%fused_computation.236 | convolution fusion | flops 12111790080 | bytes 29786112 | tf_op jit(solution)/shard_map/bshc,bsd->hcd/dot_general | solution.py:85
  1780.9 24.6 %fusion.135 = bf16[1,768,3,448]{1,3,2,0:T(8,128)(2,1)} fusion(bf16[8,1024,768]{2,1,0:T(8,128)(2,1)} %all-gather.7.cloned.1.call-done, f32[8,1024,3,64]{1,3,2,0:T(8,128)} %get-tuple-element.80, f32[8,1024,3,64]{1,3,2,0:T(8,128)} %get-tuple-element.79, bf16[8,1024,3,64]{1,3,2,0:T(8,128)(2,1)S(1)} %copy-done.10, f32[8,1024,3,256]{1,3,2,0:T(8,128)} %get-tuple-element.77), kind=kOutput, calls=%fused_computation.230 | convolution fusion | flops 16967516160 | bytes 55541760 | tf_op jit(solution)/shard_map/bsd,bshc->dhc/dot_general | solution.py:91
  1806.3 15.6 fusion.42
  1830.6 19.0 fusion.142
  1851.5 24.4 %fusion.132 = bf16[1,768,3,448]{1,3,2,0:T(8,128)(2,1)} fusion(bf16[8,1024,768]{2,1,0:T(8,128)(2,1)} %all-gather.5.cloned.1.call-done, f32[8,1024,3,64]{1,3,2,0:T(8,128)} %get-tuple-element.76, f32[8,1024,3,64]{1,3,2,0:T(8,128)} %get-tuple-element.75, bf16[8,1024,3,64]{1,3,2,0:T(8,128)(2,1)S(1)} %copy-done.11, f32[8,1024,3,256]{1,3,2,0:T(8,128)} %fusion.29), kind=kOutput, calls=%fused_computation.229 | convolution fusion | flops 16967516160 | bytes 55541760 | tf_op jit(solution)/shard_map/bsd,bshc->dhc/dot_general | solution.py:91
  1895.0 23.4 %all-reduce.20.cloned.1.call-done = (f32[8,2304]{1,0:T(8,128)}, f32[8,2304]{1,0:T(8,128)}) async-done(((f32[8,2304]{1,0:T(8,128)}, f32[8,2304]{1,0:T(8,128)}), (f32[8,2304]{1,0:T(8,128)}, f32[8,2304]{1,0:T(8,128)})) %all-reduce.20.cloned.1.call-update) | async-done | bytes 147472 | tf_op jit(solution)/shard_map/psum | solution.py:96
  1928.2 11.2 pad_maximum_fusion.2
  (319 shorter events, 326.8 us)
Async XLA Ops:
  7.2 96.6 %all-gather.5.cloned.1.call-start = ((), (), s32[]{:S(2)}) async-start(), calls=%async_computation.4 | async-start | bytes 15728640 | tf_op jit(solution)/shard_map/all_gather | solution.py:62
  13.4 20.0 %copy-start.98 = (bf16[2,64]{1,0:T(2,128)(2,1)S(1)}, bf16[2,64]{1,0:T(2,128)(2,1)}, u32[]{:S(2)}) copy-start(bf16[2,64]{1,0:T(2,128)(2,1)} %param.22) | copy-start | bytes 772
  13.4 20.6 %copy-start.99 = (bf16[2,64]{1,0:T(2,128)(2,1)S(1)}, bf16[2,64]{1,0:T(2,128)(2,1)}, u32[]{:S(2)}) copy-start(bf16[2,64]{1,0:T(2,128)(2,1)} %param.21) | copy-start | bytes 772
  19.9 427.7 %reduce-scatter.5.cloned.1.call-start = ((), (), s32[]{:S(2)}) async-start(), calls=%async_computation.5 | async-start | bytes 15728640 | tf_op jit(solution)/shard_map/reduce_scatter | solution.py:66
  27.4 151.9 %copy-start.12 = (f32[1024,32]{0,1:T(8,128)}, f32[1024,32]{0,1:T(8,128)S(1)}, u32[]{:S(2)}) copy-start(f32[1024,32]{0,1:T(8,128)S(1)} %all_gather.19) | copy-start | bytes 393220
  33.5 145.8 %copy-start.16 = (f32[1024,32]{0,1:T(8,128)}, f32[1024,32]{0,1:T(8,128)S(1)}, u32[]{:S(2)}) copy-start(f32[1024,32]{0,1:T(8,128)S(1)} %all_gather.20) | copy-start | bytes 393220
  34.0 119.8 %copy-start.86 = (f32[64]{0:T(128)}, f32[64]{0:T(128)S(1)}, u32[]{:S(2)}) copy-start(f32[64]{0:T(128)S(1)} %get-tuple-element.122) | copy-start | bytes 772
  34.5 119.3 %copy-start.88 = (f32[64]{0:T(128)}, f32[64]{0:T(128)S(1)}, u32[]{:S(2)}) copy-start(f32[64]{0:T(128)S(1)} %get-tuple-element.124) | copy-start | bytes 772
  137.4 16.3 copy-start.41
  137.5 16.3 copy-start.39
  266.6 48.3 %copy-start.47 = (f32[8,3,1024]{2,1,0:T(4,128)}, f32[8,3,1024]{2,1,0:T(4,128)S(1)}, u32[]{:S(2)}) copy-start(f32[8,3,1024]{2,1,0:T(4,128)S(1)} %get-tuple-element.125) | copy-start | bytes 294916
  334.5 20.6 %copy-start.20 = (bf16[8,1024,3,64]{1,3,2,0:T(8,128)(2,1)}, bf16[8,1024,3,64]{1,3,2,0:T(8,128)(2,1)S(1)}, u32[]{:S(2)}) copy-start(bf16[8,1024,3,64]{1,3,2,0:T(8,128)(2,1)S(1)} %convert_bitcast_fusion.7) | copy-start | bytes 9437188
  355.1 175.0 %all-gather.9.cloned.1.call-start = ((), (), s32[]{:S(2)}) async-start(), calls=%async_computation.8 | async-start | bytes 15728640 | tf_op jit(solution)/shard_map/all_gather | solution.py:84
  355.8 91.9 %copy-start.1 = (bf16[8,256,768]{2,1,0:T(8,128)(2,1)S(1)}, bf16[8,256,768]{2,1,0:T(8,128)(2,1)}, u32[]{:S(2)}) copy-start(bf16[8,256,768]{2,1,0:T(8,128)(2,1)} %param.13) | copy-start | bytes 9437188
  355.8 91.9 %copy-start.49 = (f32[8,768]{1,0:T(8,128)S(1)}, f32[8,768]{1,0:T(8,128)}, u32[]{:S(2)}) copy-start(f32[8,768]{1,0:T(8,128)} %get-tuple-element.116) | copy-start | bytes 73732
  358.6 93.5 %copy-start.43 = (f32[8,768]{1,0:T(8,128)}, f32[8,768]{1,0:T(8,128)S(1)}, u32[]{:S(2)}) copy-start(f32[8,768]{1,0:T(8,128)S(1)} %get-tuple-element.115) | copy-start | bytes 73732
  363.4 249.6 %all-gather.7.cloned.1.call-start = ((), (), s32[]{:S(2)}) async-start(), calls=%async_computation.6 | async-start | bytes 15728640 | tf_op jit(solution)/shard_map/all_gather | solution.py:62
  364.0 88.1 %copy-start.75 = (f32[768]{0:T(1024)}, f32[768]{0:T(1024)S(1)}, u32[]{:S(2)}) copy-start(f32[768]{0:T(1024)S(1)} %get-tuple-element.61) | copy-start | bytes 9220
  451.0 79.1 %copy-start.100 = (bf16[2,3,320,768]{3,2,1,0:T(8,128)(2,1)S(1)}, bf16[2,3,320,768]{3,2,1,0:T(8,128)(2,1)}, u32[]{:S(2)}) copy-start(bf16[2,3,320,768]{3,2,1,0:T(8,128)(2,1)} %param.23) | copy-start | bytes 8847364
  452.1 98.1 %copy-start.72 = (f32[8,256]{1,0:T(8,128)}, f32[8,256]{1,0:T(8,128)S(1)}, u32[]{:S(2)}) copy-start(f32[8,256]{1,0:T(8,128)S(1)} %fusion.91) | copy-start | bytes 24580
  455.3 751.0 %reduce-scatter.9.cloned.1.call-start = ((), (), s32[]{:S(2)}) async-start(), calls=%async_computation.9 | async-start | bytes 15728640 | tf_op jit(solution)/shard_map/reduce_scatter | solution.py:93
  761.0 70.0 %copy-start.25 = (bf16[8,1024,3,64]{1,3,2,0:T(8,128)(2,1)S(1)}, bf16[8,1024,3,64]{1,3,2,0:T(8,128)(2,1)}, u32[]{:S(2)}) copy-start(bf16[8,1024,3,64]{1,3,2,0:T(8,128)(2,1)} %convert_element_type.327) | copy-start | bytes 9437188
  1113.7 187.4 %reduce-scatter.7.cloned.1.call-start = ((), (), s32[]{:S(2)}) async-start(), calls=%async_computation.7 | async-start | bytes 15728640 | tf_op jit(solution)/shard_map/reduce_scatter | solution.py:66
  1133.6 20.7 %copy-start.21 = (bf16[8,1024,3,64]{1,3,2,0:T(8,128)(2,1)}, bf16[8,1024,3,64]{1,3,2,0:T(8,128)(2,1)S(1)}, u32[]{:S(2)}) copy-start(bf16[8,1024,3,64]{1,3,2,0:T(8,128)(2,1)S(1)} %convert_bitcast_fusion.6) | copy-start | bytes 9437188
  1154.3 52.0 %copy-start.4 = (bf16[8,256,768]{2,1,0:T(8,128)(2,1)S(1)}, bf16[8,256,768]{2,1,0:T(8,128)(2,1)}, u32[]{:S(2)}) copy-start(bf16[8,256,768]{2,1,0:T(8,128)(2,1)} %copy-done.3) | copy-start | bytes 9437188
  1154.3 52.0 %copy-start.44 = (f32[8,768]{1,0:T(8,128)S(1)}, f32[8,768]{1,0:T(8,128)}, u32[]{:S(2)}) copy-start(f32[8,768]{1,0:T(8,128)} %copy-done.43) | copy-start | bytes 73732
  1154.3 52.0 %copy-start.55 = (f32[8,256]{1,0:T(8,128)S(1)}, f32[8,256]{1,0:T(8,128)}, u32[]{:S(2)}) copy-start(f32[8,256]{1,0:T(8,128)} %copy-done.54) | copy-start | bytes 24580
  1154.3 56.8 %copy-start.73 = (f32[8,256]{1,0:T(8,128)S(1)}, f32[8,256]{1,0:T(8,128)}, u32[]{:S(2)}) copy-start(f32[8,256]{1,0:T(8,128)} %copy-done.72) | copy-start | bytes 24580
  1154.3 56.8 %copy-start.63 = (f32[8,256]{1,0:T(8,128)S(1)}, f32[8,256]{1,0:T(8,128)}, u32[]{:S(2)}) copy-start(f32[8,256]{1,0:T(8,128)} %copy-done.62) | copy-start | bytes 24580
  1154.4 146.8 %copy-start.50 = (f32[8,768]{1,0:T(8,128)S(1)}, f32[8,768]{1,0:T(8,128)}, u32[]{:S(2)}) copy-start(f32[8,768]{1,0:T(8,128)} %get-tuple-element.116) | copy-start | bytes 73732
  1154.4 146.8 %copy-start.61 = (f32[8,768]{1,0:T(8,128)S(1)}, f32[8,768]{1,0:T(8,128)}, u32[]{:S(2)}) copy-start(f32[8,768]{1,0:T(8,128)} %copy-done.60) | copy-start | bytes 73732
  1154.4 146.8 %copy-start.76 = (f32[768]{0:T(1024)S(1)}, f32[768]{0:T(1024)}, u32[]{:S(2)}) copy-start(f32[768]{0:T(1024)} %copy-done.75) | copy-start | bytes 9220
  1154.4 146.8 %copy-start.82 = (f32[768]{0:T(1024)S(1)}, f32[768]{0:T(1024)}, u32[]{:S(2)}) copy-start(f32[768]{0:T(1024)} %get-tuple-element.60) | copy-start | bytes 9220
  1154.4 242.4 %all-gather.11.cloned.1.call-start = ((), (), s32[]{:S(2)}) async-start(), calls=%async_computation.10 | async-start | bytes 15728640 | tf_op jit(solution)/shard_map/all_gather | solution.py:84
  1311.7 85.1 %copy-start.101 = (bf16[2,3,320,768]{3,2,1,0:T(8,128)(2,1)S(1)}, bf16[2,3,320,768]{3,2,1,0:T(8,128)(2,1)}, u32[]{:S(2)}) copy-start(bf16[2,3,320,768]{3,2,1,0:T(8,128)(2,1)} %param.23) | copy-start | bytes 8847364
  1315.8 564.9 %reduce-scatter.11.cloned.1.call-start = ((), (), s32[]{:S(2)}) async-start(), calls=%async_computation.11 | async-start | bytes 15728640 | tf_op jit(solution)/shard_map/reduce_scatter | solution.py:93
  1416.7 52.3 %copy-start.23 = (bf16[8,1024,3,64]{1,3,2,0:T(8,128)(2,1)S(1)}, bf16[8,1024,3,64]{1,3,2,0:T(8,128)(2,1)}, u32[]{:S(2)}) copy-start(bf16[8,1024,3,64]{1,3,2,0:T(8,128)(2,1)} %convert_element_type.308) | copy-start | bytes 9437188
  1685.9 21.9 %slice-start = ((s8[6291456]{0:T(1024)(128)(4,1)}), s8[2097152]{0:T(1024)(128)(4,1)S(1)}, s32[]{:S(2)}) async-start(s8[6291456]{0:T(1024)(128)(4,1)} %bitcast.260), calls=%async_computation.13 | async-start | bytes 4194304
  1744.4 174.0 %all-reduce.20.cloned.1.call-start = ((), (), s32[]{:S(2)}) async-start(), calls=%async_computation.12 | async-start | bytes 294912 | tf_op jit(solution)/shard_map/psum | solution.py:96
  1780.9 24.7 %copy-start.84 = (f32[768]{0:T(1024)S(1)}, f32[768]{0:T(1024)}, u32[]{:S(2)}) copy-start(f32[768]{0:T(1024)} %get-tuple-element.103) | copy-start | bytes 9220
  1780.9 24.7 %copy-start.83 = (f32[768]{0:T(1024)S(1)}, f32[768]{0:T(1024)}, u32[]{:S(2)}) copy-start(f32[768]{0:T(1024)} %get-tuple-element.52) | copy-start | bytes 9220
  1780.9 24.7 %copy-start.67 = (f32[8,768]{1,0:T(8,128)S(1)}, f32[8,768]{1,0:T(8,128)}, u32[]{:S(2)}) copy-start(f32[8,768]{1,0:T(8,128)} %get-tuple-element.56) | copy-start | bytes 73732
  1780.9 24.7 %copy-start.68 = (f32[8,768]{1,0:T(8,128)S(1)}, f32[8,768]{1,0:T(8,128)}, u32[]{:S(2)}) copy-start(f32[8,768]{1,0:T(8,128)} %get-tuple-element.48) | copy-start | bytes 73732
  1780.9 24.7 %copy-start.69 = (f32[8,768]{1,0:T(8,128)S(1)}, f32[8,768]{1,0:T(8,128)}, u32[]{:S(2)}) copy-start(f32[8,768]{1,0:T(8,128)} %get-tuple-element.53) | copy-start | bytes 73732
  1806.3 16.3 copy-start.97
  1830.6 19.0 copy-start.34
  1830.6 20.9 %copy-start.11 = (bf16[8,1024,3,64]{1,3,2,0:T(8,128)(2,1)S(1)}, bf16[8,1024,3,64]{1,3,2,0:T(8,128)(2,1)}, u32[]{:S(2)}) copy-start(bf16[8,1024,3,64]{1,3,2,0:T(8,128)(2,1)} %convert_bitcast_fusion.4) | copy-start | bytes 9437188
  1889.2 29.3 %copy-start.53 = (bf16[8,768]{1,0:T(8,128)(2,1)S(1)}, bf16[8,768]{1,0:T(8,128)(2,1)}, u32[]{:S(2)}) copy-start(bf16[8,768]{1,0:T(8,128)(2,1)} %param.14) | copy-start | bytes 36868
  (65 other events, 469.3 us)
Sparse Core Ops, SparseCore 0:
  20.0 83.6 all-gather.4
  355.2 92.3 reduce-scatter.4
  449.2 80.8 all-gather.8
  532.1 80.8 all-gather.6
  1113.9 92.3 reduce-scatter.8
  1208.7 92.3 reduce-scatter.6
  1315.9 80.8 all-gather.10
  1744.5 92.6 reduce-scatter.10
  1889.3 29.0 all-reduce.19
where the time goes:
time: 1950 us
  matrix products  784 us (40%)
  waiting for transfers between devices  532 us (27%)
  other arithmetic  463 us (24%)
  local copies, waits for them, and re-layouts  131 us (7%)
  blocking collectives  19.8 us (1%)
    dot_general x6, matrix products, mix_heads(): jnp.einsum('bhqk,bkhe->bqhe', attn_probs, v_part, preferred_element_type=...  207 us
    dot_general x4, matrix products, mix_heads(): jnp.einsum('bqhe,bkhe->bhqk', q_rot, k_rot, preferred_element_type=jnp.fl...  204 us
    reduce_scatter x2, waiting for transfers between devices, device_fn(): lax.psum_scatter(part_out.astype(jnp.bfloat16), 'tp', scatter_dimension=1...  169 us
    all_gather x2, waiting for transfers between devices, device_fn(): lax.all_gather(gated_grad.astype(jnp.bfloat16), 'tp', axis=1, tiled=True)  156 us
    all_gather x2, waiting for transfers between devices, device_fn(): normed_full = lax.all_gather(normed, 'tp', axis=1, tiled=True)  132 us
    sub x2, matrix products, mix_heads(): attn_probs = jax.nn.softmax(scores, axis=-1).astype(jnp.bfloat16)  79.9 us
    reshape x8, local copies, waits for them, and re-layouts, apply_rope(): pair_view = tensor.reshape(tensor.shape[:-1] + (tensor.shape[-1] // 2, 2))  67.3 us
    add_any x2, other arithmetic, mix_heads(): jax.nn.gelu(projected[..., 3 * head_dim:], approximate=True)  60.2 us
  transfers between devices with their start and end apart: 9, of which 8 were waited for; matrix products, arithmetic and copies ran while one was open for 11% of the time, Pallas kernels for 0%

commit v1 on v0

v1 whole, which is shorter than its diff:
```python
import functools
import jax
import jax.numpy as jnp
import numpy as np
from jax import lax
from jax.experimental import pallas as pl
from jax.experimental.pallas import tpu as pltpu
from jax.sharding import PartitionSpec as P

NORM_EPS = 1e-6
LOG2E = 1.4426950408889634
GELU_C = 0.7978845608028654
GELU_A = 0.044715
F32 = jnp.float32
BF16 = jnp.bfloat16
CHUNK = 256


def dot_nn(a, b):
    return lax.dot_general(a, b, (((1,), (0,)), ((), ())), preferred_element_type=F32)


def dot_nt(a, b):
    return lax.dot_general(a, b, (((1,), (1,)), ((), ())), preferred_element_type=F32)


def dot_tn(a, b):
    return lax.dot_general(a, b, (((0,), (0,)), ((), ())), preferred_element_type=F32)


def head_weights(w_ref, i):
    return jnp.concatenate([w_ref[d, i, 0] for d in range(w_ref.shape[0])], axis=0)


def norm_rope(raw, scale_col, cos_t, sin_t):
    half = raw.shape[0] // 2
    inv = lax.rsqrt(jnp.mean(raw * raw, axis=0, keepdims=True) + NORM_EPS)
    hat = raw * inv
    scaled = hat * scale_col
    a, b = scaled[:half], scaled[half:]
    rot = jnp.concatenate([a * cos_t - b * sin_t, a * sin_t + b * cos_t], axis=0)
    return hat, inv, rot.astype(BF16)


def norm_rope_bwd(d_rot, hat, inv, scale_col, cos_t, sin_t):
    half = d_rot.shape[0] // 2
    da, db = d_rot[:half], d_rot[half:]
    d_scaled = jnp.concatenate([da * cos_t + db * sin_t, db * cos_t - da * sin_t], axis=0)
    d_scale = jnp.sum(d_scaled * hat, axis=1, keepdims=True)
    d_hat = d_scaled * scale_col
    d_raw = inv * (d_hat - hat * jnp.mean(d_hat * hat, axis=0, keepdims=True))
    return d_raw, d_scale


def fwd_kernel(e, x_ref, mod_ref, w_ref, bin_ref, qs_ref, ks_ref, cos_ref, sin_ref, y_ref, o_ref, lse_ref, h_ref, br_ref, xo_ref, z_sc, h_sc):
    g, b = pl.program_id(0), pl.program_id(1)
    last = pl.num_programs(0) - 1
    cols = bin_ref.shape[2]
    s_len = x_ref.shape[2]

    @pl.when(g == 0)
    def _():
        x = x_ref[0].astype(F32)
        cent = x - jnp.mean(x, axis=0, keepdims=True)
        normed = cent * lax.rsqrt(jnp.mean(cent * cent, axis=0, keepdims=True) + NORM_EPS)
        h = (normed * (1.0 + mod_ref[0, :, 1:2]) + mod_ref[0, :, 0:1]).astype(BF16)
        h_sc[b] = h
        h_ref[0] = h

    h_t = h_sc[b]
    cos_t, sin_t = cos_ref[...], sin_ref[...]
    mul = (e ** -0.5) * LOG2E
    joined, outs = [], []
    for i in range(2):
        w = head_weights(w_ref, i)
        outs.append(w[cols:])
        y = dot_nn(w[:cols], h_t) + bin_ref[i, 0]
        y_ref[0, i, 0] = y
        q_rot = norm_rope(y[:e], qs_ref[...], cos_t, sin_t)[2]
        k_rot = norm_rope(y[e:2 * e], ks_ref[...], cos_t, sin_t)[2]
        v_t = y[2 * e:3 * e].astype(BF16)
        for c in range(s_len // CHUNK):
            span = slice(c * CHUNK, (c + 1) * CHUNK)
            s = dot_tn(k_rot, q_rot[:, span])
            top = jnp.max(s, axis=0, keepdims=True) * mul
            p = jnp.exp2(s * mul - top)
            tot = jnp.sum(p, axis=0, keepdims=True)
            p16 = (p * (1.0 / tot)).astype(BF16)
            o_ref[0, i, 0, :, span] = dot_nn(v_t, p16).astype(BF16)
            lse_ref[0, 0, i:i + 1, span] = top + jnp.log2(tot)
        u = y[3 * e:]
        t = jnp.tanh(GELU_C * (u + GELU_A * u * u * u))
        joined.append(o_ref[0, i, 0])
        joined.append((0.5 * u * (1.0 + t)).astype(BF16))
    z = dot_tn(jnp.concatenate(outs, axis=0), jnp.concatenate(joined, axis=0))

    @pl.when(g == 0)
    def _():
        z_sc[b] = z

    @pl.when(jnp.logical_and(g > 0, g < last))
    def _():
        z_sc[b] += z

    @pl.when(g == last)
    def _():
        branch = z_sc[b] + z + mod_ref[0, :, 3:4]
        br_ref[0] = branch
        xo_ref[0] = (x_ref[0].astype(F32) + mod_ref[0, :, 2:3] * branch).astype(BF16)


def bwd_kernel(e, dbr_ref, h_ref, w_ref, qs_ref, ks_ref, cos_ref, sin_ref, y_ref, o_ref, lse_ref, gw_ref, gb_ref, dqs_ref, dks_ref, dh_ref, dh_sc, acc_sc, dj_sc, dp_sc, jn_sc):
    g, b = pl.program_id(0), pl.program_id(1)
    last = pl.num_programs(0) - 1
    cols = y_ref.shape[3]
    rows = dj_sc.shape[0] // 2
    s_len = dbr_ref.shape[2]
    d_br = dbr_ref[0]
    cos_t, sin_t = cos_ref[...], sin_ref[...]
    scale = e ** -0.5
    mul = scale * LOG2E
    ws = [head_weights(w_ref, i) for i in range(2)]
    for i in range(2):
        dj_sc[i * rows:(i + 1) * rows] = dot_nn(ws[i][cols:], d_br).astype(BF16)

    @pl.when(jnp.logical_and(g == 0, b == 0))
    def _():
        dqs_ref[...] = jnp.zeros_like(dqs_ref)
        dks_ref[...] = jnp.zeros_like(dks_ref)

    @pl.when(b == 0)
    def _():
        gb_ref[...] = jnp.zeros_like(gb_ref)

    for i in range(2):
        base = i * cols
        q_hat, q_inv, q_rot = norm_rope(y_ref[0, i, 0, :e], qs_ref[...], cos_t, sin_t)
        k_hat, k_inv, k_rot = norm_rope(y_ref[0, i, 0, e:2 * e], ks_ref[...], cos_t, sin_t)
        v_t = y_ref[0, i, 0, 2 * e:3 * e].astype(BF16)
        o_t = o_ref[0, i, 0]
        d_o = dj_sc[i * rows:i * rows + e]
        d_sum = jnp.sum(d_o.astype(F32) * o_t.astype(F32), axis=0, keepdims=True)
        d_q, d_k, d_v = [], None, None
        for c in range(s_len // CHUNK):
            span = slice(c * CHUNK, (c + 1) * CHUNK)
            s = dot_tn(k_rot, q_rot[:, span])
            p = jnp.exp2(s * mul - lse_ref[0, 0, i:i + 1, span])
            d_p = dot_tn(v_t, d_o[:, span])
            d_s = (p * (d_p - d_sum[:, span])).astype(BF16)
            d_q.append(dot_nn(k_rot, d_s))
            kc = dot_nt(q_rot[:, span], d_s)
            vc = dot_nt(d_o[:, span], p.astype(BF16))
            d_k = kc if d_k is None else d_k + kc
            d_v = vc if d_v is None else d_v + vc
        d_q = jnp.concatenate(d_q, axis=1) * scale
        d_qraw, d_qs = norm_rope_bwd(d_q, q_hat, q_inv, qs_ref[...], cos_t, sin_t)
        d_kraw, d_ks = norm_rope_bwd(d_k * scale, k_hat, k_inv, ks_ref[...], cos_t, sin_t)
        dqs_ref[...] += d_qs
        dks_ref[...] += d_ks
        u = y_ref[0, i, 0, 3 * e:]
        t = jnp.tanh(GELU_C * (u + GELU_A * u * u * u))
        half = 0.5 * (1.0 + t)
        jn_sc[i * rows:i * rows + e] = o_t
        jn_sc[i * rows + e:(i + 1) * rows] = (u * half).astype(BF16)
        slope = half + 0.5 * u * (1.0 - t * t) * (GELU_C * (1.0 + 3.0 * GELU_A * u * u))
        d_u = dj_sc[i * rows + e:(i + 1) * rows].astype(F32) * slope
        off = 0
        for part in (d_qraw, d_kraw, d_v, d_u):
            n = part.shape[0]
            dp_sc[base + off:base + off + n] = part.astype(BF16)
            gb_ref[i, 0, off:off + n] += jnp.sum(part, axis=1, keepdims=True)
            off += n

    h_t = h_ref[0]
    gwi = dot_nt(dp_sc[...], h_t)
    gwo = dot_nt(jn_sc[...], d_br)
    d_h = dot_tn(jnp.concatenate([ws[0][:cols], ws[1][:cols]], axis=0), dp_sc[...])

    @pl.when(b == 0)
    def _():
        acc_sc[:2 * cols] = gwi
        acc_sc[2 * cols:] = gwo

    @pl.when(b > 0)
    def _():
        for i in range(2):
            gw_ref[i, 0, :cols] = (acc_sc[i * cols:(i + 1) * cols] + gwi[i * cols:(i + 1) * cols]).astype(BF16)
            lo = 2 * cols + i * rows
            gw_ref[i, 0, cols:] = (acc_sc[lo:lo + rows] + gwo[i * rows:(i + 1) * rows]).astype(BF16)

    @pl.when(g == 0)
    def _():
        dh_sc[b] = d_h

    @pl.when(jnp.logical_and(g > 0, g < last))
    def _():
        dh_sc[b] += d_h

    @pl.when(g == last)
    def _():
        dh_ref[0] = dh_sc[b] + d_h


def block_forward(x_t, mod_cols, w_all, b_cols, qs, ks, cos_t, sin_t):
    n_b, dim, s_len = x_t.shape
    depth, n_t, n_j, piece, _ = w_all.shape
    cols = b_cols.shape[2]
    e = qs.shape[0]
    n_g = (n_t // 2) * n_j
    half = n_t // 2
    last = n_g - 1

    def ends(g, b):
        return jnp.where(jnp.logical_or(g == 0, g == last), b, n_b - 1)

    full = lambda *shape: pl.BlockSpec(shape, lambda g, b: (0,) * len(shape))
    head4 = lambda n, m: pl.BlockSpec((2, 1, n, m), lambda g, b: (g % half, g // half, 0, 0))
    head5 = lambda n, m: pl.BlockSpec((1, 2, 1, n, m), lambda g, b: (b, g % half, g // half, 0, 0))
    flops = 2 * n_b * s_len * dim * (n_t * n_j) * (cols + dim - cols) + 4 * n_b * n_t * n_j * s_len * s_len * e * 4
    return pl.pallas_call(
        functools.partial(fwd_kernel, e),
        grid=(n_g, n_b),
        in_specs=[
            pl.BlockSpec((1, dim, s_len), lambda g, b: (ends(g, b), 0, 0)),
            pl.BlockSpec((1, dim, 4), lambda g, b: (b, 0, 0)),
            pl.BlockSpec((depth, 2, 1, piece, dim), lambda g, b: (0, g % half, g // half, 0, 0)),
            head4(cols, 1),
            full(e, 1), full(e, 1), full(e // 2, s_len), full(e // 2, s_len),
        ],
        out_specs=[
            head5(cols, s_len),
            head5(e, s_len),
            pl.BlockSpec((1, 1, 2, s_len), lambda g, b: (b, g, 0, 0)),
            pl.BlockSpec((1, dim, s_len), lambda g, b: (jnp.where(g == 0, b, n_b - 1), 0, 0)),
            pl.BlockSpec((1, dim, s_len), lambda g, b: (jnp.where(g == last, b, 0), 0, 0)),
            pl.BlockSpec((1, dim, s_len), lambda g, b: (jnp.where(g == last, b, 0), 0, 0)),
        ],
        out_shape=[
            jax.ShapeDtypeStruct((n_b, n_t, n_j, cols, s_len), F32),
            jax.ShapeDtypeStruct((n_b, n_t, n_j, e, s_len), BF16),
            jax.ShapeDtypeStruct((n_b, n_g, 2, s_len), F32),
            jax.ShapeDtypeStruct((n_b, dim, s_len), BF16),
            jax.ShapeDtypeStruct((n_b, dim, s_len), F32),
            jax.ShapeDtypeStruct((n_b, dim, s_len), BF16),
        ],
        scratch_shapes=[pltpu.VMEM((n_b, dim, s_len), F32), pltpu.VMEM((n_b, dim, s_len), BF16)],
        compiler_params=pltpu.CompilerParams(dimension_semantics=("arbitrary", "arbitrary"), vmem_limit_bytes=63 * 1024 * 1024),
        cost_estimate=pl.CostEstimate(flops=flops, bytes_accessed=100_000_000, transcendentals=n_b * n_t * n_j * s_len * s_len),
        name="block_fwd",
    )(x_t, mod_cols, w_all, b_cols, qs, ks, cos_t, sin_t)


def block_backward(j_lo, j_n, d_br, h_t, w_all, qs, ks, cos_t, sin_t, y, o, lse):
    n_b, dim, s_len = d_br.shape
    depth, n_t, n_j, piece, _ = w_all.shape
    cols = y.shape[3]
    e = qs.shape[0]
    rows = dim - cols
    half = n_t // 2
    n_g = half * j_n

    full = lambda *shape: pl.BlockSpec(shape, lambda g, b: (0,) * len(shape))
    head5 = lambda n, m: pl.BlockSpec((1, 2, 1, n, m), lambda g, b: (b, g % half, j_lo + g // half, 0, 0))
    act = pl.BlockSpec((1, dim, s_len), lambda g, b: (b, 0, 0))
    flops = 4 * n_b * s_len * dim * (n_t * j_n) * dim + 10 * n_b * n_t * j_n * s_len * s_len * e * 4
    return pl.pallas_call(
        functools.partial(bwd_kernel, e),
        grid=(n_g, n_b),
        in_specs=[
            act, act,
            pl.BlockSpec((depth, 2, 1, piece, dim), lambda g, b: (0, g % half, j_lo + g // half, 0, 0)),
            full(e, 1), full(e, 1), full(e // 2, s_len), full(e // 2, s_len),
            head5(cols, s_len),
            head5(e, s_len),
            pl.BlockSpec((1, 1, 2, s_len), lambda g, b: (b, half * j_lo + g, 0, 0)),
        ],
        out_specs=[
            pl.BlockSpec((2, 1, dim, dim), lambda g, b: (g % half, g // half, 0, 0)),
            pl.BlockSpec((2, 1, cols, 1), lambda g, b: (g % half, g // half, 0, 0)),
            full(e, 1), full(e, 1),
            pl.BlockSpec((1, dim, s_len), lambda g, b: (jnp.where(g == n_g - 1, b, 0), 0, 0)),
        ],
        out_shape=[
            jax.ShapeDtypeStruct((n_t, j_n, dim, dim), BF16),
            jax.ShapeDtypeStruct((n_t, j_n, cols, 1), F32),
            jax.ShapeDtypeStruct((e, 1), F32),
            jax.ShapeDtypeStruct((e, 1), F32),
            jax.ShapeDtypeStruct((n_b, dim, s_len), F32),
        ],
        scratch_shapes=[
            pltpu.VMEM((n_b, dim, s_len), F32),
            pltpu.VMEM((2 * dim, dim), F32),
            pltpu.VMEM((2 * rows, s_len), BF16),
            pltpu.VMEM((2 * cols, s_len), BF16),
            pltpu.VMEM((2 * rows, s_len), BF16),
        ],
        compiler_params=pltpu.CompilerParams(dimension_semantics=("arbitrary", "arbitrary"), vmem_limit_bytes=63 * 1024 * 1024),
        cost_estimate=pl.CostEstimate(flops=flops, bytes_accessed=100_000_000, transcendentals=n_b * n_t * j_n * s_len * s_len),
        name="block_bwd",
    )(d_br, h_t, w_all, qs, ks, cos_t, sin_t, y, o, lse)


def swap_to_samples(arr, n):
    me = lax.axis_index("tp")
    k, s = arr.shape[0] // n, arr.shape[2]
    out = jnp.zeros((k, arr.shape[1], n * s), arr.dtype)
    own = lax.dynamic_slice_in_dim(arr, me * k, k, 0)
    out = lax.dynamic_update_slice_in_dim(out, own, me * s, 2)
    for step in range(1, n):
        peer = me ^ step
        got = lax.ppermute(lax.dynamic_slice_in_dim(arr, peer * k, k, 0), "tp", [(i, i ^ step) for i in range(n)])
        out = lax.dynamic_update_slice_in_dim(out, got, peer * s, 2)
    return out


def swap_to_tokens(arr, n):
    me = lax.axis_index("tp")
    k, s = arr.shape[0], arr.shape[2] // n
    out = jnp.zeros((n * k, arr.shape[1], s), arr.dtype)
    own = lax.dynamic_slice_in_dim(arr, me * s, s, 2)
    out = lax.dynamic_update_slice_in_dim(out, own, me * k, 0)
    for step in range(1, n):
        peer = me ^ step
        got = lax.ppermute(lax.dynamic_slice_in_dim(arr, peer * s, s, 2), "tp", [(i, i ^ step) for i in range(n)])
        out = lax.dynamic_update_slice_in_dim(out, got, peer * k, 0)
    return out


def pair_split(e):
    return np.concatenate([np.arange(0, e, 2), np.arange(1, e, 2)])


def solution(mesh):
    n_tp = mesh.shape["tp"]
    act_spec = P("dp", "tp", None)
    in_specs = (act_spec, P("dp", None), P("tp", None), P("tp", None), P(None, None, None), P(None, None), P(None, None, "tp", None), P(None, "tp", None), P(None, None), P(None, None), P(None, "tp", None, None), P(None, None), act_spec)
    out_specs = (act_spec, act_spec, P("dp", None, None), P("dp", None), P("dp", None, "tp", None), P("dp", "tp", None), P("dp", None), P("dp", None), P("dp", "tp", None, None), P("dp", None))

    def device_fn(x_in, cond_vec, rope_cos, rope_sin, w_mod, b_mod, w_in, b_in, q_scale, k_scale, w_out, b_out, d_out):
        n_l, dim, n_j, cols = w_in.shape
        e = q_scale.shape[1]
        rows = w_out.shape[2]
        n_all = x_in.shape[0]
        n_b = n_all // n_tp
        me = lax.axis_index("tp")
        order = pair_split(e)
        perm = np.concatenate([order, e + order, np.arange(2 * e, cols)])
        perm_mat = jnp.asarray(np.eye(cols, dtype=np.float32)[perm], BF16)

        w_in_t = jnp.einsum("ec,ldhc->lhed", perm_mat, w_in, preferred_element_type=F32).astype(BF16)
        w_local = jnp.concatenate([w_in_t, w_out], axis=2)
        w_full = [lax.all_gather(w_local[l], "tp", axis=0, tiled=False)[None] for l in range(n_l)]

        x_t = swap_to_samples(jnp.swapaxes(x_in, 1, 2), n_tp)
        g_t = swap_to_samples(jnp.swapaxes(d_out, 1, 2), n_tp)
        small_in = jnp.concatenate([rope_cos.T, rope_sin.T], axis=0)
        b_in_all = lax.all_gather(b_in, "tp", axis=0, tiled=False)
        tables = lax.all_gather(small_in, "tp", axis=1, tiled=True)
        cos_t, sin_t = tables[:e // 2], tables[e // 2:]
        b_cols = jnp.moveaxis(b_in_all, 1, 0).astype(F32)[..., perm, None]

        silu_all = jax.nn.silu(cond_vec.astype(F32)).astype(BF16)
        silu_own = lax.dynamic_slice_in_dim(silu_all, me * n_b, n_b, 0)
        mod = jnp.einsum("bd,ldm->lbm", silu_own, w_mod, preferred_element_type=F32) + b_mod.astype(F32)[:, None, :]
        shift, scale, gate = jnp.split(mod, 3, axis=-1)
        bias = jnp.broadcast_to(b_out.astype(F32)[:, None, :], shift.shape)
        mod_cols = jnp.stack([shift, scale, gate, bias], axis=-1)
        qs = q_scale.astype(F32)[:, order, None]
        ks = k_scale.astype(F32)[:, order, None]

        saved = []
        for l in range(n_l):
            y, o, lse, h_t, branch, x_new = block_forward(x_t, mod_cols[l], w_full[l], b_cols[l], qs[l], ks[l], cos_t, sin_t)
            saved.append((x_t, y, o, lse, h_t, branch))
            x_t = x_new
        x_out = jnp.swapaxes(swap_to_tokens(x_t, n_tp), 1, 2)

        grads = [None] * n_l
        small = [None] * n_l
        for l in reversed(range(n_l)):
            x_t, y, o, lse, h_t, branch = saved[l]
            g32 = g_t.astype(F32)
            d_gate = jnp.sum(g32 * branch, axis=2)
            gated = g32 * gate[l][:, :, None]
            d_bout = jnp.sum(gated, axis=(0, 2))
            d_br = gated.astype(BF16)
            d_h, d_qs, d_ks, gb, gw = 0.0, 0.0, 0.0, [], []
            for j in range(n_j):
                gw_j, gb_j, dq_j, dk_j, dh_j = block_backward(j, 1, d_br, h_t, w_full[l], qs[l], ks[l], cos_t, sin_t, y, o, lse)
                d_h, d_qs, d_ks = d_h + dh_j, d_qs + dq_j, d_ks + dk_j
                gb.append(gb_j)
                gw.append(lax.psum_scatter(gw_j[:, 0], "tp", scatter_dimension=0, tiled=False))
            x32 = x_t.astype(F32)
            cent = x32 - jnp.mean(x32, axis=1, keepdims=True)
            inv = lax.rsqrt(jnp.mean(cent * cent, axis=1, keepdims=True) + NORM_EPS)
            hat = cent * inv
            d_shift = jnp.sum(d_h, axis=2)
            d_scale = jnp.sum(d_h * hat, axis=2)
            d_hat = d_h * (1.0 + scale[l])[:, :, None]
            d_x = inv * (d_hat - jnp.mean(d_hat, axis=1, keepdims=True) - hat * jnp.mean(d_hat * hat, axis=1, keepdims=True))
            g_t = (g32 + d_x).astype(BF16)
            grads[l] = jnp.stack(gw)
            d_mod = jnp.concatenate([d_shift, d_scale, d_gate], axis=-1)
            small[l] = jnp.concatenate([d_mod.reshape(-1), d_bout, d_qs[:, 0], d_ks[:, 0], jnp.concatenate(gb, axis=1).reshape(-1)])

        grad_x = jnp.swapaxes(swap_to_tokens(g_t, n_tp), 1, 2)
        gathered = lax.all_gather(jnp.stack(small), "tp", axis=0, tiled=False)
        n_mod = n_b * 3 * dim
        d_mod = jnp.moveaxis(gathered[:, :, :n_mod].reshape(n_tp, n_l, n_b, 3 * dim), 1, 0).reshape(n_l, n_all, 3 * dim)
        sums = jnp.sum(gathered[:, :, n_mod:], axis=0)
        g_wmod = jnp.einsum("bd,lbm->ldm", silu_all.astype(F32), d_mod, preferred_element_type=F32)
        g_bmod = jnp.sum(d_mod, axis=1)
        inverse = np.argsort(order)
        g_bout = sums[:, :dim]
        g_qs = sums[:, dim:dim + e][:, inverse]
        g_ks = sums[:, dim + e:dim + 2 * e][:, inverse]
        g_bin = lax.dynamic_index_in_dim(sums[:, dim + 2 * e:].reshape(n_l, n_tp, n_j, cols), me, 1, keepdims=False)[..., np.argsort(perm)]
        gw_all = jnp.stack(grads)
        g_win = jnp.einsum("ec,lhed->ldhc", perm_mat, gw_all[:, :, :cols], preferred_element_type=F32).astype(BF16)
        g_wout = gw_all[:, :, cols:]
        return (x_out, grad_x, g_wmod, g_bmod, g_win, g_bin, g_qs, g_ks, g_wout, g_bout)

    return jax.shard_map(device_fn, mesh=mesh, in_specs=in_specs, out_specs=out_specs, check_vma=False)
```

time: 1950 us -> 1010 us (0.52)
  matrix products: 784 us -> 19.9 us
  Pallas kernels: 0 us -> 623 us
  waiting for transfers between devices: 532 us -> 46.2 us
  other arithmetic: 463 us -> 62.8 us
  blocking collectives: 19.8 us -> 107 us
    dot_general x26 -> x4, matrix products: 705 us -> 19.9 us  [the longest x1 7.11 us: device_fn(): jnp.einsum('bd,lbm->ldm', silu_all.astype(F32), d_mod, preferred_element_...]
    pallas_call x0 -> x8, Pallas kernels: none -> 623 us  [the longest x6 370 us: block_backward(): pl.pallas_call(functools.partial(bwd_kernel, e), grid=(n_g, n_b), in_spec...]
    all_gather x4 -> x2, waiting for transfers between devices: 288 us -> 0.02 us  [device_fn(): lax.all_gather(w_local[l], 'tp', axis=0, tiled=False)[None]]
    reduce_scatter x4 -> x6, waiting for transfers between devices: 221 us -> 0.06 us  [device_fn(): lax.psum_scatter(gw_j[:, 0], 'tp', scatter_dimension=0, tiled=False)]
    add_any x10 -> x0, other arithmetic: 161 us -> none  [the longest x2 60.2 us: mix_heads(): jax.nn.gelu(projected[..., 3 * head_dim:], approximate=True)]
    reshape x12 -> x8, local copies, waits for them, and re-layouts: 100 us -> 5.22 us  [the longest x2 3.34 us: device_fn(): gathered[:, :, :n_mod].reshape(n_tp, n_l, n_b, 3 * dim)]
    all_gather x2 -> x3, blocking collectives: 12.9 us -> 107 us  [the longest x1 90.2 us: device_fn(): b_in_all = lax.all_gather(b_in, 'tp', axis=0, tiled=False)]
    another operation x13 -> x4, other arithmetic: 91.7 us -> 8.89 us  [the longest x3 6.2 us: device_fn(): gw_all = jnp.stack(grads)]
  transfers between devices with their start and end apart: 9 -> 20, of which waited for: 8 -> 3; matrix products, arithmetic and copies ran while one was open for 11% -> 17% of each run, Pallas kernels for 0% -> 43%
where the time goes in v1:
time: 1010 us
  Pallas kernels  623 us (62%)
  local copies, waits for them, and re-layouts  121 us (12%)
  blocking collectives  107 us (11%)
  other arithmetic  62.8 us (6%)
  waiting for transfers between devices  46.2 us (5%)
  matrix products  19.9 us (2%)
  between operations  15.6 us (2%)
  starting transfers between devices  11.8 us (1%)
    pallas_call x6, Pallas kernels, block_backward(): pl.pallas_call(functools.partial(bwd_kernel, e), grid=(n_g, n_b), in_spec...  370 us
    pallas_call x2, Pallas kernels, block_forward(): pl.pallas_call(functools.partial(fwd_kernel, e), grid=(n_g, n_b), in_spec...  253 us
    all_gather x1, blocking collectives, device_fn(): b_in_all = lax.all_gather(b_in, 'tp', axis=0, tiled=False)  90.2 us
    unnamed x123, local copies, waits for them, and re-layouts  37 us
    ppermute x6, waiting for transfers between devices, swap_to_samples(): lax.ppermute(lax.dynamic_slice_in_dim(arr, peer * k, k, 0), 'tp', [(i, i...  23.8 us
    ppermute x6, waiting for transfers between devices, swap_to_tokens(): lax.ppermute(lax.dynamic_slice_in_dim(arr, peer * s, s, 2), 'tp', [(i, i...  21.5 us
  transfers between devices with their start and end apart: 20, of which 3 were waited for; matrix products, arithmetic and copies ran while one was open for 17% of the time, Pallas kernels for 43%

profile of v1, /device:TPU:0, one launch (start us, length us, event | category | flops | bytes accessed | tf_op | source)
XLA Modules:
  0.0 1006.6 jit_solution(15601421794734648922)
XLA Ops:
  7.2 4.8 convert_bitcast_fusion
  12.0 3.3 pad_maximum_fusion
  17.3 4.6 constant_dynamic-slice_fusion.5
  21.8 2.4 copy.480
  25.0 2.3 copy.481
  27.3 2.6 collective-permute-start.1
  36.7 4.0 fusion.32
  43.5 90.2 %all-gather = bf16[8,3,448]{2,1,0:T(4,128)(2,1)S(1)} all-gather(bf16[2,3,448]{2,1,0:T(4,128)(2,1)S(1)} %copy.416), channel_id=2, replica_groups=mesh['dp'=4,'tp'=4] {'tp'}, dimensions={0}, use_global_device_ids=true | all-gather | bytes 26880 | tf_op jit(solution)/shard_map/all_gather | solution.py:357
  135.8 2.3 copy.475
  138.1 5.0 gather_fusion
  143.1 8.2 all_gather.24
  151.5 2.7 pad_maximum_fusion.2
  154.3 2.1 broadcast.102.clone
  166.3 2.4 copy.422.bin_ref
  169.5 2.5 copy.426.bin_ref
  174.6 2.1 constant_dynamic-update-slice_fusion.13
  176.7 2.1 constant_dynamic-update-slice_fusion.6
  178.8 2.1 constant_dynamic-update-slice_fusion.12
  180.9 2.1 constant_dynamic-update-slice_fusion.5
  183.0 2.1 constant_dynamic-update-slice_fusion.11.x_ref
  185.1 23.8 %collective-permute-done.8 = bf16[2,768,256]{2,1,0:T(8,128)(2,1)S(1)} collective-permute-done((bf16[2,768,256]{2,1,0:T(8,128)(2,1)S(1)}, bf16[2,768,256]{2,1,0:T(8,128)(2,1)S(1)}, u32[]{:S(2)}, u32[]{:S(2)}) %collective-permute-start.8) | collective-permute-done | bytes 786464 | tf_op jit(solution)/shard_map/ppermute | solution.py:311
  209.8 126.5 %block_fwd.2 = (f32[2,4,3,448,1024]{4,3,2,1,0:T(8,128)}, bf16[2,4,3,64,1024]{4,3,2,1,0:T(8,128)(2,1)}, f32[2,6,2,1024]{3,2,1,0:T(2,128)}, bf16[2,768,1024]{2,1,0...) custom-call(bf16[2,768,1024]{2,1,0:T(8,128)(2,1)} %constant_dynamic-update-slice_fusion.11.x_ref, ...), custom_call_target="tpu_custom_call" | custom-call | flops 54760833024 | bytes 100000000 | tf_op jit(solution)/shard_map/block_fwd/pallas_call | solution.py:220
  336.4 126.4 %block_fwd.3 = (f32[2,4,3,448,1024]{4,3,2,1,0:T(8,128)}, bf16[2,4,3,64,1024]{4,3,2,1,0:T(8,128)(2,1)}, f32[2,6,2,1024]{3,2,1,0:T(2,128)}, bf16[2,768,1024]{2,1,0...) custom-call(bf16[2,768,1024]{2,1,0:T(8,128)(2,1)} %get-tuple-element.52.x_ref, ...), custom_call_target="tpu_custom_call" | custom-call | flops 54760833024 | bytes 100000000 | tf_op jit(solution)/shard_map/block_fwd/pallas_call | solution.py:220
  462.8 6.5 fusion.10
  469.2 61.8 %block_bwd.7 = (bf16[4,1,768,768]{3,2,1,0:T(8,128)(2,1)}, f32[4,1,448,1]{3,2,1,0:T(8,128)}, f32[64,1]{1,0:T(8,128)}, f32[64,1]{1,0:T(8,128)}, f32[2,768,1024]{2,1,0:T(8,128)}) custom-call(bf16[2,768,1024]{2,1,0:T(8,128)(2,1)} %get-tuple-element.191.dbr_ref, bf16[2,768,1024]{2,1,0:T(8,128)(2,1)} %get-tuple-element.54.h_ref, ...), custom_call_target="tpu_custom_call" | custom-call | flops 40802189312 | bytes 100000000 | tf_op jit(solution)/shard_map/block_bwd/pallas_call | solution.py:266
  531.1 61.7 %block_bwd.6 = (bf16[4,1,768,768]{3,2,1,0:T(8,128)(2,1)}, f32[4,1,448,1]{3,2,1,0:T(8,128)}, f32[64,1]{1,0:T(8,128)}, f32[64,1]{1,0:T(8,128)}, f32[2,768,1024]{2,1,0:T(8,128)}) custom-call(bf16[2,768,1024]{2,1,0:T(8,128)(2,1)} %get-tuple-element.191.dbr_ref, bf16[2,768,1024]{2,1,0:T(8,128)(2,1)} %get-tuple-element.54.h_ref, ...), custom_call_target="tpu_custom_call" | custom-call | flops 40802189312 | bytes 100000000 | tf_op jit(solution)/shard_map/block_bwd/pallas_call | solution.py:266
  592.9 61.5 %block_bwd.8 = (bf16[4,1,768,768]{3,2,1,0:T(8,128)(2,1)}, f32[4,1,448,1]{3,2,1,0:T(8,128)}, f32[64,1]{1,0:T(8,128)}, f32[64,1]{1,0:T(8,128)}, f32[2,768,1024]{2,1,0:T(8,128)}) custom-call(bf16[2,768,1024]{2,1,0:T(8,128)(2,1)} %get-tuple-element.191.dbr_ref, bf16[2,768,1024]{2,1,0:T(8,128)(2,1)} %get-tuple-element.54.h_ref, ...), custom_call_target="tpu_custom_call" | custom-call | flops 40802189312 | bytes 100000000 | tf_op jit(solution)/shard_map/block_bwd/pallas_call | solution.py:266
  659.0 7.3 fusion.22
  666.4 5.2 fusion.12
  673.4 2.2 fusion.13.dbr_ref
  675.6 61.6 %block_bwd.10 = (bf16[4,1,768,768]{3,2,1,0:T(8,128)(2,1)}, f32[4,1,448,1]{3,2,1,0:T(8,128)}, f32[64,1]{1,0:T(8,128)}, f32[64,1]{1,0:T(8,128)}, f32[2,768,1024]{2,1,0:T(8,128)}) custom-call(bf16[2,768,1024]{2,1,0:T(8,128)(2,1)} %fusion.13.dbr_ref, bf16[2,768,1024]{2,1,0:T(8,128)(2,1)} %get-tuple-element.61.h_ref, bf16[1,4,3,768,768]{4,3,2,1,0:T(8,128)(2,1)} %bitcast.137, ...), custom_call_target="tpu_custom_call" | custom-call | flops 40802189312 | bytes 100000000 | tf_op jit(solution)/shard_map/block_bwd/pallas_call | solution.py:266
  737.3 61.5 %block_bwd.9 = (bf16[4,1,768,768]{3,2,1,0:T(8,128)(2,1)}, f32[4,1,448,1]{3,2,1,0:T(8,128)}, f32[64,1]{1,0:T(8,128)}, f32[64,1]{1,0:T(8,128)}, f32[2,768,1024]{2,1,0:T(8,128)}) custom-call(bf16[2,768,1024]{2,1,0:T(8,128)(2,1)} %fusion.13.dbr_ref, bf16[2,768,1024]{2,1,0:T(8,128)(2,1)} %get-tuple-element.61.h_ref, bf16[1,4,3,768,768]{4,3,2,1,0:T(8,128)(2,1)} %bitcast.138, ...), custom_call_target="tpu_custom_call" | custom-call | flops 40802189312 | bytes 100000000 | tf_op jit(solution)/shard_map/block_bwd/pallas_call | solution.py:266
  798.9 61.5 %block_bwd.11 = (bf16[4,1,768,768]{3,2,1,0:T(8,128)(2,1)}, f32[4,1,448,1]{3,2,1,0:T(8,128)}, f32[64,1]{1,0:T(8,128)}, f32[64,1]{1,0:T(8,128)}, f32[2,768,1024]{2,1,0:T(8,128)}) custom-call(bf16[2,768,1024]{2,1,0:T(8,128)(2,1)} %fusion.13.dbr_ref, bf16[2,768,1024]{2,1,0:T(8,128)(2,1)} %get-tuple-element.61.h_ref, bf16[1,4,3,768,768]{4,3,2,1,0:T(8,128)(2,1)} %bitcast.139, ...), custom_call_target="tpu_custom_call" | custom-call | flops 40802189312 | bytes 100000000 | tf_op jit(solution)/shard_map/block_bwd/pallas_call | solution.py:266
  862.3 2.6 convert_reduce_fusion
  864.9 2.7 fusion.18
  868.9 11.5 %fusion.17 = (f32[2,768]{1,0:T(2,128)S(1)}, f32[2,1024]{1,0:T(2,128)S(1)}, f32[2,1024]{1,0:T(2,128)S(1)}, f32[2,768]{1,0:T(2,128)S(1)}, f32[2,768,1024]{2,1,0:T(8,128)}) fusion(bf16[2,768,1024]{2,1,0:T(8,128)(2,1)} %constant_dynamic-update-slice_fusion.11.x_ref, f32[2,1024]{1,0:T(2,128)S(1)} %add_rsqrt_fusion, f32[2,1024]{1,0:T(2,128)S(1)} %broadcast_multiply_fusion.2, ...), kind=kLoop, calls=%fused_computation.38 | loop fusion | flops 18867200 | bytes 28362752 | tf_op jit(solution)/shard_map/reduce_sum | solution.py:398
  889.6 4.9 fusion.26
  897.2 8.6 all-gather.2
  916.7 7.1 convolution_bitcast_fusion
  924.5 15.7 %copy.467 = f32[2,768,2304]{2,1,0:T(8,128)} copy(f32[2,768,2304]{1,2,0:T(8,128)} %convolution_bitcast_fusion) | data formatting | bytes 28311552
  940.6 2.0 gather_fusion.3
  957.3 8.2 collective-permute-done.4
  965.5 2.3 copy.431
  967.8 13.3 %collective-permute-done.5 = bf16[2,768,256]{2,1,0:T(8,128)(2,1)} collective-permute-done((bf16[2,768,256]{2,1,0:T(8,128)(2,1)}, bf16[2,768,256]{2,1,0:T(8,128)(2,1)}, u32[]{:S(2)}, u32[]{:S(2)}) %collective-permute-start.5) | collective-permute-done | bytes 786464 | tf_op jit(solution)/shard_map/ppermute | solution.py:324
  981.1 2.3 copy.432
  989.0 2.2 maximum_bitcast_fusion.1
  991.3 2.2 maximum_bitcast_fusion
  995.3 4.0 convert_bitcast_fusion.1
  (264 shorter events, 84.1 us)
Async XLA Ops:
  7.2 202.7 %all-gather.6.cloned.1.call-start = ((), (), s32[]{:S(2)}) async-start(), calls=%async_computation.6 | async-start | bytes 17694720 | tf_op jit(solution)/shard_map/all_gather | solution.py:352
  15.4 321.0 %all-gather.8.cloned.1.call-start = ((), (), s32[]{:S(2)}) async-start(), calls=%async_computation.7 | async-start | bytes 17694720 | tf_op jit(solution)/shard_map/all_gather | solution.py:352
  16.2 972.8 %reduce-scatter.15.cloned.1.call-start = ((), (), s32[]{:S(2)}) async-start(), calls=%async_computation.12 | async-start | bytes 5898240 | tf_op jit(solution)/shard_map/reduce_scatter | solution.py:392
  21.8 8.1 copy-start.17
  21.8 9.2 copy-start.16
  21.8 10.5 %copy-start.15 = (bf16[2,256,768]{2,1,0:T(8,128)(2,1)S(1)}, bf16[2,256,768]{2,1,0:T(8,128)(2,1)}, u32[]{:S(2)}) copy-start(bf16[2,256,768]{2,1,0:T(8,128)(2,1)} %get-tuple-element.197) | copy-start | bytes 2359300
  24.3 11.2 %copy-start.14 = (bf16[2,256,768]{2,1,0:T(8,128)(2,1)S(1)}, bf16[2,256,768]{2,1,0:T(8,128)(2,1)}, u32[]{:S(2)}) copy-start(bf16[2,256,768]{2,1,0:T(8,128)(2,1)} %get-tuple-element.227) | copy-start | bytes 2359300
  24.3 148.0 %collective-permute-start = (bf16[2,768,256]{2,1,0:T(8,128)(2,1)}, bf16[2,768,256]{2,1,0:T(8,128)(2,1)}, u32[]{:S(2)}, u32[]{:S(2)}) collective-permute-start(bf16[2,768,256]{2,1,0:T(8,128)(2,1)} %bitcast.123), channel_id=1, source_target_pairs={{0,1},{1,0},{2,3},{3,2},{4,5},{5,4},{6,7},{7,6},{8,9},{9,8},{10,11... | collective-permute-start | bytes 2359304 | tf_op jit(solution)/shard_map/ppermute | solution.py:311
  27.3 9.4 copy-start.42
  27.3 9.4 copy-start.28
  27.3 151.5 %collective-permute-start.1 = (bf16[2,768,256]{2,1,0:T(8,128)(2,1)}, bf16[2,768,256]{2,1,0:T(8,128)(2,1)}, u32[]{:S(2)}, u32[]{:S(2)}) collective-permute-start(bf16[2,768,256]{2,1,0:T(8,128)(2,1)} %bitcast.122), channel_id=1, source_target_pairs={{0,2},{1,3},{2,0},{3,1},{4,6},{5,7},{6,4},{7,5},{8,10},{9,11},{10,... | collective-permute-start | bytes 2359304 | tf_op jit(solution)/shard_map/ppermute | solution.py:311
  31.0 152.0 %collective-permute-start.2 = (bf16[2,768,256]{2,1,0:T(8,128)(2,1)}, bf16[2,768,256]{2,1,0:T(8,128)(2,1)}, u32[]{:S(2)}, u32[]{:S(2)}) collective-permute-start(bf16[2,768,256]{2,1,0:T(8,128)(2,1)} %bitcast.121), channel_id=1, source_target_pairs={{0,3},{1,2},{2,1},{3,0},{4,7},{5,6},{6,5},{7,4},{8,11},{9,10},{10,... | collective-permute-start | bytes 2359304 | tf_op jit(solution)/shard_map/ppermute | solution.py:311
  32.3 144.4 %collective-permute-start.6 = (bf16[2,768,256]{2,1,0:T(8,128)(2,1)}, bf16[2,768,256]{2,1,0:T(8,128)(2,1)}, u32[]{:S(2)}, u32[]{:S(2)}) collective-permute-start(bf16[2,768,256]{2,1,0:T(8,128)(2,1)} %bitcast.30), channel_id=1, source_target_pairs={{0,1},{1,0},{2,3},{3,2},{4,5},{5,4},{6,7},{7,6},{8,9},{9,8},{10,11... | collective-permute-start | bytes 2359304 | tf_op jit(solution)/shard_map/ppermute | solution.py:311
  33.5 147.3 %collective-permute-start.7 = (bf16[2,768,256]{2,1,0:T(8,128)(2,1)}, bf16[2,768,256]{2,1,0:T(8,128)(2,1)}, u32[]{:S(2)}, u32[]{:S(2)}) collective-permute-start(bf16[2,768,256]{2,1,0:T(8,128)(2,1)} %bitcast.31), channel_id=1, source_target_pairs={{0,2},{1,3},{2,0},{3,1},{4,6},{5,7},{6,4},{7,5},{8,10},{9,11},{10,... | collective-permute-start | bytes 2359304 | tf_op jit(solution)/shard_map/ppermute | solution.py:311
  41.3 96.8 %copy-start.47 = (s32[448]{0:T(512)S(1)}, s32[448]{0:T(512)}, u32[]{:S(2)}) copy-start(s32[448]{0:T(512)} %constant.75) | copy-start | bytes 5380
  41.3 101.8 %copy-start.38 = (f32[256,32]{0,1:T(8,128)S(1)}, f32[256,32]{0,1:T(8,128)}, u32[]{:S(2)}) copy-start(f32[256,32]{0,1:T(8,128)} %param.27) | copy-start | bytes 98308
  41.3 101.8 %copy-start.39 = (f32[256,32]{0,1:T(8,128)S(1)}, f32[256,32]{0,1:T(8,128)}, u32[]{:S(2)}) copy-start(f32[256,32]{0,1:T(8,128)} %param.26) | copy-start | bytes 98308
  41.3 109.9 %copy-start.45 = (bf16[2,768]{1,0:T(2,128)(2,1)S(1)}, bf16[2,768]{1,0:T(2,128)(2,1)}, u32[]{:S(2)}) copy-start(bf16[2,768]{1,0:T(2,128)(2,1)} %param.35) | copy-start | bytes 9220
  172.3 36.5 %collective-permute-start.8 = (bf16[2,768,256]{2,1,0:T(8,128)(2,1)S(1)}, bf16[2,768,256]{2,1,0:T(8,128)(2,1)S(1)}, u32[]{:S(2)}, u32[]{:S(2)}) collective-permute-start(bf16[2,768,256]{2,1,0:T(8,128)(2,1)S(1)} %bitcast.124), channel_id=1, source_target_pairs={{0,3},{1,2},{2,1},{3,0},{4,7},{5,6},{6,5},{7,4},{8,11},{9,10},{10,... | collective-permute-start | bytes 2359304 | tf_op jit(solution)/shard_map/ppermute | solution.py:311
  531.1 457.9 %reduce-scatter.13.cloned.1.call-start = ((), (), s32[]{:S(2)}) async-start(), calls=%async_computation.11 | async-start | bytes 5898240 | tf_op jit(solution)/shard_map/reduce_scatter | solution.py:392
  592.8 396.2 %reduce-scatter.17.cloned.1.call-start = ((), (), s32[]{:S(2)}) async-start(), calls=%async_computation.13 | async-start | bytes 5898240 | tf_op jit(solution)/shard_map/reduce_scatter | solution.py:392
  654.4 336.8 %reduce-scatter.9.cloned.1.call-start = ((), (), s32[]{:S(2)}) async-start(), calls=%async_computation.9 | async-start | bytes 5898240 | tf_op jit(solution)/shard_map/reduce_scatter | solution.py:392
  657.7 8.7 slice-start
  659.0 7.4 copy-start.25
  737.2 254.0 %reduce-scatter.7.cloned.1.call-start = ((), (), s32[]{:S(2)}) async-start(), calls=%async_computation.8 | async-start | bytes 5898240 | tf_op jit(solution)/shard_map/reduce_scatter | solution.py:392
  798.8 192.4 %reduce-scatter.11.cloned.1.call-start = ((), (), s32[]{:S(2)}) async-start(), calls=%async_computation.10 | async-start | bytes 5898240 | tf_op jit(solution)/shard_map/reduce_scatter | solution.py:392
  868.8 11.7 %copy-start.37 = (f32[64,1]{1,0:T(8,128)S(1)}, f32[64,1]{1,0:T(8,128)}, u32[]{:S(2)}) copy-start(f32[64,1]{1,0:T(8,128)} %get-tuple-element.73) | copy-start | bytes 772
  868.8 13.2 %copy-start.36 = (f32[64,1]{1,0:T(8,128)S(1)}, f32[64,1]{1,0:T(8,128)}, u32[]{:S(2)}) copy-start(f32[64,1]{1,0:T(8,128)} %get-tuple-element.70) | copy-start | bytes 772
  868.8 19.5 %copy-start.40 = (f32[2,768]{1,0:T(2,128)S(1)}, f32[2,768]{1,0:T(2,128)}, u32[]{:S(2)}) copy-start(f32[2,768]{1,0:T(2,128)} %get-tuple-element.185) | copy-start | bytes 18436
  868.8 20.3 %copy-start.31 = (f32[64,1]{1,0:T(8,128)S(1)}, f32[64,1]{1,0:T(8,128)}, u32[]{:S(2)}) copy-start(f32[64,1]{1,0:T(8,128)} %get-tuple-element.83) | copy-start | bytes 772
  868.9 20.3 %copy-start.33 = (f32[64,1]{1,0:T(8,128)S(1)}, f32[64,1]{1,0:T(8,128)}, u32[]{:S(2)}) copy-start(f32[64,1]{1,0:T(8,128)} %get-tuple-element.82) | copy-start | bytes 772
  868.9 20.3 %copy-start.35 = (f32[64,1]{1,0:T(8,128)S(1)}, f32[64,1]{1,0:T(8,128)}, u32[]{:S(2)}) copy-start(f32[64,1]{1,0:T(8,128)} %get-tuple-element.84) | copy-start | bytes 772
  880.4 8.9 copy-start.30
  880.4 8.9 copy-start.32
  880.4 8.9 copy-start.34
  880.4 9.0 copy-start.41
  880.4 9.1 copy-start.2
  894.5 18.6 %copy-start.4 = (bf16[2,768,1024]{2,1,0:T(8,128)(2,1)S(1)}, bf16[2,768,1024]{2,1,0:T(8,128)(2,1)}, u32[]{:S(2)}) copy-start(bf16[2,768,1024]{2,1,0:T(8,128)(2,1)} %get-tuple-element.53) | copy-start | bytes 9437188
  896.3 27.5 %collective-permute-start.9 = (bf16[2,768,256]{2,1,0:T(8,128)(2,1)}, bf16[2,768,256]{2,1,0:T(8,128)(2,1)}, u32[]{:S(2)}, u32[]{:S(2)}) collective-permute-start(bf16[2,768,256]{2,1,0:T(8,128)(2,1)} %get-tuple-element.194), channel_id=1, source_target_pairs={{0,1},{1,0},{2,3},{3,2},{4,5},{5,4},{6,7},{7,6},{8,9},{9,8},{10,11... | collective-permute-start | bytes 2359304 | tf_op jit(solution)/shard_map/ppermute | solution.py:324
  906.5 10.2 %copy-start.29 = (bf16[8,768]{1,0:T(8,128)(2,1)S(1)}, bf16[8,768]{1,0:T(8,128)(2,1)}, u32[]{:S(2)}) copy-start(bf16[8,768]{1,0:T(8,128)(2,1)} %param.25) | copy-start | bytes 36868
  911.4 41.6 %collective-permute-start.10 = (bf16[2,768,256]{2,1,0:T(8,128)(2,1)}, bf16[2,768,256]{2,1,0:T(8,128)(2,1)}, u32[]{:S(2)}, u32[]{:S(2)}) collective-permute-start(bf16[2,768,256]{2,1,0:T(8,128)(2,1)} %get-tuple-element.193), channel_id=1, source_target_pairs={{0,2},{1,3},{2,0},{3,1},{4,6},{5,7},{6,4},{7,5},{8,10},{9,11},{10,... | collective-permute-start | bytes 2359304 | tf_op jit(solution)/shard_map/ppermute | solution.py:324
  912.8 41.7 %collective-permute-start.11 = (bf16[2,768,256]{2,1,0:T(8,128)(2,1)}, bf16[2,768,256]{2,1,0:T(8,128)(2,1)}, u32[]{:S(2)}, u32[]{:S(2)}) collective-permute-start(bf16[2,768,256]{2,1,0:T(8,128)(2,1)} %get-tuple-element.192), channel_id=1, source_target_pairs={{0,3},{1,2},{2,1},{3,0},{4,7},{5,6},{6,5},{7,4},{8,11},{9,10},{10,... | collective-permute-start | bytes 2359304 | tf_op jit(solution)/shard_map/ppermute | solution.py:324
  914.9 41.0 %collective-permute-start.3 = (bf16[2,768,256]{2,1,0:T(8,128)(2,1)}, bf16[2,768,256]{2,1,0:T(8,128)(2,1)}, u32[]{:S(2)}, u32[]{:S(2)}) collective-permute-start(bf16[2,768,256]{2,1,0:T(8,128)(2,1)} %get-tuple-element.202), channel_id=1, source_target_pairs={{0,1},{1,0},{2,3},{3,2},{4,5},{5,4},{6,7},{7,6},{8,9},{9,8},{10,11... | collective-permute-start | bytes 2359304 | tf_op jit(solution)/shard_map/ppermute | solution.py:324
  915.3 50.2 %collective-permute-start.4 = (bf16[2,768,256]{2,1,0:T(8,128)(2,1)}, bf16[2,768,256]{2,1,0:T(8,128)(2,1)}, u32[]{:S(2)}, u32[]{:S(2)}) collective-permute-start(bf16[2,768,256]{2,1,0:T(8,128)(2,1)} %get-tuple-element.201), channel_id=1, source_target_pairs={{0,2},{1,3},{2,0},{3,1},{4,6},{5,7},{6,4},{7,5},{8,10},{9,11},{10,... | collective-permute-start | bytes 2359304 | tf_op jit(solution)/shard_map/ppermute | solution.py:324
  923.8 57.3 %collective-permute-start.5 = (bf16[2,768,256]{2,1,0:T(8,128)(2,1)}, bf16[2,768,256]{2,1,0:T(8,128)(2,1)}, u32[]{:S(2)}, u32[]{:S(2)}) collective-permute-start(bf16[2,768,256]{2,1,0:T(8,128)(2,1)} %get-tuple-element.200), channel_id=1, source_target_pairs={{0,3},{1,2},{2,1},{3,0},{4,7},{5,6},{6,5},{7,4},{8,11},{9,10},{10,... | collective-permute-start | bytes 2359304 | tf_op jit(solution)/shard_map/ppermute | solution.py:324
  924.5 16.1 %copy-start.43 = (s32[1024]{0:T(1024)S(1)}, s32[1024]{0:T(1024)}, u32[]{:S(2)}) copy-start(s32[1024]{0:T(1024)} %pad_clamp_fusion.1) | copy-start | bytes 12292
  924.5 21.9 %copy-start.10 = (bf16[2,768,256]{2,1,0:T(8,128)(2,1)S(1)}, bf16[2,768,256]{2,1,0:T(8,128)(2,1)}, u32[]{:S(2)}) copy-start(bf16[2,768,256]{2,1,0:T(8,128)(2,1)} %get-tuple-element.195) | copy-start | bytes 2359300
  924.5 22.2 %copy-start.11 = (bf16[2,768,256]{2,1,0:T(8,128)(2,1)S(1)}, bf16[2,768,256]{2,1,0:T(8,128)(2,1)}, u32[]{:S(2)}) copy-start(bf16[2,768,256]{2,1,0:T(8,128)(2,1)} %get-tuple-element.203) | copy-start | bytes 2359300
  (27 other events, 106.2 us)
Sparse Core Ops, SparseCore 0:
  15.5 144.9 all-gather.5
  162.6 106.7 all-gather.7
  531.2 45.0 reduce-scatter.14
  592.9 45.0 reduce-scatter.12
  654.5 45.0 reduce-scatter.16
  737.4 45.0 reduce-scatter.8
  799.0 45.0 reduce-scatter.6
  860.6 46.8 reduce-scatter.10

commit v2 on v1

v2 whole, which is shorter than its diff:
```python
import functools
import jax
import jax.numpy as jnp
import numpy as np
from jax import lax
from jax.experimental import pallas as pl
from jax.experimental.pallas import tpu as pltpu
from jax.sharding import PartitionSpec as P

NORM_EPS = 1e-6
LOG2E = 1.4426950408889634
GELU_C = 0.7978845608028654
GELU_A = 0.044715
F32 = jnp.float32
BF16 = jnp.bfloat16
CHUNK = 256
VMEM = 63 * 1024 * 1024


def dot_nn(a, b):
    return lax.dot_general(a, b, (((1,), (0,)), ((), ())), preferred_element_type=F32)


def dot_nt(a, b):
    return lax.dot_general(a, b, (((1,), (1,)), ((), ())), preferred_element_type=F32)


def dot_tn(a, b):
    return lax.dot_general(a, b, (((0,), (0,)), ((), ())), preferred_element_type=F32)


def norm_rope(raw, scale_col, cos_t, sin_t):
    half = raw.shape[0] // 2
    inv = lax.rsqrt(jnp.mean(raw * raw, axis=0, keepdims=True) + NORM_EPS)
    hat = raw * inv
    scaled = hat * scale_col
    a, b = scaled[:half], scaled[half:]
    rot = jnp.concatenate([a * cos_t - b * sin_t, a * sin_t + b * cos_t], axis=0)
    return hat, inv, rot.astype(BF16)


def norm_rope_bwd(d_rot, hat, inv, scale_col, cos_t, sin_t):
    half = d_rot.shape[0] // 2
    da, db = d_rot[:half], d_rot[half:]
    d_scaled = jnp.concatenate([da * cos_t + db * sin_t, db * cos_t - da * sin_t], axis=0)
    d_scale = jnp.sum(d_scaled * hat, axis=1, keepdims=True)
    d_hat = d_scaled * scale_col
    d_raw = inv * (d_hat - hat * jnp.mean(d_hat * hat, axis=0, keepdims=True))
    return d_raw, d_scale


def softmax_head(q_rot, k_rot, v_t, o_ref, lse_ref, i, mul):
    n_c = q_rot.shape[1] // CHUNK
    spans = [slice(c * CHUNK, (c + 1) * CHUNK) for c in range(n_c)]
    nxt = dot_tn(k_rot, q_rot[:, spans[0]])
    outs = []
    for c in range(n_c):
        s = nxt
        if c + 1 < n_c:
            nxt = dot_tn(k_rot, q_rot[:, spans[c + 1]])
        top = jnp.max(s, axis=0, keepdims=True) * mul
        p = jnp.exp2(s * mul - top)
        tot = jnp.sum(p, axis=0, keepdims=True)
        out = (dot_nn(v_t, p.astype(BF16)) * (1.0 / tot)).astype(BF16)
        o_ref[0, 0, i, 0, :, spans[c]] = out
        outs.append(out)
        lse_ref[0, 0, 0, i:i + 1, spans[c]] = top + jnp.log2(tot)
    return jnp.concatenate(outs, axis=1)


def fwd_kernel(e, first, last, token_in, token_out, *refs):
    refs = list(refs)
    mod_ref, w_ref, bin_ref, qs_ref, ks_ref, cos_ref, sin_ref, x_ref = refs[:8]
    refs = refs[8:]
    if not first:
        h_in, z_in = refs[:2]
        refs = refs[5:]
    y_ref, o_ref, lse_ref = refs[:3]
    refs = refs[3:]
    if first:
        h_ref = refs.pop(0)
        if token_in:
            xt_ref = refs.pop(0)
    if last:
        br_ref, xo_ref = refs.pop(0), refs.pop(0)
    else:
        z_out = refs.pop(0)
    z_sc, h_sc = refs
    g, b = pl.program_id(0), pl.program_id(1)
    final = pl.num_programs(0) - 1
    cols = bin_ref.shape[2]

    @pl.when(g == 0)
    def _():
        if first:
            if token_in:
                x = jnp.concatenate([x_ref[t, 0].astype(F32).T for t in range(x_ref.shape[0])], axis=1)
                xt_ref[0] = x.astype(BF16)
            else:
                x = x_ref[0].astype(F32)
            cent = x - jnp.mean(x, axis=0, keepdims=True)
            normed = cent * lax.rsqrt(jnp.mean(cent * cent, axis=0, keepdims=True) + NORM_EPS)
            h = (normed * (1.0 + mod_ref[0, :, 1:2]) + mod_ref[0, :, 0:1]).astype(BF16)
            h_sc[b] = h
            h_ref[0] = h
        else:
            h_sc[b] = h_in[0]
            z_sc[b] = z_in[0]

    h_t = h_sc[b]
    cos_t, sin_t = cos_ref[...], sin_ref[...]
    mul = (e ** -0.5) * LOG2E
    joined = []
    ys = []
    for i in range(2):
        y = dot_nn(w_ref[i, 0, :cols], h_t) + bin_ref[i, 0]
        y_ref[0, 0, i, 0] = y
        ys.append(y)
    for i in range(2):
        y = ys[i]
        q_rot = norm_rope(y[:e], qs_ref[...], cos_t, sin_t)[2]
        k_rot = norm_rope(y[e:2 * e], ks_ref[...], cos_t, sin_t)[2]
        joined.append(softmax_head(q_rot, k_rot, y[2 * e:3 * e].astype(BF16), o_ref, lse_ref, i, mul))
        u = y[3 * e:]
        t = jnp.tanh(GELU_C * (u + GELU_A * u * u * u))
        joined.append((0.5 * u * (1.0 + t)).astype(BF16))
    z = dot_tn(jnp.concatenate([w_ref[0, 0, cols:], w_ref[1, 0, cols:]], axis=0), jnp.concatenate(joined, axis=0))

    if first:
        @pl.when(g == 0)
        def _():
            z_sc[b] = z

        @pl.when(jnp.logical_and(g > 0, g < final))
        def _():
            z_sc[b] += z
    else:
        @pl.when(g < final)
        def _():
            z_sc[b] += z

    @pl.when(g == final)
    def _():
        total = z_sc[b] + z
        if last:
            branch = total + mod_ref[0, :, 3:4]
            br_ref[0] = branch
            x_new = x_ref[0].astype(F32) + mod_ref[0, :, 2:3] * branch
            if token_out:
                n_t, s_t = xo_ref.shape[0], xo_ref.shape[2]
                for t in range(n_t):
                    xo_ref[t, 0] = x_new[:, t * s_t:(t + 1) * s_t].T.astype(BF16)
            else:
                xo_ref[0] = x_new.astype(BF16)
        else:
            z_out[0] = total


def bwd_kernel(e, chip_ref, dbr_ref, h_ref, wa_ref, wb_ref, qs_ref, ks_ref, cos_ref, sin_ref, y_ref, o_ref, lse_ref, gw_ref, gb_ref, dqs_ref, dks_ref, dh_ref, dh_sc, acc_sc, dj_sc, dp_sc, jn_sc):
    g, b = pl.program_id(0), pl.program_id(1)
    last = pl.num_programs(0) - 1
    cols = y_ref.shape[4]
    rows = dj_sc.shape[0] // 2
    s_len = dbr_ref.shape[2]
    d_br = dbr_ref[0]
    cos_t, sin_t = cos_ref[...], sin_ref[...]
    scale = e ** -0.5
    mul = scale * LOG2E
    own = lax.rem(g, 2) == 0
    ws = [jnp.where(own, wa_ref[i, 0], wb_ref[i, 0]) for i in range(2)]
    for i in range(2):
        dj_sc[i * rows:(i + 1) * rows] = dot_nn(ws[i][cols:], d_br).astype(BF16)

    @pl.when(jnp.logical_and(g == 0, b == 0))
    def _():
        dqs_ref[...] = jnp.zeros_like(dqs_ref)
        dks_ref[...] = jnp.zeros_like(dks_ref)

    @pl.when(b == 0)
    def _():
        gb_ref[...] = jnp.zeros_like(gb_ref)

    for i in range(2):
        base = i * cols
        q_hat, q_inv, q_rot = norm_rope(y_ref[0, 0, i, 0, :e], qs_ref[...], cos_t, sin_t)
        k_hat, k_inv, k_rot = norm_rope(y_ref[0, 0, i, 0, e:2 * e], ks_ref[...], cos_t, sin_t)
        v_t = y_ref[0, 0, i, 0, 2 * e:3 * e].astype(BF16)
        o_t = o_ref[0, 0, i, 0]
        d_o = dj_sc[i * rows:i * rows + e]
        d_sum = jnp.sum(d_o.astype(F32) * o_t.astype(F32), axis=0, keepdims=True)
        d_q, d_k, d_v = [], None, None
        for c in range(s_len // CHUNK):
            span = slice(c * CHUNK, (c + 1) * CHUNK)
            s = dot_tn(k_rot, q_rot[:, span])
            p = jnp.exp2(s * mul - lse_ref[0, 0, 0, i:i + 1, span])
            d_p = dot_tn(v_t, d_o[:, span])
            d_s = (p * (d_p - d_sum[:, span])).astype(BF16)
            d_q.append(dot_nn(k_rot, d_s))
            kc = dot_nt(q_rot[:, span], d_s)
            vc = dot_nt(d_o[:, span], p.astype(BF16))
            d_k = kc if d_k is None else d_k + kc
            d_v = vc if d_v is None else d_v + vc
        d_q = jnp.concatenate(d_q, axis=1) * scale
        d_qraw, d_qs = norm_rope_bwd(d_q, q_hat, q_inv, qs_ref[...], cos_t, sin_t)
        d_kraw, d_ks = norm_rope_bwd(d_k * scale, k_hat, k_inv, ks_ref[...], cos_t, sin_t)
        dqs_ref[...] += d_qs
        dks_ref[...] += d_ks
        u = y_ref[0, 0, i, 0, 3 * e:]
        t = jnp.tanh(GELU_C * (u + GELU_A * u * u * u))
        half = 0.5 * (1.0 + t)
        jn_sc[i * rows:i * rows + e] = o_t
        jn_sc[i * rows + e:(i + 1) * rows] = (u * half).astype(BF16)
        slope = half + 0.5 * u * (1.0 - t * t) * (GELU_C * (1.0 + 3.0 * GELU_A * u * u))
        d_u = dj_sc[i * rows + e:(i + 1) * rows].astype(F32) * slope
        off = 0
        for part in (d_qraw, d_kraw, d_v, d_u):
            n = part.shape[0]
            dp_sc[base + off:base + off + n] = part.astype(BF16)
            gb_ref[0, i, 0, off:off + n] += jnp.sum(part, axis=1, keepdims=True)
            off += n

    h_t = h_ref[0]
    gwi = dot_nt(dp_sc[...], h_t)
    gwo = dot_nt(jn_sc[...], d_br)
    d_h = dot_tn(jnp.concatenate([ws[0][:cols], ws[1][:cols]], axis=0), dp_sc[...])

    @pl.when(b == 0)
    def _():
        acc_sc[:2 * cols] = gwi
        acc_sc[2 * cols:] = gwo

    @pl.when(b > 0)
    def _():
        for i in range(2):
            gw_ref[0, i, 0, :cols] = (acc_sc[i * cols:(i + 1) * cols] + gwi[i * cols:(i + 1) * cols]).astype(BF16)
            lo = 2 * cols + i * rows
            gw_ref[0, i, 0, cols:] = (acc_sc[lo:lo + rows] + gwo[i * rows:(i + 1) * rows]).astype(BF16)

    @pl.when(g == 0)
    def _():
        dh_sc[b] = d_h

    @pl.when(jnp.logical_and(g > 0, g < last))
    def _():
        dh_sc[b] += d_h

    @pl.when(g == last)
    def _():
        dh_ref[0] = dh_sc[b] + d_h


def edge_kernel(has_exit, has_entry, token_g, token_out, *refs):
    refs = list(refs)
    g_ref = refs.pop(0)
    if has_exit:
        x_ref, mod_ref = refs.pop(0), refs.pop(0)
        dh_refs = [refs.pop(0) for _ in range(has_exit)]
    if has_entry:
        mod2_ref, br_ref = refs.pop(0), refs.pop(0)
    if has_exit:
        gx_ref, dmod_ref = refs.pop(0), refs.pop(0)
    if has_entry:
        if token_g:
            gt_ref = refs.pop(0)
        dbr_ref, dent_ref = refs.pop(0), refs.pop(0)
    if token_g:
        grad = jnp.concatenate([g_ref[t, 0].astype(F32).T for t in range(g_ref.shape[0])], axis=1)
        gt_ref[0] = grad.astype(BF16)
    else:
        grad = g_ref[0].astype(F32)
    if has_exit:
        d_h = dh_refs[0][0]
        for ref in dh_refs[1:]:
            d_h = d_h + ref[0]
        x = x_ref[0].astype(F32)
        cent = x - jnp.mean(x, axis=0, keepdims=True)
        inv = lax.rsqrt(jnp.mean(cent * cent, axis=0, keepdims=True) + NORM_EPS)
        hat = cent * inv
        dmod_ref[0, :, 0:1] = jnp.sum(d_h, axis=1, keepdims=True)
        dmod_ref[0, :, 1:2] = jnp.sum(d_h * hat, axis=1, keepdims=True)
        d_hat = d_h * (1.0 + mod_ref[0, :, 1:2])
        d_x = inv * (d_hat - jnp.mean(d_hat, axis=0, keepdims=True) - hat * jnp.mean(d_hat * hat, axis=0, keepdims=True))
        if token_out:
            s_t = gx_ref.shape[2]
            for t in range(gx_ref.shape[0]):
                span = slice(t * s_t, (t + 1) * s_t)
                gx_ref[t, 0] = (grad[:, span] + d_x[:, span]).T.astype(BF16)
        else:
            grad16 = (grad + d_x).astype(BF16)
            gx_ref[0] = grad16
            grad = grad16.astype(F32)
    if has_entry:
        dent_ref[0, :, 0:1] = jnp.sum(grad * br_ref[0], axis=1, keepdims=True)
        gated = grad * mod2_ref[0, :, 2:3]
        dent_ref[0, :, 1:2] = jnp.sum(gated, axis=1, keepdims=True)
        dbr_ref[0] = gated.astype(BF16)


def edge(grad, exit_args, entry_args, token_g, token_out):
    if token_g:
        n_t, n_b, s_t, dim = grad.shape
        s_len = n_t * s_t
    else:
        n_b, dim, s_len = grad.shape
    act = pl.BlockSpec((1, dim, s_len), lambda b: (b, 0, 0))
    small = lambda k: pl.BlockSpec((1, dim, k), lambda b: (b, 0, 0))
    tok = lambda n, s: pl.BlockSpec((n, 1, s, dim), lambda b: (0, b, 0, 0))
    args, in_specs, out_specs, out_shape = [grad], [tok(n_t, s_t) if token_g else act], [], []
    n_exit = 0
    if exit_args:
        x_t, mod_l, d_hs = exit_args
        n_exit = len(d_hs)
        args += [x_t, mod_l, *d_hs]
        in_specs += [act, small(4)] + [act] * n_exit
        if token_out:
            out_specs.append(tok(token_out, s_len // token_out))
            out_shape.append(jax.ShapeDtypeStruct((token_out, n_b, s_len // token_out, dim), BF16))
        else:
            out_specs.append(act)
            out_shape.append(jax.ShapeDtypeStruct((n_b, dim, s_len), BF16))
        out_specs.append(small(2))
        out_shape.append(jax.ShapeDtypeStruct((n_b, dim, 2), F32))
    if entry_args:
        mod_2, branch = entry_args
        args += [mod_2, branch]
        in_specs += [small(4), act]
        if token_g:
            out_specs.append(act)
            out_shape.append(jax.ShapeDtypeStruct((n_b, dim, s_len), BF16))
        out_specs += [act, small(2)]
        out_shape += [jax.ShapeDtypeStruct((n_b, dim, s_len), BF16), jax.ShapeDtypeStruct((n_b, dim, 2), F32)]
    return pl.pallas_call(
        functools.partial(edge_kernel, n_exit, bool(entry_args), token_g, token_out),
        grid=(n_b,), in_specs=in_specs, out_specs=out_specs, out_shape=out_shape,
        compiler_params=pltpu.CompilerParams(dimension_semantics=("arbitrary",), vmem_limit_bytes=VMEM),
        cost_estimate=pl.CostEstimate(flops=1_000_000, bytes_accessed=20_000_000, transcendentals=0),
        name="edge",
    )(*args)


def wmod_kernel(s_ref, d_ref, o_ref):
    o_ref[0] = dot_tn(s_ref[...], d_ref[0].astype(BF16))


def wmod_grad(silu_all, d_mod):
    n_l, n_all, width = d_mod.shape
    dim = silu_all.shape[1]
    piece = dim // 3
    return pl.pallas_call(
        wmod_kernel,
        grid=(n_l, 3),
        in_specs=[pl.BlockSpec((n_all, piece), lambda l, i: (0, i)), pl.BlockSpec((1, n_all, width), lambda l, i: (l, 0, 0))],
        out_specs=pl.BlockSpec((1, piece, width), lambda l, i: (l, i, 0)),
        out_shape=jax.ShapeDtypeStruct((n_l, dim, width), F32),
        compiler_params=pltpu.CompilerParams(dimension_semantics=("arbitrary", "arbitrary")),
        cost_estimate=pl.CostEstimate(flops=2 * n_l * n_all * dim * width, bytes_accessed=4 * n_l * dim * width, transcendentals=0),
        name="wmod_grad",
    )(silu_all, d_mod)


def block_forward(slot, x_in, mod_cols, w_pair, b_cols, qs, ks, cos_t, sin_t, prev, token_in, token_out):
    first, last = slot == 0, slot == 1
    token_in = token_in and first
    n_c, n_j, dim, _ = w_pair.shape
    cols = b_cols.shape[2]
    e = qs.shape[0]
    s_len = cos_t.shape[1]
    n_b = mod_cols.shape[0]
    final = n_j - 1
    full = lambda *shape: pl.BlockSpec(shape, lambda g, b: (0,) * len(shape))
    head6 = lambda n, m: pl.BlockSpec((1, 1, n_c, 1, n, m), lambda g, b: (b, slot, 0, g, 0, 0))
    act = lambda idx: pl.BlockSpec((1, dim, s_len), lambda g, b: (idx(g, b), 0, 0))
    at_start = lambda g, b: jnp.where(g == 0, b, n_b - 1)
    at_end = lambda g, b: jnp.where(g == final, b, 0)
    tok = lambda n, idx: pl.BlockSpec((n, 1, s_len // n, dim), lambda g, b: (0, idx(g, b), 0, 0))
    args = [mod_cols, w_pair, b_cols, qs, ks, cos_t, sin_t, x_in]
    in_specs = [
        pl.BlockSpec((1, dim, 4), lambda g, b: (b, 0, 0)),
        pl.BlockSpec((n_c, 1, dim, dim), lambda g, b: (0, g, 0, 0)),
        pl.BlockSpec((n_c, 1, cols, 1), lambda g, b: (0, g, 0, 0)),
        full(e, 1), full(e, 1), full(e // 2, s_len), full(e // 2, s_len),
        tok(x_in.shape[0], at_start) if token_in else act(at_start if first else at_end),
    ]
    aliases = {}
    if not first:
        y, o, lse, h_t, z = prev
        args += [h_t, z, y, o, lse]
        in_specs += [act(at_start), act(at_start)] + [pl.BlockSpec(memory_space=pl.ANY)] * 3
        aliases = {10: 0, 11: 1, 12: 2}
    out_specs = [head6(cols, s_len), head6(e, s_len), pl.BlockSpec((1, 1, 1, n_c, s_len), lambda g, b: (b, slot, g, 0, 0))]
    out_shape = [
        jax.ShapeDtypeStruct((n_b, 2, n_c, n_j, cols, s_len), F32),
        jax.ShapeDtypeStruct((n_b, 2, n_c, n_j, e, s_len), BF16),
        jax.ShapeDtypeStruct((n_b, 2, n_j, n_c, s_len), F32),
    ]
    shape16, shape32 = jax.ShapeDtypeStruct((n_b, dim, s_len), BF16), jax.ShapeDtypeStruct((n_b, dim, s_len), F32)
    if first:
        out_specs.append(act(at_start))
        out_shape.append(shape16)
        if token_in:
            out_specs.append(act(at_start))
            out_shape.append(shape16)
    if last:
        out_specs += [act(at_end), tok(token_out, at_end) if token_out else act(at_end)]
        out_shape += [shape32, jax.ShapeDtypeStruct((token_out, n_b, s_len // token_out, dim), BF16) if token_out else shape16]
    else:
        out_specs.append(act(at_end))
        out_shape.append(shape32)
    heads = n_c * n_j
    return pl.pallas_call(
        functools.partial(fwd_kernel, e, first, last, token_in, token_out),
        grid=(n_j, n_b), in_specs=in_specs, out_specs=out_specs, out_shape=out_shape,
        input_output_aliases=aliases,
        scratch_shapes=[pltpu.VMEM((n_b, dim, s_len), F32), pltpu.VMEM((n_b, dim, s_len), BF16)],
        compiler_params=pltpu.CompilerParams(dimension_semantics=("arbitrary", "arbitrary"), vmem_limit_bytes=VMEM),
        cost_estimate=pl.CostEstimate(flops=2 * n_b * heads * s_len * dim * dim + 16 * n_b * heads * s_len * s_len * e, bytes_accessed=60_000_000, transcendentals=n_b * heads * s_len * s_len),
        name="block_fwd",
    )(*args)


def block_backward(j_lo, j_n, chip, d_br, h_t, w_own, w_other, qs, ks, cos_t, sin_t, y, o, lse):
    n_b, dim, s_len = d_br.shape
    n_c = w_own.shape[0]
    cols = y.shape[4]
    e = qs.shape[0]
    rows = dim - cols
    n_g = 2 * j_n
    full = lambda *shape: pl.BlockSpec(shape, lambda g, b, c: (0,) * len(shape))
    head6 = lambda n, m: pl.BlockSpec((1, 1, n_c, 1, n, m), lambda g, b, c: (b, g % 2, 0, j_lo + g // 2, 0, 0))
    act = pl.BlockSpec((1, dim, s_len), lambda g, b, c: (b, 0, 0))
    pair = pl.BlockSpec((n_c, 1, dim, dim), lambda g, b, c: (0, j_lo + g // 2, 0, 0))
    grad = lambda n, m: pl.BlockSpec((1, n_c, 1, n, m), lambda g, b, c: (lax.rem(c[0] + g, 2), 0, g // 2, 0, 0))
    heads = 2 * n_c * j_n
    return pl.pallas_call(
        functools.partial(bwd_kernel, e),
        grid_spec=pltpu.PrefetchScalarGridSpec(
            num_scalar_prefetch=1,
            grid=(n_g, n_b),
            in_specs=[
                act, act, pair, pair,
                full(e, 1), full(e, 1), full(e // 2, s_len), full(e // 2, s_len),
                head6(cols, s_len), head6(e, s_len),
                pl.BlockSpec((1, 1, 1, n_c, s_len), lambda g, b, c: (b, g % 2, j_lo + g // 2, 0, 0)),
            ],
            out_specs=[
                grad(dim, dim), grad(cols, 1), full(e, 1), full(e, 1),
                pl.BlockSpec((1, dim, s_len), lambda g, b, c: (jnp.where(g == n_g - 1, b, 0), 0, 0)),
            ],
            scratch_shapes=[
                pltpu.VMEM((n_b, dim, s_len), F32),
                pltpu.VMEM((2 * dim, dim), F32),
                pltpu.VMEM((2 * rows, s_len), BF16),
                pltpu.VMEM((2 * cols, s_len), BF16),
                pltpu.VMEM((2 * rows, s_len), BF16),
            ],
        ),
        out_shape=[
            jax.ShapeDtypeStruct((2, n_c, j_n, dim, dim), BF16),
            jax.ShapeDtypeStruct((2, n_c, j_n, cols, 1), F32),
            jax.ShapeDtypeStruct((e, 1), F32),
            jax.ShapeDtypeStruct((e, 1), F32),
            jax.ShapeDtypeStruct((n_b, dim, s_len), F32),
        ],
        compiler_params=pltpu.CompilerParams(dimension_semantics=("arbitrary", "arbitrary"), vmem_limit_bytes=VMEM),
        cost_estimate=pl.CostEstimate(flops=4 * n_b * heads * s_len * dim * dim + 40 * n_b * heads * s_len * s_len * e, bytes_accessed=60_000_000, transcendentals=n_b * heads * s_len * s_len),
        name="block_bwd",
    )(chip, d_br, h_t, w_own, w_other, qs, ks, cos_t, sin_t, y, o, lse)


def even_first(arr, e):
    lead = arr.shape[:-1]
    return jnp.swapaxes(arr.reshape(*lead, e // 2, 2), -1, -2).reshape(*lead, e)


def interleave(arr, e):
    lead = arr.shape[:-1]
    return jnp.swapaxes(arr.reshape(*lead, 2, e // 2), -1, -2).reshape(*lead, e)


def pair_split(e):
    return np.concatenate([np.arange(0, e, 2), np.arange(1, e, 2)])


def solution(mesh):
    n_tp = mesh.shape["tp"]
    act_spec = P("dp", "tp", None)
    in_specs = (act_spec, P("dp", None), P("tp", None), P("tp", None), P(None, None, None), P(None, None), P(None, None, "tp", None), P(None, "tp", None), P(None, None), P(None, None), P(None, "tp", None, None), P(None, None), act_spec)
    out_specs = (act_spec, act_spec, P("dp", None, None), P("dp", None), P("dp", None, "tp", None), P("dp", "tp", None), P("dp", None), P("dp", None), P("dp", "tp", None, None), P("dp", None))
    same_chip = [[i, i + 1] for i in range(0, n_tp, 2)]
    across = [(i, (i + 2) % n_tp) for i in range(n_tp)]

    def device_step(x_in, cond_vec, rope_cos, rope_sin, w_mod, b_mod, w_in, b_in, q_scale, k_scale, w_out, b_out, d_out):
        n_l, dim, n_j, cols = w_in.shape
        e = q_scale.shape[1]
        n_all, s_own = x_in.shape[:2]
        n_b = n_all // n_tp
        me = lax.axis_index("tp")
        chip = me // 2
        order = pair_split(e)
        perm = np.concatenate([order, e + order, np.arange(2 * e, cols)])
        perm_mat = jnp.asarray(np.eye(cols, dtype=np.float32)[perm], BF16)

        n_rope = e * s_own
        b_perm = jnp.einsum("ec,lhc->lhe", perm_mat, b_in, preferred_element_type=F32)
        small_in = jnp.concatenate([rope_cos.T.reshape(-1), rope_sin.T.reshape(-1), b_perm.reshape(-1)])
        small_all = lax.all_gather(small_in, "tp", axis=0, tiled=False)
        small_all, x_in, w_in, w_out = lax.optimization_barrier((small_all, x_in, w_in, w_out))

        x_tok = lax.all_to_all(x_in.reshape(n_tp, n_b, s_own, dim), "tp", 0, 0)
        w_other, w_local = [], []
        for l in range(n_l):
            w_in_t = jnp.einsum("ec,dhc->hed", perm_mat, w_in[l], preferred_element_type=F32).astype(BF16)
            w_local.append(jnp.concatenate([w_in_t, w_out[l]], axis=1))
        gather_core = lambda w: lax.all_gather(w, "tp", axis=0, tiled=False, axis_index_groups=same_chip)
        w_own = [gather_core(w) for w in w_local]
        tie = x_tok

        tables = jnp.moveaxis(small_all[:, :n_rope].reshape(n_tp, e, s_own), 0, 1).reshape(e, n_tp * s_own)
        cos_t, sin_t = tables[:e // 2], tables[e // 2:]
        b_all = jnp.moveaxis(small_all[:, n_rope:].reshape(2, n_tp // 2, n_l, n_j, cols), 2, 0)[..., None]
        b_own = lax.dynamic_index_in_dim(b_all, chip, 1, keepdims=False)
        b_other = lax.dynamic_index_in_dim(b_all, 1 - chip, 1, keepdims=False)

        silu_all = jax.nn.silu(cond_vec.astype(F32)).astype(BF16)
        silu_own = lax.dynamic_slice_in_dim(silu_all, me * n_b, n_b, 0)
        mod = jnp.einsum("bd,ldm->lbm", silu_own, w_mod, preferred_element_type=F32) + b_mod.astype(F32)[:, None, :]
        bias = jnp.broadcast_to(b_out.astype(F32)[:, None, None, :], (n_l, n_b, 1, dim))
        mod_cols = jnp.swapaxes(jnp.concatenate([mod.reshape(n_l, n_b, 3, dim), bias], axis=2), 2, 3)
        qs = even_first(q_scale.astype(F32), e)[..., None]
        ks = even_first(k_scale.astype(F32), e)[..., None]

        saved = []
        x_cur = x_tok
        for l in range(n_l):
            consts = (qs[l], ks[l], cos_t, sin_t)
            mine, tie = lax.optimization_barrier((w_local[l], tie))
            if l == 0:
                x_cur = tie
            got = lax.ppermute(mine, "tp", across)
            half = block_forward(0, x_cur, mod_cols[l], w_own[l], b_own[l], *consts, None, l == 0, 0)
            y, o, lse, h_t = half[:4]
            x_t = half[4] if l == 0 else x_cur
            got, h_t = lax.optimization_barrier((got, h_t))
            tie = got
            w_other.append(gather_core(got))
            y, o, lse, branch, x_new = block_forward(1, x_t, mod_cols[l], w_other[l], b_other[l], *consts, (y, o, lse, h_t, half[-1]), False, n_tp if l == n_l - 1 else 0)
            saved.append((x_t, y, o, lse, h_t, branch))
            x_cur = x_new
        d_late, tie = lax.optimization_barrier((d_out, tie))
        g_tok = lax.all_to_all(d_late.reshape(n_tp, n_b, s_own, dim), "tp", 0, 0)
        x_out = lax.all_to_all(x_cur, "tp", 0, 0)

        grads = [None] * n_l
        d_mods = [None] * n_l
        small = [None] * n_l
        chip_arr = chip.astype(jnp.int32).reshape(1)
        top = n_l - 1
        g_t, d_br, d_ent = edge(g_tok, None, (mod_cols[top], saved[top][5]), True, 0)
        for l in reversed(range(n_l)):
            x_t, y, o, lse, h_t, branch = saved[l]
            splits = [(j, 1) for j in range(n_j)]
            if l == 0:
                d_br, x_out = lax.optimization_barrier((d_br, x_out))
            d_hs, d_qs, d_ks, gb, gw = [], 0.0, 0.0, [], []
            for j, width in splits:
                gw_j, gb_j, dq_j, dk_j, dh_j = block_backward(j, width, chip_arr, d_br, h_t, w_own[l], w_other[l], qs[l], ks[l], cos_t, sin_t, y, o, lse)
                d_hs.append(dh_j)
                d_qs, d_ks = d_qs + dq_j, d_ks + dk_j
                gb.append(gb_j)
                gw.append(lax.psum_scatter(gw_j.reshape(n_tp, width, dim, dim), "tp", scatter_dimension=0, tiled=False))
            entry = (mod_cols[l - 1], saved[l - 1][5]) if l > 0 else None
            edge_out = edge(g_t, (x_t, mod_cols[l], d_hs), entry, False, 0 if l > 0 else n_tp)
            d_out_cols = d_ent
            g_t, d_norm = edge_out[:2]
            if l > 0:
                d_br, d_ent = edge_out[2:]
            grads[l] = gw[0] if len(gw) == 1 else jnp.concatenate(gw, axis=0)
            d_mods[l] = jnp.swapaxes(jnp.concatenate([d_norm, d_out_cols[:, :, :1]], axis=2), 1, 2).reshape(n_b, 3 * dim)
            gb = gb[0] if len(gb) == 1 else jnp.concatenate(gb, axis=2)
            small[l] = jnp.concatenate([d_mods[l].reshape(-1), jnp.sum(d_out_cols[:, :, 1], axis=0), d_qs[:, 0], d_ks[:, 0], gb.reshape(-1)])

        grad_x = lax.all_to_all(g_t, "tp", 0, 0).reshape(n_all, s_own, dim)
        gathered = lax.all_gather(jnp.stack(small), "tp", axis=0, tiled=False)
        n_mod = n_b * 3 * dim
        d_mod = jnp.moveaxis(gathered[:, :, :n_mod].reshape(n_tp, n_l, n_b, 3 * dim), 1, 0).reshape(n_l, n_all, 3 * dim)
        sums = jnp.sum(gathered[:, :, n_mod:], axis=0)
        g_wmod = wmod_grad(silu_all, d_mod)
        g_bmod = jnp.sum(d_mod, axis=1)
        g_bout = sums[:, :dim]
        g_qs = interleave(sums[:, dim:dim + e], e)
        g_ks = interleave(sums[:, dim + e:dim + 2 * e], e)
        g_b = lax.dynamic_index_in_dim(sums[:, dim + 2 * e:].reshape(n_l, n_tp, n_j, cols), me, 1, keepdims=False)
        g_bin = jnp.concatenate([interleave(g_b[..., :e], e), interleave(g_b[..., e:2 * e], e), g_b[..., 2 * e:]], axis=-1)
        gw_all = jnp.stack(grads)
        g_win = jnp.einsum("ec,lhed->ldhc", perm_mat, gw_all[:, :, :cols], preferred_element_type=F32).astype(BF16)
        g_wout = gw_all[:, :, cols:]
        return (x_out.reshape(n_all, s_own, dim), grad_x, g_wmod, g_bmod, g_win, g_bin, g_qs, g_ks, g_wout, g_bout)

    return jax.shard_map(device_step, mesh=mesh, in_specs=in_specs, out_specs=out_specs, check_vma=False)
```

time: 1010 us -> 903 us (0.89)
  local copies, waits for them, and re-layouts: 121 us -> 44.6 us
  waiting for transfers between devices: 46.2 us -> 104 us
  blocking collectives: 107 us -> 55.7 us
  other arithmetic: 62.8 us -> 13.9 us
    all_to_all x0 -> x4, waiting for transfers between devices: none -> 68.8 us  [the longest x1 41.8 us: device_step(): x_out = lax.all_to_all(x_cur, 'tp', 0, 0)]
    all_gather x3 -> x2, blocking collectives: 107 us -> 55.7 us  [the longest x1 47.9 us: device_step(): gathered = lax.all_gather(jnp.stack(small), 'tp', axis=0, tiled=False)]
    reduce_sum x10 -> x4, other arithmetic: 38 us -> 1.53 us  [the longest x2 0.79 us: device_step(): jnp.sum(d_out_cols[:, :, 1], axis=0)]
    ppermute x12 -> x2, waiting for transfers between devices: 45.3 us -> 18.6 us  [device_step(): got = lax.ppermute(mine, 'tp', across)]
    unnamed x123 -> x76, local copies, waits for them, and re-layouts: 37 us -> 12.8 us
    dynamic_update_slice x16 -> x0, local copies, waits for them, and re-layouts: 19.9 us -> none  [the longest x6 11.4 us: swap_to_samples(): out = lax.dynamic_update_slice_in_dim(out, got, peer * s, 2)]
    all_to_all x0 -> x4, starting transfers between devices: none -> 16.9 us  [the longest x1 4.67 us: device_step(): g_tok = lax.all_to_all(d_late.reshape(n_tp, n_b, s_own, dim), 'tp', 0, 0)]
    all_gather x2 -> x4, waiting for transfers between devices: 0.02 us -> 16.5 us  [device_step(): lax.all_gather(w, 'tp', axis=0, tiled=False, axis_index_groups=same_chip)]
  transfers between devices with their start and end apart: 20 -> 16, of which waited for: 3 -> 5; matrix products, arithmetic and copies ran while one was open for 17% -> 5% of each run, Pallas kernels for 43% -> 62%
where the time goes in v2:
time: 903 us; the launch traced here: 899 us
  Pallas kernels  630 us (70%)
  waiting for transfers between devices  104 us (12%)
  blocking collectives  55.7 us (6%)
  local copies, waits for them, and re-layouts  44.6 us (5%)
  starting transfers between devices  19.3 us (2%)
  matrix products  16.4 us (2%)
  between operations  15.2 us (2%)
  other arithmetic  13.9 us (2%)
    pallas_call x6, Pallas kernels, block_backward(): pl.pallas_call(functools.partial(bwd_kernel, e), grid_spec=pltpu.Prefetch...  378 us
    pallas_call x4, Pallas kernels, block_forward(): pl.pallas_call(functools.partial(fwd_kernel, e, first, last, token_in, to...  205 us
    all_gather x1, blocking collectives, device_step(): gathered = lax.all_gather(jnp.stack(small), 'tp', axis=0, tiled=False)  47.9 us
    all_to_all x1, waiting for transfers between devices, device_step(): x_out = lax.all_to_all(x_cur, 'tp', 0, 0)  41.8 us
    pallas_call x3, Pallas kernels, edge(): pl.pallas_call(functools.partial(edge_kernel, n_exit, bool(entry_args), t...  39.1 us
    all_to_all x1, waiting for transfers between devices, device_step(): x_tok = lax.all_to_all(x_in.reshape(n_tp, n_b, s_own, dim), 'tp', 0, 0)  27 us
    ppermute x2, waiting for transfers between devices, device_step(): got = lax.ppermute(mine, 'tp', across)  18.6 us
  transfers between devices with their start and end apart: 16, of which 5 were waited for; matrix products, arithmetic and copies ran while one was open for 5% of the time, Pallas kernels for 62%

profile of v2, /device:TPU:0, one launch (start us, length us, event | category | flops | bytes accessed | tf_op | source)
XLA Modules:
  0.0 899.2 jit_solution(2370403308768662709)
XLA Ops:
  10.9 7.8 all-gather.6
  18.8 3.0 convert_bitcast_fusion.1
  21.8 1.3 slice_bitcast_fusion
  23.1 2.0 pad_maximum_fusion.1
  25.1 3.7 all-to-all-start
  30.6 5.2 fusion.3
  36.8 1.4 fusion.29
  38.8 27.0 %all-to-all-done.refs_7_ = bf16[4,2,256,768]{3,2,1,0:T(8,128)(2,1)S(1)} async-done(((bf16[4,2,256,768]{3,2,1,0:T(8,128)(2,1)}), bf16[4,2,256,768]{3,2,1,0:T(8,128)(2,1)S(1)}, u32[]{:S(2)}, u32[]{:S(2)}) %all-to-all-start) | async-done | bytes 3145760 | tf_op jit(solution)/shard_map/all_to_all | solution.py:509
  70.7 1.5 copy.218.refs_2_
  74.1 51.3 %block_fwd.4 = (f32[2,2,2,3,448,1024]{5,4,3,2,1,0:T(8,128)}, bf16[2,2,2,3,64,1024]{5,4,3,2,1,0:T(8,128)(2,1)}, f32[2,2,3,2,1024]{4,3,2,1,0:T(2,128)}, bf16[2,768...) custom-call(f32[2,768,4]{2,1,0:T(8,128)} %get-tuple-element.161.refs_0_.refs_6_.refs_2_, ...), custom_call_target="tpu_custom_call" | custom-call | flops 27380416512 | bytes 60000000 | tf_op jit(solution)/shard_map/block_fwd/pallas_call | solution.py:410
  125.4 18.6 %collective-permute-done = bf16[3,768,768]{2,1,0:T(8,128)(2,1)} collective-permute-done((bf16[3,768,768]{2,1,0:T(8,128)(2,1)}, bf16[3,768,768]{2,1,0:T(8,128)(2,1)}, u32[]{:S(2)}, u32[]{:S(2)}) %collective-permute-start) | collective-permute-done | bytes 3538976 | tf_op jit(solution)/shard_map/ppermute | solution.py:539
  144.1 2.9 convert_bitcast_fusion.2
  147.1 2.0 pad_maximum_fusion
  151.4 1.5 copy.225.refs_2_
  153.0 1.6 copy.228.refs_2_
  155.3 5.3 all-gather.17.cloned.1.call-done
  160.6 51.1 %block_fwd.5 = (f32[2,2,2,3,448,1024]{5,4,3,2,1,0:T(8,128)}, bf16[2,2,2,3,64,1024]{5,4,3,2,1,0:T(8,128)(2,1)}, f32[2,2,3,2,1024]{4,3,2,1,0:T(2,128)}, f32[2,768,1024]{2,1,0:T(8,128)}, bf16[2,768,1024]{2,1,0:T(8,128)(2,1)}) custom-call(f32[2,768,4]{2,1,0:T(8,128)} %get-tuple-element.161.refs_0_.refs_6_.r, ...), custom_call_target="tpu_custom_call", output_to_operand_aliasing={{0}: (10, {}), {1}: (11, {}), {2}: (12, {})} | custom-call | flops 27380416512 | bytes 60000000 | tf_op jit(solution)/shard_map/block_fwd/pallas_call | solution.py:410
  211.7 50.9 %block_fwd.6 = (f32[2,2,2,3,448,1024]{5,4,3,2,1,0:T(8,128)}, bf16[2,2,2,3,64,1024]{5,4,3,2,1,0:T(8,128)(2,1)}, f32[2,2,3,2,1024]{4,3,2,1,0:T(2,128)}, bf16[2,768,1024]{2,1,0:T(8,128)(2,1)}, f32[2,768,1024]{2,1,0:T(8,128)}) custom-call(f32[2,768,4]{2,1,0:T(8,128)} %get-tuple-element.160.refs_0_.refs_1_.refs_2_, bf16[2,3,768,768]{3,2,1,0:T(8,128)(2,1)} %bitcast.200, ...), custom_call_target="tpu_custom_call" | custom-call | flops 27380416512 | bytes 60000000 | tf_op jit(solution)/shard_map/block_fwd/pallas_call | solution.py:410
  262.7 1.5 copy.232.refs_2_
  264.2 4.7 all-to-all-start.1
  269.0 11.1 %all-gather.19.cloned.1.call-done = bf16[6,768,768]{2,1,0:T(8,128)(2,1)} async-done(((bf16[3,768,768]{2,1,0:T(8,128)(2,1)}), bf16[6,768,768]{2,1,0:T(8,128)(2,1)}) %all-gather.19.cloned.1.call-update) | async-done | bytes 7077904 | tf_op jit(solution)/shard_map/all_gather | solution.py:514
  280.1 51.9 %block_fwd.7 = (f32[2,2,2,3,448,1024]{5,4,3,2,1,0:T(8,128)}, bf16[2,2,2,3,64,1024]{5,4,3,2,1,0:T(8,128)(2,1)}, f32[2,2,3,2,1024]{4,3,2,1,0:T(2,128)}, f32[2,768,1024]{2,1,0:T(8,128)}, bf16[4,2,256,768]{3,2,1,0:T(8,128)(2,1)}) custom-call(f32[2,768,4]{2,1,0:T(8,128)} %get-tuple-element.160.refs_0_.refs_1, ...), custom_call_target="tpu_custom_call", output_to_operand_aliasing={{0}: (10, {}), {1}: (11, {}), {2}: (12, {})} | custom-call | flops 27380416512 | bytes 60000000 | tf_op jit(solution)/shard_map/block_fwd/pallas_call | solution.py:410
  332.0 6.4 edge.3
  338.4 62.7 %block_bwd.8 = (bf16[2,2,1,768,768]{4,3,2,1,0:T(8,128)(2,1)}, f32[2,2,1,448,1]{4,3,2,1,0:T(8,128)}, f32[64,1]{1,0:T(8,128)}, f32[64,1]{1,0:T(8,128)}, f32[2,768,1024]{2,1,0:T(8,128)}) custom-call(s32[1]{0:T(128)} %bitcast.32.chip_ref, bf16[2,768,1024]{2,1,0:T(8,128)(2,1)} %get-tuple-element.110.dbr_ref, ...), custom_call_target="tpu_custom_call" | custom-call | flops 40802189312 | bytes 60000000 | tf_op jit(solution)/shard_map/block_bwd/pallas_call | solution.py:434
  401.2 63.0 %block_bwd.7 = (bf16[2,2,1,768,768]{4,3,2,1,0:T(8,128)(2,1)}, f32[2,2,1,448,1]{4,3,2,1,0:T(8,128)}, f32[64,1]{1,0:T(8,128)}, f32[64,1]{1,0:T(8,128)}, f32[2,768,1024]{2,1,0:T(8,128)}) custom-call(s32[1]{0:T(128)} %bitcast.32.chip_ref, bf16[2,768,1024]{2,1,0:T(8,128)(2,1)} %get-tuple-element.110.dbr_ref, ...), custom_call_target="tpu_custom_call" | custom-call | flops 40802189312 | bytes 60000000 | tf_op jit(solution)/shard_map/block_bwd/pallas_call | solution.py:434
  464.3 62.5 %block_bwd.6 = (bf16[2,2,1,768,768]{4,3,2,1,0:T(8,128)(2,1)}, f32[2,2,1,448,1]{4,3,2,1,0:T(8,128)}, f32[64,1]{1,0:T(8,128)}, f32[64,1]{1,0:T(8,128)}, f32[2,768,1024]{2,1,0:T(8,128)}) custom-call(s32[1]{0:T(128)} %bitcast.32.chip_ref, bf16[2,768,1024]{2,1,0:T(8,128)(2,1)} %get-tuple-element.110.dbr_ref, ...), custom_call_target="tpu_custom_call" | custom-call | flops 40802189312 | bytes 60000000 | tf_op jit(solution)/shard_map/block_bwd/pallas_call | solution.py:434
  526.9 4.7 all-to-all-start.2
  531.6 18.6 %edge.4 = (bf16[2,768,1024]{2,1,0:T(8,128)(2,1)}, f32[2,768,2]{2,1,0:T(8,128)}, bf16[2,768,1024]{2,1,0:T(8,128)(2,1)}, f32[2,768,2]{2,1,0:T(8,128)}) custom-call(bf16[2,768,1024]{2,1,0:T(8,128)(2,1)} %get-tuple-element.109.refs_0_, bf16[2,768,1024]{2,1,0:T(8,128)(2,1)} %get-tuple-element.99.refs_7_.refs_1_, ...), custom_call_target="tpu_custom_call" | custom-call | flops 1000000 | bytes 20000000 | tf_op jit(solution)/shard_map/edge/pallas_call | solution.py:332
  550.2 41.8 %all-to-all-done.2 = bf16[4,2,256,768]{3,2,1,0:T(8,128)(2,1)} async-done(((bf16[4,2,256,768]{3,2,1,0:T(8,128)(2,1)}), bf16[4,2,256,768]{3,2,1,0:T(8,128)(2,1)}, u32[]{:S(2)}, u32[]{:S(2)}) %all-to-all-start.2) | async-done | bytes 3145760 | tf_op jit(solution)/shard_map/all_to_all | solution.py:551
  592.1 62.6 %block_bwd.11 = (bf16[2,2,1,768,768]{4,3,2,1,0:T(8,128)(2,1)}, f32[2,2,1,448,1]{4,3,2,1,0:T(8,128)}, f32[64,1]{1,0:T(8,128)}, f32[64,1]{1,0:T(8,128)}, f32[2,768,1024]{2,1,0:T(8,128)}) custom-call(s32[1]{0:T(128)} %bitcast.32.chip_ref, bf16[2,768,1024]{2,1,0:T(8,128)(2,1)} %get-tuple-element.122.dbr_ref, ...), custom_call_target="tpu_custom_call" | custom-call | flops 40802189312 | bytes 60000000 | tf_op jit(solution)/shard_map/block_bwd/pallas_call | solution.py:434
  654.8 63.7 %block_bwd.10 = (bf16[2,2,1,768,768]{4,3,2,1,0:T(8,128)(2,1)}, f32[2,2,1,448,1]{4,3,2,1,0:T(8,128)}, f32[64,1]{1,0:T(8,128)}, f32[64,1]{1,0:T(8,128)}, f32[2,768,1024]{2,1,0:T(8,128)}) custom-call(s32[1]{0:T(128)} %bitcast.32.chip_ref, bf16[2,768,1024]{2,1,0:T(8,128)(2,1)} %get-tuple-element.122.dbr_ref, ...), custom_call_target="tpu_custom_call" | custom-call | flops 40802189312 | bytes 60000000 | tf_op jit(solution)/shard_map/block_bwd/pallas_call | solution.py:434
  718.6 63.4 %block_bwd.9 = (bf16[2,2,1,768,768]{4,3,2,1,0:T(8,128)(2,1)}, f32[2,2,1,448,1]{4,3,2,1,0:T(8,128)}, f32[64,1]{1,0:T(8,128)}, f32[64,1]{1,0:T(8,128)}, f32[2,768,1024]{2,1,0:T(8,128)}) custom-call(s32[1]{0:T(128)} %bitcast.32.chip_ref, bf16[2,768,1024]{2,1,0:T(8,128)(2,1)} %get-tuple-element.122.dbr_ref, ...), custom_call_target="tpu_custom_call" | custom-call | flops 40802189312 | bytes 60000000 | tf_op jit(solution)/shard_map/block_bwd/pallas_call | solution.py:434
  784.2 1.7 copy.258
  785.8 1.6 copy.257
  787.5 1.6 copy.254
  791.7 1.6 copy.250
  793.4 14.1 %edge.5 = (bf16[4,2,256,768]{3,2,1,0:T(8,128)(2,1)}, f32[2,768,2]{2,1,0:T(8,128)}) custom-call(bf16[2,768,1024]{2,1,0:T(8,128)(2,1)} %get-tuple-element.121.refs_0_, bf16[2,768,1024]{2,1,0:T(8,128)(2,1)} %get-tuple-element.93.refs_7_.refs_1_, f32[2,768,4]{2,1,0:T(8,128)} %get-tuple-element.161.refs_0_.refs_6_.refs_2_, ...), custom_call_target="tpu_custom_call" | custom-call | flops 1000000 | bytes 20000000 | tf_op jit(solution)/shard_map/edge/pallas_call | solution.py:332
  807.5 3.8 all-to-all-start.3
  811.4 1.4 copy.247
  813.3 47.9 %all-gather.7 = f32[4,2,10880]{2,1,0:T(2,128)S(1)} all-gather(f32[1,2,10880]{2,1,0:T(2,128)S(1)} %maximum_bitcast_fusion.2), channel_id=7, replica_groups=mesh['dp'=4,'tp'=4] {'tp'}, dimensions={0}, use_global_device_ids=true | all-gather | bytes 435200 | tf_op jit(solution)/shard_map/all_gather | solution.py:583
  865.6 7.7 wmod_grad.1
  874.6 1.6 copy-done.2
  876.2 2.2 maximum_bitcast_fusion.1
  878.5 2.2 maximum_bitcast_fusion
  880.7 1.9 pad_maximum_fusion.2
  882.5 4.0 convert_bitcast_fusion
  886.6 3.9 copy.307
  890.5 1.7 copy.308
  (188 shorter events, 28.3 us)
Async XLA Ops:
  7.2 66.9 %all-gather.13.cloned.1.call-start = ((), (), s32[]{:S(2)}) async-start(), calls=%async_computation.16 | async-start | bytes 10616832 | tf_op jit(solution)/shard_map/all_gather | solution.py:514
  10.8 11.0 %copy-start.8 = (bf16[2,3,320,768]{3,2,1,0:T(8,128)(2,1)S(1)}, bf16[2,3,320,768]{3,2,1,0:T(8,128)(2,1)}, u32[]{:S(2)}) copy-start(bf16[2,3,320,768]{3,2,1,0:T(8,128)(2,1)} %param.24) | copy-start | bytes 8847364
  25.1 4.8 copy-start.29
  25.1 4.8 copy-start.28
  25.1 40.6 %all-to-all-start = ((bf16[4,2,256,768]{3,2,1,0:T(8,128)(2,1)}), bf16[4,2,256,768]{3,2,1,0:T(8,128)(2,1)S(1)}, u32[]{:S(2)}, u32[]{:S(2)}) async-start(bf16[4,2,256,768]{3,2,1,0:T(8,128)(2,1)} %bitcast.10), calls=%async_computation | async-start | bytes 6291456 | tf_op jit(solution)/shard_map/all_to_all | solution.py:509
  28.9 131.7 %all-gather.17.cloned.1.call-start = ((), (), s32[]{:S(2)}) async-start(), calls=%async_computation.18 | async-start | bytes 10616832 | tf_op jit(solution)/shard_map/all_gather | solution.py:514
  30.6 5.3 copy-start.31
  30.6 6.0 copy-start.32
  30.6 38.6 %copy-start.9 = (f32[4,16384]{1,0:T(4,128)S(1)}, f32[4,16384]{1,0:T(4,128)}, u32[]{:S(2)}) copy-start(f32[4,16384]{1,0:T(4,128)} %slice.140) | copy-start | bytes 786436
  30.6 41.7 %copy-start.30 = (bf16[2,768]{1,0:T(2,128)(2,1)S(1)}, bf16[2,768]{1,0:T(2,128)(2,1)}, u32[]{:S(2)}) copy-start(bf16[2,768]{1,0:T(2,128)(2,1)} %param.25) | copy-start | bytes 9220
  65.7 6.5 copy-start.5
  65.7 78.3 %collective-permute-start = (bf16[3,768,768]{2,1,0:T(8,128)(2,1)}, bf16[3,768,768]{2,1,0:T(8,128)(2,1)}, u32[]{:S(2)}, u32[]{:S(2)}) collective-permute-start(bf16[3,768,768]{2,1,0:T(8,128)(2,1)} %pad_maximum_fusion.1), channel_id=1, source_target_pairs={{0,2},{1,3},{2,0},{3,1},{4,6},{5,7},{6,4},{7,5},{8,10},{9,11},{10,... | collective-permute-start | bytes 10616840 | tf_op jit(solution)/shard_map/ppermute | solution.py:539
  125.4 18.7 %copy-start.13 = (bf16[448,448,1]{1,0,2:T(8,128)(2,1)S(1)}, bf16[448,448,1]{1,0,2:T(8,128)(2,1)}, u32[]{:S(2)}) copy-start(bf16[448,448,1]{1,0,2:T(8,128)(2,1)} %constant.47) | copy-start | bytes 1204228
  144.0 3.0 copy-start.4
  144.1 67.7 %all-gather.15.cloned.1.call-start = ((), (), s32[]{:S(2)}) async-start(), calls=%async_computation.17 | async-start | bytes 10616832 | tf_op jit(solution)/shard_map/all_gather | solution.py:514
  149.1 0.7 copy-start.15
  149.1 1.5 copy-start.14
  149.1 131.0 %all-gather.19.cloned.1.call-start = ((), (), s32[]{:S(2)}) async-start(), calls=%async_computation.19 | async-start | bytes 10616832 | tf_op jit(solution)/shard_map/all_gather | solution.py:514
  154.5 108.2 %collective-permute-start.1 = (bf16[3,768,768]{2,1,0:T(8,128)(2,1)}, bf16[3,768,768]{2,1,0:T(8,128)(2,1)}, u32[]{:S(2)}, u32[]{:S(2)}) collective-permute-start(bf16[3,768,768]{2,1,0:T(8,128)(2,1)} %pad_maximum_fusion), channel_id=1, source_target_pairs={{0,2},{1,3},{2,0},{3,1},{4,6},{5,7},{6,4},{7,5},{8,10},{9,11},{10,... | collective-permute-start | bytes 10616840 | tf_op jit(solution)/shard_map/ppermute | solution.py:539
  264.2 67.8 %all-to-all-start.1 = ((bf16[4,2,256,768]{3,2,1,0:T(8,128)(2,1)}), bf16[4,2,256,768]{3,2,1,0:T(8,128)(2,1)}, u32[]{:S(2)}, u32[]{:S(2)}) async-start(bf16[4,2,256,768]{3,2,1,0:T(8,128)(2,1)} %bitcast.29), calls=%async_computation.1 | async-start | bytes 6291456 | tf_op jit(solution)/shard_map/all_to_all | solution.py:550
  268.9 605.7 %reduce-scatter.17.cloned.1.call-start = ((), (), s32[]{:S(2)}) async-start(), calls=%async_computation.15 | async-start | bytes 5898240 | tf_op jit(solution)/shard_map/reduce_scatter | solution.py:570
  401.2 473.4 %reduce-scatter.15.cloned.1.call-start = ((), (), s32[]{:S(2)}) async-start(), calls=%async_computation.14 | async-start | bytes 5898240 | tf_op jit(solution)/shard_map/reduce_scatter | solution.py:570
  464.3 410.4 %reduce-scatter.13.cloned.1.call-start = ((), (), s32[]{:S(2)}) async-start(), calls=%async_computation.13 | async-start | bytes 5898240 | tf_op jit(solution)/shard_map/reduce_scatter | solution.py:570
  526.9 65.2 %all-to-all-start.2 = ((bf16[4,2,256,768]{3,2,1,0:T(8,128)(2,1)}), bf16[4,2,256,768]{3,2,1,0:T(8,128)(2,1)}, u32[]{:S(2)}, u32[]{:S(2)}) async-start(bf16[4,2,256,768]{3,2,1,0:T(8,128)(2,1)} %get-tuple-element.119), calls=%async_computation.2 | async-start | bytes 6291456 | tf_op jit(solution)/shard_map/all_to_all | solution.py:551
  531.5 346.9 %reduce-scatter.11.cloned.1.call-start = ((), (), s32[]{:S(2)}) async-start(), calls=%async_computation.12 | async-start | bytes 5898240 | tf_op jit(solution)/shard_map/reduce_scatter | solution.py:570
  654.7 223.7 %reduce-scatter.9.cloned.1.call-start = ((), (), s32[]{:S(2)}) async-start(), calls=%async_computation.11 | async-start | bytes 5898240 | tf_op jit(solution)/shard_map/reduce_scatter | solution.py:570
  718.5 159.9 %reduce-scatter.7.cloned.1.call-start = ((), (), s32[]{:S(2)}) async-start(), calls=%async_computation.10 | async-start | bytes 5898240 | tf_op jit(solution)/shard_map/reduce_scatter | solution.py:570
  782.0 1.1 copy-start.6
  782.0 1.8 copy-start.10
  782.0 7.2 copy-start.18
  782.0 7.2 copy-start.21
  783.1 7.0 copy-start.17
  783.1 7.0 copy-start.19
  783.1 7.2 copy-start.7
  783.5 6.6 copy-start.23
  784.1 6.9 copy-start.11
  784.1 7.2 copy-start.12
  807.5 5.4 copy-start.22
  807.5 5.4 copy-start.25
  807.5 5.4 copy-start.27
  807.5 5.5 copy-start.20
  807.5 5.5 copy-start.24
  807.5 5.5 copy-start.26
  807.5 67.0 %all-to-all-start.3 = ((bf16[4,2,256,768]{3,2,1,0:T(8,128)(2,1)}), bf16[4,2,256,768]{3,2,1,0:T(8,128)(2,1)S(1)}, u32[]{:S(2)}, u32[]{:S(2)}) async-start(bf16[4,2,256,768]{3,2,1,0:T(8,128)(2,1)} %get-tuple-element.129), calls=%async_computation.3 | async-start | bytes 6291456 | tf_op jit(solution)/shard_map/all_to_all | solution.py:582
  874.6 1.7 copy-start.2
  880.7 1.9 copy-start.33
  886.6 3.9 copy-start.3
  886.6 5.6 copy-start.1
  (2 other events, 1.3 us)
Sparse Core Ops, SparseCore 0:
  25.2 17.0 all-gather.12
  144.2 16.3 all-gather.16
  162.7 17.2 all-gather.14
  262.8 17.2 all-gather.18
  401.3 45.3 reduce-scatter.16
  464.4 45.2 reduce-scatter.14
  527.0 68.2 reduce-scatter.12
  654.8 44.3 reduce-scatter.10
  718.7 44.3 reduce-scatter.8
  782.2 54.5 reduce-scatter.6

commit v3 on v0

v3 whole, which is shorter than its diff:
```python
import functools
import jax
import jax.numpy as jnp
import numpy as np
from jax import lax
from jax.experimental import pallas as pl
from jax.experimental.pallas import tpu as pltpu
from jax.sharding import PartitionSpec as P

NORM_EPS = 1e-6
LOG2E = 1.4426950408889634
GELU_C = 0.7978845608028654
GELU_A = 0.044715
F32 = jnp.float32
BF16 = jnp.bfloat16
CHUNK = 256
VMEM = 63 * 1024 * 1024
SPLIT = 4
SQ = pl.squeezed
FULL = ...
SMALL_FIRST = False


def dot_nn(a, b):
    return lax.dot_general(a, b, (((1,), (0,)), ((), ())), preferred_element_type=F32)


def dot_nt(a, b):
    return lax.dot_general(a, b, (((1,), (1,)), ((), ())), preferred_element_type=F32)


def dot_tn(a, b):
    return lax.dot_general(a, b, (((0,), (0,)), ((), ())), preferred_element_type=F32)


def norm_rope(raw, scale_col, cos_t, sin_t):
    half = raw.shape[0] // 2
    inv = lax.rsqrt(jnp.mean(raw * raw, axis=0, keepdims=True) + NORM_EPS)
    hat = raw * inv
    scaled = hat * scale_col
    a, b = scaled[:half], scaled[half:]
    rot = jnp.concatenate([a * cos_t - b * sin_t, a * sin_t + b * cos_t], axis=0)
    return hat, inv, rot.astype(BF16)


def norm_rope_bwd(d_rot, hat, inv, scale_col, cos_t, sin_t):
    half = d_rot.shape[0] // 2
    da, db = d_rot[:half], d_rot[half:]
    d_scaled = jnp.concatenate([da * cos_t + db * sin_t, db * cos_t - da * sin_t], axis=0)
    d_scale = jnp.sum(d_scaled * hat, axis=1, keepdims=True)
    d_hat = d_scaled * scale_col
    d_raw = inv * (d_hat - hat * jnp.mean(d_hat * hat, axis=0, keepdims=True))
    return d_raw, d_scale


def softmax_head(q_rot, k_rot, v_t, o_ref, lse_ref, i, mul, between):
    n_c = q_rot.shape[1] // CHUNK
    spans = [slice(c * CHUNK, (c + 1) * CHUNK) for c in range(n_c)]
    nxt = dot_tn(k_rot, q_rot[:, spans[0]])
    outs = []
    for c in range(n_c):
        s = nxt
        if c + 1 < n_c:
            nxt = dot_tn(k_rot, q_rot[:, spans[c + 1]])
        between(c, outs)
        top = jnp.max(s, axis=0, keepdims=True) * mul
        p = jnp.exp2(s * mul - top)
        tot = jnp.sum(p, axis=0, keepdims=True)
        out = (dot_nn(v_t, p.astype(BF16)) * (1.0 / tot)).astype(BF16)
        o_ref[i, :, spans[c]] = out
        outs.append(out)
        lse_ref[i:i + 1, spans[c]] = top + jnp.log2(tot)
    return jnp.concatenate(outs, axis=1)


def as_col(rows):
    return rows.T


def as_row(col):
    n = col.shape[0]
    return jnp.broadcast_to(col, (n, 128)).T[:1]


def from_tokens(ref):
    return jnp.concatenate([ref[t].astype(F32).T for t in range(ref.shape[0])], axis=1)


def gelu_parts(u):
    t = jnp.tanh(GELU_C * (u + GELU_A * u * u * u))
    return t, 0.5 * (1.0 + t)


def fwd_kernel(e, first, last, token_in, token_out, *refs):
    refs = list(refs)
    take = refs.pop
    mod_ref, wa_ref, wb_ref, bin_ref, qk_ref, cos_ref, sin_ref, x_ref = [take(0) for _ in range(8)]
    if not first:
        h_in, z_in = take(0), take(0)
        del refs[:3]
    y_ref, o_ref, lse_ref = take(0), take(0), take(0)
    if first:
        h_ref = take(0)
        if token_in:
            xt_ref = take(0)
    if last:
        br_ref = take(0)
        xo_ref = take(0)
    else:
        z_out = take(0)
    z_sc, h_sc, wo_sc = refs
    g, b = pl.program_id(0), pl.program_id(1)
    final = pl.num_programs(0) - 1
    cols = bin_ref.shape[-1]

    @pl.when(g == 0)
    def _():
        if first:
            mod = as_col(mod_ref[FULL])
            if token_in:
                x = from_tokens(x_ref)
                xt_ref[FULL] = x.astype(BF16)
            else:
                x = x_ref[FULL].astype(F32)
            cent = x - jnp.mean(x, axis=0, keepdims=True)
            normed = cent * lax.rsqrt(jnp.mean(cent * cent, axis=0, keepdims=True) + NORM_EPS)
            h = (normed * (1.0 + mod[:, 1:2]) + mod[:, :1]).astype(BF16)
            h_sc[b] = h
            h_ref[FULL] = h
            z_sc[b] = jnp.zeros_like(x)
        else:
            h_sc[b] = h_in[FULL]
            z_sc[b] = z_in[FULL]

    h_t = h_sc[b]
    cos_t, sin_t = cos_ref[FULL], sin_ref[FULL]
    q_col, k_col = [as_col(qk_ref[i])[:, :1] for i in range(2)]
    mul = (e ** -0.5) * LOG2E
    n_c = h_t.shape[1] // CHUNK
    spans = [slice(c * CHUNK, (c + 1) * CHUNK) for c in range(n_c)]
    bias = [as_col(bin_ref[i])[:, :1] for i in range(2)]
    wo_sc[FULL] = jnp.concatenate([wa_ref[cols:], wb_ref[cols:]], axis=0).T
    y_a = dot_nn(wa_ref[:cols], h_t) + bias[0]
    y_ref[0] = y_a

    def next_head(c, outs):
        y_ref[1, :, spans[c]] = dot_nn(wb_ref[:cols], h_t[:, spans[c]]) + bias[1]

    def attend(i, y, between):
        q_rot = norm_rope(y[:e], q_col, cos_t, sin_t)[-1]
        k_rot = norm_rope(y[e:2 * e], k_col, cos_t, sin_t)[-1]
        return softmax_head(q_rot, k_rot, y[2 * e:3 * e].astype(BF16), o_ref, lse_ref, i, mul, between)

    def mlp(u):
        return (u * gelu_parts(u)[1]).astype(BF16)

    def project(c, outs):
        tall = jnp.concatenate([o_a[:, spans[c]], m_a[:, spans[c]], outs[c], m_b[:, spans[c]]], axis=0)
        z_sc[b, :, spans[c]] += dot_nn(wo_sc[FULL], tall)

    def project_late(c, outs):
        if c > 0:
            project(c - 1, outs)

    o_a = attend(0, y_a, next_head)
    m_a = mlp(y_a[3 * e:])
    m_b = mlp(y_ref[1, 3 * e:])
    o_b = attend(1, y_ref[1, :3 * e], project_late)
    project(n_c - 1, [o_b[:, span] for span in spans])

    @pl.when(g == final)
    def _():
        if last:
            mod = as_col(mod_ref[FULL])
            branch = z_sc[b] + mod[:, 3:4]
            br_ref[FULL] = branch
            x_new = x_ref[FULL].astype(F32) + mod[:, 2:3] * branch
            if token_out:
                s_t = xo_ref.shape[1]
                for t in range(token_out):
                    xo_ref[t] = x_new[:, t * s_t:(t + 1) * s_t].T.astype(BF16)
            else:
                xo_ref[FULL] = x_new.astype(BF16)
        else:
            z_out[FULL] = z_sc[b]


def bwd_kernel(e, dbr_ref, h_ref, wa0_ref, wb0_ref, wa1_ref, wb1_ref, qk_ref, cos_ref, sin_ref, y_ref, o_ref, lse_ref, keep_ref, send_ref, gb_ref, dqk_ref, dh_ref, dh_sc, acc_sc, dj_sc, dp_new, jn_new, dp_sc, jn_sc, win_sc):
    step = pl.program_id(0)
    n = pl.num_programs(0) - 1
    cols = y_ref.shape[1]
    rows = dj_sc.shape[0] // 2
    s_len = dbr_ref.shape[-1]
    b = lax.rem(step, 2)
    scale = e ** -0.5
    mul = scale * LOG2E

    @pl.when(step == 0)
    def _():
        for ref in (dqk_ref, dh_sc, acc_sc, dp_sc, jn_sc, win_sc):
            ref[FULL] = jnp.zeros_like(ref)

    def dense():
        b_prev = 1 - b
        again = b_prev.astype(F32)
        gwi = dot_nt(dp_sc[FULL], h_ref[b_prev]) + again * acc_sc[:2 * cols]
        acc_sc[:2 * cols] = gwi
        gwo = dot_nt(jn_sc[FULL], dbr_ref[b_prev]) + again * acc_sc[2 * cols:]
        acc_sc[2 * cols:] = gwo
        for i, ref in enumerate((keep_ref, send_ref)):
            ref[:cols] = gwi[i * cols:(i + 1) * cols].astype(BF16)
            ref[cols:] = gwo[i * rows:(i + 1) * rows].astype(BF16)
        dh_sc[b_prev] += dot_nn(win_sc[FULL], dp_sc[FULL])

    def attention():
        own = lax.rem(step // 2, 2) == 0
        d_br = dbr_ref[b]
        cos_t, sin_t = cos_ref[FULL], sin_ref[FULL]
        q_col, k_col = [as_col(qk_ref[i])[:, :1] for i in range(2)]
        w_pair = [jnp.where(own, x[FULL], y[FULL]) for x, y in ((wa0_ref, wa1_ref), (wb0_ref, wb1_ref))]
        for i in range(2):
            dj_sc[i * rows:(i + 1) * rows] = dot_nn(w_pair[i][cols:], d_br).astype(BF16)
        sums = []
        for i in range(2):
            q_hat, q_inv, q_rot = norm_rope(y_ref[i, :e], q_col, cos_t, sin_t)
            k_hat, k_inv, k_rot = norm_rope(y_ref[i, e:2 * e], k_col, cos_t, sin_t)
            v_t = y_ref[i, 2 * e:3 * e].astype(BF16)
            o_t = o_ref[i]
            d_o = dj_sc[i * rows:i * rows + e]
            d_sum = jnp.sum(d_o.astype(F32) * o_t.astype(F32), axis=0, keepdims=True)
            d_q, d_k, d_v = [], 0.0, 0.0
            for c in range(s_len // CHUNK):
                span = slice(c * CHUNK, (c + 1) * CHUNK)
                p = jnp.exp2(dot_tn(k_rot, q_rot[:, span]) * mul - lse_ref[i:i + 1, span])
                d_p = dot_tn(v_t, d_o[:, span])
                d_s = (p * (d_p - d_sum[:, span])).astype(BF16)
                d_q.append(dot_nn(k_rot, d_s))
                d_k = d_k + dot_nt(q_rot[:, span], d_s)
                d_v = d_v + dot_nt(d_o[:, span], p.astype(BF16))
            d_qraw, d_qs = norm_rope_bwd(jnp.concatenate(d_q, axis=1) * scale, q_hat, q_inv, q_col, cos_t, sin_t)
            d_kraw, d_ks = norm_rope_bwd(d_k * scale, k_hat, k_inv, k_col, cos_t, sin_t)
            dqk_ref[0] += d_qs
            dqk_ref[1] += d_ks
            u = y_ref[i, 3 * e:]
            t, half = gelu_parts(u)
            jn_new[i * rows:i * rows + e] = o_t
            jn_new[i * rows + e:(i + 1) * rows] = (u * half).astype(BF16)
            slope = half + 0.5 * u * (1.0 - t * t) * (GELU_C * (1.0 + 3.0 * GELU_A * u * u))
            d_u = dj_sc[i * rows + e:(i + 1) * rows].astype(F32) * slope
            off = i * cols
            part_sums = []
            for part in (d_qraw, d_kraw, d_v, d_u):
                dp_new[off:off + part.shape[0]] = part.astype(BF16)
                part_sums.append(jnp.sum(part, axis=1, keepdims=True))
                off += part.shape[0]
            sums.append(as_row(jnp.concatenate(part_sums, axis=0)))
        for i in range(2):
            gb_ref[i] = jnp.where(b == 0, sums[i], gb_ref[i] + sums[i])
        return w_pair

    @pl.when(step < n)
    def _():
        dense()
        w_pair = attention()
        dp_sc[FULL] = dp_new[FULL]
        jn_sc[FULL] = jn_new[FULL]
        win_sc[FULL] = jnp.concatenate([w[:cols] for w in w_pair], axis=0).T

    @pl.when(step == n)
    def _():
        dense()

    @pl.when(step >= n - 1)
    def _():
        dh_ref[FULL] = dh_sc[1 - b]


def edge_kernel(n_exit, has_entry, token_g, token_out, *refs):
    refs = list(refs)
    take = refs.pop
    g_ref = take(0)
    if n_exit:
        x_ref, mod_ref = take(0), take(0)
        dh_refs = [take(0) for _ in range(n_exit)]
    if has_entry:
        mod2_ref, br_ref = take(0), take(0)
    if n_exit:
        gx_ref = take(0)
    if has_entry:
        if token_g:
            gt_ref = take(0)
        dbr_ref = take(0)
    sum_ref = take(0)
    grad = g_ref[FULL].astype(F32).T if token_g else g_ref[FULL].astype(F32)
    parts = []
    if n_exit:
        d_h = dh_refs[0][FULL]
        for ref in dh_refs[1:]:
            d_h = d_h + ref[FULL]
        x = x_ref[FULL].astype(F32)
        cent = x - jnp.mean(x, axis=0, keepdims=True)
        inv = lax.rsqrt(jnp.mean(cent * cent, axis=0, keepdims=True) + NORM_EPS)
        hat = cent * inv
        parts += [jnp.sum(d_h, axis=1, keepdims=True), jnp.sum(d_h * hat, axis=1, keepdims=True)]
        d_hat = d_h * (1.0 + as_col(mod_ref[FULL])[:, 1:2])
        d_x = inv * (d_hat - jnp.mean(d_hat, axis=0, keepdims=True) - hat * jnp.mean(d_hat * hat, axis=0, keepdims=True))
        grad = grad + d_x
        if token_out:
            gx_ref[FULL] = grad.T.astype(BF16)
        else:
            gx_ref[FULL] = grad.astype(BF16)
            grad = grad.astype(BF16).astype(F32)
    if has_entry:
        if token_g:
            gt_ref[FULL] = grad.astype(BF16)
        gated = grad * as_col(mod2_ref[FULL])[:, 2:3]
        parts += [jnp.sum(grad * br_ref[FULL], axis=1, keepdims=True), jnp.sum(gated, axis=1, keepdims=True)]
        dbr_ref[FULL] = gated.astype(BF16)

    @pl.when(pl.program_id(1) == 0)
    def _():
        sum_ref[FULL] = jnp.zeros_like(sum_ref)

    for i, part in enumerate(parts):
        sum_ref[i:i + 1] += as_row(part)


def params(n_axes):
    return pltpu.CompilerParams(dimension_semantics=("arbitrary",) * n_axes, vmem_limit_bytes=VMEM)


def shape_of(dtype, *shape):
    return jax.ShapeDtypeStruct(shape, dtype)


def edge(grad, exit_args, entry_args, token_g, token_out):
    if token_g:
        n_t, n_b, s_t, dim = grad.shape
    else:
        n_t, (n_b, dim, s_t) = SPLIT, grad.shape
        s_t = s_t // n_t
    act = pl.BlockSpec((SQ, dim, s_t), lambda b, t: (b, 0, t))
    rows = pl.BlockSpec((SQ, 8, dim), lambda b, t: (b, 0, 0))
    tok = pl.BlockSpec((SQ, SQ, s_t, dim), lambda b, t: (t, b, 0, 0))
    shape_act = shape_of(BF16, n_b, dim, n_t * s_t)
    args, in_specs, out_specs, out_shape = [grad], [tok if token_g else act], [], []
    if exit_args:
        x_t, mod_l, d_hs = exit_args
        args += [x_t, mod_l, *d_hs]
        in_specs += [act, rows] + [act] * len(d_hs)
        out_specs.append(tok if token_out else act)
        out_shape.append(shape_of(BF16, n_t, n_b, s_t, dim) if token_out else shape_act)
    if entry_args:
        args += entry_args
        in_specs += [rows, act]
        out_specs += [act] * (1 + token_g)
        out_shape += [shape_act] * (1 + token_g)
    return pl.pallas_call(
        functools.partial(edge_kernel, len(exit_args[2]) if exit_args else 0, bool(entry_args), token_g, token_out),
        grid=(n_b, n_t), in_specs=in_specs, out_specs=out_specs + [rows], out_shape=out_shape + [shape_of(F32, n_b, 8, dim)],
        compiler_params=params(2),
        cost_estimate=pl.CostEstimate(flops=10 ** 6, bytes_accessed=10 ** 7, transcendentals=0),
        name="edge",
    )(*args)


def wmod_kernel(s_ref, d_ref, o_ref):
    o_ref[FULL] = dot_tn(s_ref[FULL], d_ref[FULL].astype(BF16))


def wmod_grad(silu_all, d_mod):
    n_l, n_all, width = d_mod.shape
    dim = silu_all.shape[1]
    piece = dim // 3
    return pl.pallas_call(
        wmod_kernel,
        grid=(n_l, 3),
        in_specs=[pl.BlockSpec((n_all, piece), lambda l, i: (0, i)), pl.BlockSpec((SQ, n_all, width), lambda l, i: (l, 0, 0))],
        out_specs=pl.BlockSpec((SQ, piece, width), lambda l, i: (l, i, 0)),
        out_shape=shape_of(F32, n_l, dim, width),
        compiler_params=params(2),
        cost_estimate=pl.CostEstimate(flops=10 ** 6, bytes_accessed=10 ** 7, transcendentals=0),
        name="wmod_grad",
    )(silu_all, d_mod)


def block_forward(slot, x_in, mod_rows, w_pair, b_rows, qk, cos_t, sin_t, prev, token_in, token_out):
    first, last = slot == 0, slot == 1
    token_in = token_in and first
    n_j, dim = w_pair[0].shape[:2]
    n_c = len(w_pair)
    cols = b_rows.shape[-1]
    e = qk.shape[-1]
    s_len = cos_t.shape[1]
    n_b = mod_rows.shape[0]
    final = n_j - 1
    full = lambda *shape: pl.BlockSpec(shape, lambda g, b: (0,) * len(shape))
    head6 = lambda n, m: pl.BlockSpec((SQ, SQ, n_c, SQ, n, m), lambda g, b: (b, slot, 0, g, 0, 0))
    act = lambda idx: pl.BlockSpec((SQ, dim, s_len), lambda g, b: (idx(g, b), 0, 0))
    at_start = lambda g, b: jnp.where(g == 0, b, n_b - 1)
    at_end = lambda g, b: jnp.where(g == final, b, 0)
    tok = lambda n, idx: pl.BlockSpec((n, SQ, s_len // n, dim), lambda g, b: (0, idx(g, b), 0, 0))
    weight = pl.BlockSpec((SQ, dim, dim), lambda g, b: (g, 0, 0))
    args = [mod_rows, *w_pair, b_rows, qk, cos_t, sin_t, x_in]
    in_specs = [
        pl.BlockSpec((SQ, 8, dim), lambda g, b: (b, 0, 0)), weight, weight,
        pl.BlockSpec((n_c, SQ, 8, cols), lambda g, b: (0, g, 0, 0)),
        full(2, 8, e), full(e // 2, s_len), full(e // 2, s_len),
        tok(x_in.shape[0], at_start) if token_in else act(at_start if first else at_end),
    ]
    aliases = {}
    if not first:
        args += [prev[3], prev[4], *prev[:3]]
        in_specs += [act(at_start), act(at_start)] + [pl.BlockSpec(memory_space=pl.ANY)] * 3
        aliases = {len(args) - 3 + i: i for i in range(3)}
    shape16, shape32 = shape_of(BF16, n_b, dim, s_len), shape_of(F32, n_b, dim, s_len)
    out_specs = [head6(cols, s_len), head6(e, s_len), pl.BlockSpec((SQ, SQ, SQ, n_c, s_len), lambda g, b: (b, slot, g, 0, 0))]
    out_shape = [shape_of(F32, n_b, 2, n_c, n_j, cols, s_len), shape_of(BF16, n_b, 2, n_c, n_j, e, s_len), shape_of(F32, n_b, 2, n_j, n_c, s_len)]
    if first:
        out_specs += [act(at_start)] * (1 + token_in)
        out_shape += [shape16] * (1 + token_in)
    out_specs.append(act(at_end))
    out_shape.append(shape32)
    if last:
        out_specs.append(tok(token_out, at_end) if token_out else act(at_end))
        out_shape.append(shape_of(BF16, token_out, n_b, s_len // token_out, dim) if token_out else shape16)
    heads = n_c * n_j * n_b
    return pl.pallas_call(
        functools.partial(fwd_kernel, e, first, last, token_in, token_out),
        grid=(n_j, n_b), in_specs=in_specs, out_specs=out_specs, out_shape=out_shape,
        input_output_aliases=aliases,
        scratch_shapes=[pltpu.VMEM((n_b, dim, s_len), F32), pltpu.VMEM((n_b, dim, s_len), BF16), pltpu.VMEM((dim, 2 * (dim - cols)), BF16)],
        compiler_params=params(2),
        cost_estimate=pl.CostEstimate(flops=2 * heads * s_len * (dim * dim + 8 * s_len * e), bytes_accessed=10 ** 7, transcendentals=heads * s_len * s_len),
        name="block_fwd",
    )(*args)


def block_backward(j_lo, j_n, d_br, h_t, ws, qk, cos_t, sin_t, y, o, lse):
    n_b, dim, s_len = d_br.shape
    n_c, cols = y.shape[2], y.shape[4]
    e = qk.shape[-1]
    rows = dim - cols
    n = 2 * j_n * n_b
    group = lambda s: jnp.minimum(s, n - 1) // n_b
    before = lambda s: jnp.maximum(s - 1, 0) // n_b
    once = pl.Buffered(1)
    full = lambda *shape: pl.BlockSpec(shape, lambda s: (0,) * len(shape), pipeline_mode=once)
    head6 = lambda n_r, m: pl.BlockSpec((SQ, SQ, n_c, SQ, n_r, m), lambda s: (jnp.minimum(s, n - 1) % n_b, group(s) % 2, 0, j_lo + group(s) // 2, 0, 0))
    weight = pl.BlockSpec((SQ, dim, dim), lambda s: (j_lo + group(s) // 2, 0, 0))
    grad = pl.BlockSpec((SQ, SQ, dim, dim), lambda s: (before(s) % 2, before(s) // 2, 0, 0))
    heads = 2 * n_c * j_n * n_b
    return pl.pallas_call(
        functools.partial(bwd_kernel, e),
        grid=(n + 1,),
        in_specs=[
            full(n_b, dim, s_len), full(n_b, dim, s_len), weight, weight, weight, weight,
            full(2, 8, e), full(e // 2, s_len), full(e // 2, s_len),
            head6(cols, s_len), head6(e, s_len),
            pl.BlockSpec((SQ, SQ, SQ, n_c, s_len), lambda s: (jnp.minimum(s, n - 1) % n_b, group(s) % 2, j_lo + group(s) // 2, 0, 0)),
        ],
        out_specs=[
            grad, grad,
            pl.BlockSpec((n_c, SQ, SQ, 1, cols), lambda s: (0, group(s) % 2, group(s) // 2, 0, 0)),
            pl.BlockSpec((2, e, 1), lambda s: (0, 0, 0)),
            pl.BlockSpec((SQ, dim, s_len), lambda s: (jnp.where(s == n, 1, 0), 0, 0)),
        ],
        out_shape=[
            shape_of(BF16, 2, j_n, dim, dim), shape_of(BF16, 2, j_n, dim, dim),
            shape_of(F32, n_c, 2, j_n, 1, cols), shape_of(F32, 2, e, 1), shape_of(F32, n_b, dim, s_len),
        ],
        scratch_shapes=[
            pltpu.VMEM((n_b, dim, s_len), F32),
            pltpu.VMEM((2 * dim, dim), F32),
            pltpu.VMEM((2 * rows, s_len), BF16),
            pltpu.VMEM((2 * cols, s_len), BF16), pltpu.VMEM((2 * rows, s_len), BF16),
            pltpu.VMEM((2 * cols, s_len), BF16), pltpu.VMEM((2 * rows, s_len), BF16),
            pltpu.VMEM((dim, 2 * cols), BF16),
        ],
        compiler_params=params(1),
        cost_estimate=pl.CostEstimate(flops=4 * heads * s_len * (dim * dim + 10 * s_len * e), bytes_accessed=10 ** 7, transcendentals=heads * s_len * s_len),
        name="block_bwd",
    )(d_br, h_t, *ws, qk, cos_t, sin_t, y, o, lse)


def even_first(arr, e):
    lead = arr.shape[:-1]
    return jnp.swapaxes(arr.reshape(*lead, e // 2, 2), -1, -2).reshape(*lead, e)


def interleave(arr, e):
    lead = arr.shape[:-1]
    return jnp.swapaxes(arr.reshape(*lead, 2, e // 2), -1, -2).reshape(*lead, e)


def solution(mesh):
    n_tp = mesh.shape["tp"]
    act, part, heads1, heads2, whole = P("dp", "tp"), P("dp"), P(None, "tp"), P(None, None, "tp"), P()
    in_specs = (act, part, P("tp"), P("tp"), whole, whole, heads2, heads1, whole, whole, heads1, whole, act)
    out_specs = (act, act, part, part, P("dp", None, "tp"), act, part, part, act, part)
    peer_core = [(i, i ^ 1) for i in range(n_tp)]
    across = [(i, i ^ 2) for i in range(n_tp)]

    def swap(arr):
        return lax.all_to_all(arr, "tp", 0, 0)

    def device_step(x_in, cond_vec, rope_cos, rope_sin, w_mod, b_mod, w_in, b_in, q_scale, k_scale, w_out, b_out, d_out):
        n_l, dim, n_j, cols = w_in.shape
        e = q_scale.shape[1]
        n_all, s_own = x_in.shape[:2]
        n_b = n_all // n_tp
        me = lax.axis_index("tp")
        pairs = np.arange(e).reshape(e // 2, 2).T.reshape(-1)
        perm = np.concatenate([pairs, e + pairs, np.arange(2 * e, cols)])
        perm_mat = jnp.asarray(np.eye(cols, dtype=np.float32)[perm], BF16)

        n_rope = e * s_own
        b_perm = jnp.einsum("ec,lhc->lhe", perm_mat, b_in, preferred_element_type=F32)
        small_in = jnp.concatenate([rope_cos.T.reshape(-1), rope_sin.T.reshape(-1), b_perm.reshape(-1)])
        small_all = lax.all_gather(small_in, "tp", axis=0, tiled=False)
        small_all, x_in, w_in, w_out = lax.optimization_barrier((small_all, x_in, w_in, w_out))

        tie = swap(x_in.reshape(n_tp, n_b, s_own, dim))
        w_local = []
        for l in range(n_l):
            w_in_t = jnp.einsum("ec,dhc->hed", perm_mat, w_in[l], preferred_element_type=F32).astype(BF16)
            w_local.append(jnp.concatenate([w_in_t, w_out[l]], axis=1))
        w_own = [(w, lax.ppermute(w, "tp", peer_core)) for w in w_local]

        tables = jnp.moveaxis(small_all[:, :n_rope].reshape(n_tp, e, s_own), 0, 1).reshape(e, n_tp * s_own)
        cos_t, sin_t = tables[:e // 2], tables[e // 2:]
        b_all = small_all[:, n_rope:].reshape(n_tp, n_l, n_j, 1, cols)
        b_rel = jnp.stack([lax.dynamic_index_in_dim(b_all, me ^ i, 0, keepdims=False) for i in range(n_tp)])
        b_rel = jnp.broadcast_to(b_rel, (n_tp, n_l, n_j, 8, cols))

        silu_all = jax.nn.silu(cond_vec.astype(F32)).astype(BF16)
        silu_own = lax.dynamic_slice_in_dim(silu_all, me * n_b, n_b, 0)
        mod = jnp.einsum("bd,ldm->lbm", silu_own, w_mod, preferred_element_type=F32) + b_mod.astype(F32)[:, None]
        bias = jnp.broadcast_to(b_out.astype(F32)[:, None, None], (n_l, n_b, 5, dim))
        mod_rows = jnp.concatenate([mod.reshape(n_l, n_b, 3, dim), bias], axis=2)
        qk = even_first(jnp.stack([q_scale, k_scale], axis=1).astype(F32), e)
        qk = jnp.broadcast_to(qk[:, :, None], (n_l, 2, 8, e))

        saved, ws = [], []
        for l in range(n_l):
            consts = (qk[l], cos_t, sin_t)
            mine, tie = lax.optimization_barrier((w_local[l], tie))
            if l == 0:
                x_cur = tie
            got = lax.ppermute(mine, "tp", across)
            half = block_forward(0, x_cur, mod_rows[l], w_own[l], b_rel[:2, l], *consts, (), l == 0, 0)
            x_t = half[4] if l == 0 else x_cur
            got, h_t = lax.optimization_barrier((got, half[3]))
            tie = got
            w_other = (got, lax.ppermute(got, "tp", peer_core))
            y, o, lse, branch, x_cur = block_forward(1, x_t, mod_rows[l], w_other, b_rel[2:, l], *consts, (*half[:3], h_t, half[-1]), False, n_tp * (l == n_l - 1))
            saved.append((x_t, y, o, lse, h_t, branch))
            ws.append((*w_own[l], *w_other))
        d_late, tie = lax.optimization_barrier((d_out, tie))
        g_tok = swap(d_late.reshape(n_tp, n_b, s_own, dim))
        x_out = swap(x_cur)

        grads, small = [None] * n_l, [None] * n_l
        top = n_l - 1
        g_t, d_br, sums_in = edge(g_tok, (), (mod_rows[top], saved[top][5]), True, False)
        d_gate, d_bias = sums_in[:, 0], sums_in[:, 1]
        for l in reversed(range(n_l)):
            x_t, y, o, lse, h_t, branch = saved[l]
            if l == 0:
                d_br, x_out = lax.optimization_barrier((d_br, x_out))
            d_hs, d_qk, gb, gw = [], 0.0, [], []
            for j, width in ((0, n_j),) if l else ((0, n_j - 1), (n_j - 1, 1)):
                keep, send, gb_j, dqk_j, dh_j = block_backward(j, width, d_br, h_t, ws[l], qk[l], cos_t, sin_t, y, o, lse)
                d_hs.append(dh_j)
                d_qk = d_qk + dqk_j
                gb.append(gb_j)
                chip_sum = (keep.astype(F32) + lax.ppermute(send, "tp", peer_core).astype(F32)).astype(BF16)
                from_chip = lax.ppermute(chip_sum[1], "tp", across)
                gw.append((chip_sum[0].astype(F32) + from_chip.astype(F32)).astype(BF16))
            entry = (mod_rows[l - 1], saved[l - 1][5]) if l > 0 else ()
            edge_out = edge(g_t, (x_t, mod_rows[l], d_hs), entry, False, l == 0)
            g_t, sums = edge_out[0], edge_out[-1]
            grads[l] = jnp.concatenate(gw)
            d_mod = jnp.stack([sums[:, 0], sums[:, 1], d_gate], axis=1)
            gb = jnp.concatenate(gb, axis=2).reshape(2, 2, n_j * cols)
            gb = jnp.stack([lax.dynamic_index_in_dim(lax.dynamic_index_in_dim(gb, (i ^ me) % 2, 0, keepdims=False), (i ^ me) // 2, 0, keepdims=False) for i in range(n_tp)])
            small[l] = jnp.concatenate([d_mod.reshape(-1), jnp.sum(d_bias, axis=0), d_qk.reshape(-1), gb.reshape(-1)])
            if l > 0:
                d_br = edge_out[1]
                d_gate, d_bias = sums[:, 2], sums[:, 3]

        gathered = swap(jnp.broadcast_to(jnp.stack(small), (n_tp, n_l, small[0].shape[0])))
        g_t, gathered = lax.optimization_barrier((g_t, gathered)) if SMALL_FIRST else (g_t, gathered)
        grad_x = swap(g_t)
        n_mod = n_b * 3 * dim
        d_mod = jnp.moveaxis(gathered[:, :, :n_mod].reshape(n_tp, n_l, n_b, 3 * dim), 1, 0).reshape(n_l, n_all, 3 * dim)
        sums = jnp.sum(gathered[:, :, n_mod:], axis=0)
        g_wmod = wmod_grad(silu_all, d_mod)
        g_bmod = jnp.sum(d_mod, axis=1)
        g_qk = interleave(sums[:, dim:dim + 2 * e].reshape(n_l, 2, e), e)
        g_b = lax.dynamic_index_in_dim(sums[:, dim + 2 * e:].reshape(n_l, n_tp, n_j, cols), me, 1, keepdims=False)
        g_bin = jnp.concatenate([interleave(g_b[..., :e], e), interleave(g_b[..., e:2 * e], e), g_b[..., 2 * e:]], axis=-1)
        gw_all = jnp.stack(grads)
        g_win = jnp.einsum("ec,lhed->ldhc", perm_mat, gw_all[:, :, :cols], preferred_element_type=F32).astype(BF16)
        return (x_out.reshape(n_all, s_own, dim), grad_x.reshape(n_all, s_own, dim), g_wmod, g_bmod, g_win, g_bin, g_qk[:, 0], g_qk[:, 1], gw_all[:, :, cols:], sums[:, :dim])

    return jax.shard_map(device_step, mesh=mesh, in_specs=in_specs, out_specs=out_specs, check_vma=False)
```

time: 1950 us -> 928 us (0.48)
  matrix products: 784 us -> 13.3 us
  Pallas kernels: 0 us -> 587 us
  other arithmetic: 463 us -> 38.5 us
  waiting for transfers between devices: 532 us -> 211 us
  local copies, waits for them, and re-layouts: 131 us -> 34.7 us
  starting transfers between devices: 0.37 us -> 29.8 us
    dot_general x26 -> x5, matrix products: 705 us -> 13.3 us  [the longest x2 4.05 us: device_step(): jnp.einsum('ec,dhc->hed', perm_mat, w_in[l], preferred_element_type=F32)]
    pallas_call x0 -> x11, Pallas kernels: none -> 587 us  [the longest x3 340 us: block_backward(): pl.pallas_call(functools.partial(bwd_kernel, e), grid=(n + 1,), in_specs=...]
    all_gather x4 -> x0, waiting for transfers between devices: 288 us -> none  [the longest x2 156 us: device_fn(): lax.all_gather(gated_grad.astype(jnp.bfloat16), 'tp', axis=1, tiled=True)]
    reduce_scatter x4 -> x0, waiting for transfers between devices: 221 us -> none  [the longest x2 169 us: device_fn(): lax.psum_scatter(part_out.astype(jnp.bfloat16), 'tp', scatter_dimension=1...]
    add_any x10 -> x0, other arithmetic: 161 us -> none  [the longest x2 60.2 us: mix_heads(): jax.nn.gelu(projected[..., 3 * head_dim:], approximate=True)]
    all_to_all x0 -> x5, waiting for transfers between devices: none -> 110 us  [swap(): return lax.all_to_all(arr, 'tp', 0, 0)]
    reduce_sum x17 -> x2, other arithmetic: 104 us -> 0.74 us  [the longest x1 0.68 us: device_step(): g_bmod = jnp.sum(d_mod, axis=1)]
    ppermute x0 -> x12, waiting for transfers between devices: none -> 101 us  [the longest x3 75.3 us: device_step(): from_chip = lax.ppermute(chip_sum[1], 'tp', across)]
  transfers between devices with their start and end apart: 9 -> 17, of which waited for: 8 -> 6; matrix products, arithmetic and copies ran while one was open for 11% -> 6% of each run, Pallas kernels for 0% -> 64%
where the time goes in v3:
time: 928 us; the launch traced here: 923 us
  Pallas kernels  587 us (63%)
  waiting for transfers between devices  211 us (23%)
  other arithmetic  38.5 us (4%)
  local copies, waits for them, and re-layouts  34.7 us (4%)
  starting transfers between devices  29.8 us (3%)
  matrix products  13.3 us (1%)
    pallas_call x3, Pallas kernels, block_backward(): pl.pallas_call(functools.partial(bwd_kernel, e), grid=(n + 1,), in_specs=...  340 us
    pallas_call x4, Pallas kernels, block_forward(): pl.pallas_call(functools.partial(fwd_kernel, e, first, last, token_in, to...  198 us
    all_to_all x5, waiting for transfers between devices, swap(): return lax.all_to_all(arr, 'tp', 0, 0)  110 us
    ppermute x3, waiting for transfers between devices, device_step(): from_chip = lax.ppermute(chip_sum[1], 'tp', across)  75.3 us
    pallas_call x3, Pallas kernels, edge(): pl.pallas_call(functools.partial(edge_kernel, len(exit_args[2]) if exit_a...  40.5 us
    ppermute x2, waiting for transfers between devices, device_step(): got = lax.ppermute(mine, 'tp', across)  24.1 us
    all_to_all x5, starting transfers between devices, swap(): return lax.all_to_all(arr, 'tp', 0, 0)  22.6 us
    convert_element_type x3, other arithmetic, device_step(): (keep.astype(F32) + lax.ppermute(send, 'tp', peer_core).astype(F32)).asty...  18.9 us
  transfers between devices with their start and end apart: 17, of which 6 were waited for; matrix products, arithmetic and copies ran while one was open for 6% of the time, Pallas kernels for 64%

profile of v3, /device:TPU:0, one launch (start us, length us, event | category | flops | bytes accessed | tf_op | source)
XLA Modules:
  0.0 923.5 jit_solution(2199148431909621966)
XLA Ops:
  2.2 1.2 convolution_bitcast_fusion
  3.7 7.8 all-gather.1
  11.6 3.1 slice_bitcast_fusion.4
  14.7 1.2 convert_bitcast_fusion.1
  16.0 2.0 pad_maximum_fusion.1.refs_1_.wa0_ref
  18.3 4.9 all-to-all-start
  23.4 4.0 fusion.6
  27.5 32.8 %all-to-all-done.refs_7_ = bf16[4,2,256,768]{3,2,1,0:T(8,128)(2,1)} async-done(((bf16[4,2,256,768]{3,2,1,0:T(8,128)(2,1)}), bf16[4,2,256,768]{3,2,1,0:T(8,128)(2,1)}, u32[]{:S(2)}, u32[]{:S(2)}) %all-to-all-start) | async-done | bytes 3145760 | tf_op jit(solution)/shard_map/all_to_all | solution.py:505
  64.7 49.7 %block_fwd.4 = (f32[2,2,2,3,448,1024]{5,4,3,2,1,0:T(8,128)}, bf16[2,2,2,3,64,1024]{5,4,3,2,1,0:T(8,128)(2,1)}, f32[2,2,3,2,1024]{4,3,2,1,0:T(2,128)}, bf16[2,768...) custom-call(f32[2,8,768]{2,1,0:T(8,128)} %get-tuple-element.131.refs_0_.refs_4_.refs_2_, ...), custom_call_target="tpu_custom_call" | custom-call | flops 27380416512 | bytes 10000000 | tf_op jit(solution)/shard_map/block_fwd/pallas_call | solution.py:428
  114.4 24.1 %collective-permute-done.refs_1_.wa1_ref = bf16[3,768,768]{2,1,0:T(8,128)(2,1)} collective-permute-done((bf16[3,768,768]{2,1,0:T(8,128)(2,1)}, bf16[3,768,768]{2,1,0:T(8,128)(2,1)}, u32[]{:S(2)}, u32[]{:S(2)}) %collective-permute-start) | collective-permute-done | bytes 3538976 | tf_op jit(solution)/shard_map/ppermute | solution.py:550
  138.5 2.8 convert_bitcast_fusion.2
  141.3 2.0 pad_maximum_fusion.refs_1_.wa0_ref
  145.7 49.8 %block_fwd.5 = (f32[2,2,2,3,448,1024]{5,4,3,2,1,0:T(8,128)}, bf16[2,2,2,3,64,1024]{5,4,3,2,1,0:T(8,128)(2,1)}, f32[2,2,3,2,1024]{4,3,2,1,0:T(2,128)}, f32[2,768,1024]{2,1,0:T(8,128)}, bf16[2,768,1024]{2,1,0:T(8,128)(2,1)}) custom-call(f32[2,8,768]{2,1,0:T(8,128)} %get-tuple-element.131.refs_0_.refs_4_.r, ...), custom_call_target="tpu_custom_call", output_to_operand_aliasing={{0}: (10, {}), {1}: (11, {}), {2}: (12, {})} | custom-call | flops 27380416512 | bytes 10000000 | tf_op jit(solution)/shard_map/block_fwd/pallas_call | solution.py:428
  196.8 49.2 %block_fwd.6 = (f32[2,2,2,3,448,1024]{5,4,3,2,1,0:T(8,128)}, bf16[2,2,2,3,64,1024]{5,4,3,2,1,0:T(8,128)(2,1)}, f32[2,2,3,2,1024]{4,3,2,1,0:T(2,128)}, bf16[2,768,1024]{2,1,0:T(8,128)(2,1)}, f32[2,768,1024]{2,1,0:T(8,128)}) custom-call(f32[2,8,768]{2,1,0:T(8,128)} %get-tuple-element.130.refs_0_.refs_1_.refs_2_, ...), custom_call_target="tpu_custom_call" | custom-call | flops 27380416512 | bytes 10000000 | tf_op jit(solution)/shard_map/block_fwd/pallas_call | solution.py:428
  246.2 4.8 all-to-all-start.1
  251.0 1.5 collective-permute-done.5.refs_2_.wb1_ref
  253.2 49.7 %block_fwd.7 = (f32[2,2,2,3,448,1024]{5,4,3,2,1,0:T(8,128)}, bf16[2,2,2,3,64,1024]{5,4,3,2,1,0:T(8,128)(2,1)}, f32[2,2,3,2,1024]{4,3,2,1,0:T(2,128)}, f32[2,768,1024]{2,1,0:T(8,128)}, bf16[4,2,256,768]{3,2,1,0:T(8,128)(2,1)}) custom-call(f32[2,8,768]{2,1,0:T(8,128)} %get-tuple-element.130.refs_0_.refs_1, ...), custom_call_target="tpu_custom_call", output_to_operand_aliasing={{0}: (10, {}), {1}: (11, {}), {2}: (12, {})} | custom-call | flops 27380416512 | bytes 10000000 | tf_op jit(solution)/shard_map/block_fwd/pallas_call | solution.py:428
  302.9 4.7 all-to-all-start.2
  307.6 10.7 %edge.3 = (bf16[2,768,1024]{2,1,0:T(8,128)(2,1)}, bf16[2,768,1024]{2,1,0:T(8,128)(2,1)}, f32[2,8,768]{2,1,0:T(8,128)}) custom-call(bf16[4,2,256,768]{3,2,1,0:T(8,128)(2,1)} %all-to-all-done.1.refs_0_, f32[2,8,768]{2,1,0:T(8,128)} %get-tuple-element.130.refs_0_.refs_1_.refs_2_, f32[2,768,1024]{2,1,0:T(8,128)} %get-tuple-element.92.refs_2_), custom_call_target="tpu_custom_call" | custom-call | flops 1000000 | bytes 10000000 | tf_op jit(solution)/shard_map/edge/pallas_call | solution.py:358
  318.3 162.9 %block_bwd.3 = (bf16[2,3,768,768]{3,2,1,0:T(8,128)(2,1)}, bf16[2,3,768,768]{3,2,1,0:T(8,128)(2,1)}, f32[2,2,3,1,448]{4,3,2,1,0:T(1,128)}, f32[2,64,1]{2,1,0:T(8,128)}, f32[2,768,1024]{2,1,0:T(8,128)}) custom-call(bf16[2,768,1024]{2,1,0:T(8,128)(2,1)} %get-tuple-element.94.dbr_ref, bf16[2,768,1024]{2,1,0:T(8,128)(2,1)} %get-tuple-element.87.refs_8_.h_ref, ...), custom_call_target="tpu_custom_call" | custom-call | flops 122406567936 | bytes 10000000 | tf_op jit(solution)/shard_map/block_bwd/pallas_call | solution.py:453
  482.6 15.9 %edge.4 = (bf16[2,768,1024]{2,1,0:T(8,128)(2,1)}, bf16[2,768,1024]{2,1,0:T(8,128)(2,1)}, f32[2,8,768]{2,1,0:T(8,128)}) custom-call(bf16[2,768,1024]{2,1,0:T(8,128)(2,1)} %get-tuple-element.93.refs_0_, bf16[2,768,1024]{2,1,0:T(8,128)(2,1)} %get-tuple-element.83.refs_7_.refs_1_, f32[2,8,768]{2,1,0:T(8,128)} %get-tuple-element.130.refs_0_.refs_1_.refs_2_, ...), custom_call_target="tpu_custom_call" | custom-call | flops 1000000 | bytes 10000000 | tf_op jit(solution)/shard_map/edge/pallas_call | solution.py:358
  499.2 0.9 fusion.34
  500.4 0.9 fusion.33
  501.3 113.1 %block_bwd.4 = (bf16[2,2,768,768]{3,2,1,0:T(8,128)(2,1)}, bf16[2,2,768,768]{3,2,1,0:T(8,128)(2,1)}, f32[2,2,2,1,448]{4,3,2,1,0:T(1,128)}, f32[2,64,1]{2,1,0:T(8,128)}, f32[2,768,1024]{2,1,0:T(8,128)}) custom-call(bf16[2,768,1024]{2,1,0:T(8,128)(2,1)} %get-tuple-element.104.dbr_ref, bf16[2,768,1024]{2,1,0:T(8,128)(2,1)} %get-tuple-element.78.refs_8_.h_ref, ...), custom_call_target="tpu_custom_call" | custom-call | flops 81604378624 | bytes 10000000 | tf_op jit(solution)/shard_map/block_bwd/pallas_call | solution.py:453
  614.5 64.1 %block_bwd.5 = (bf16[2,1,768,768]{3,2,1,0:T(8,128)(2,1)}, bf16[2,1,768,768]{3,2,1,0:T(8,128)(2,1)}, f32[2,2,1,1,448]{4,3,2,1,0:T(1,128)}, f32[2,64,1]{2,1,0:T(8,128)}, f32[2,768,1024]{2,1,0:T(8,128)}) custom-call(bf16[2,768,1024]{2,1,0:T(8,128)(2,1)} %get-tuple-element.104.dbr_ref, bf16[2,768,1024]{2,1,0:T(8,128)(2,1)} %get-tuple-element.78.refs_8_.h_ref, ...), custom_call_target="tpu_custom_call" | custom-call | flops 40802189312 | bytes 10000000 | tf_op jit(solution)/shard_map/block_bwd/pallas_call | solution.py:453
  679.0 14.0 %edge.5 = (bf16[4,2,256,768]{3,2,1,0:T(8,128)(2,1)}, f32[2,8,768]{2,1,0:T(8,128)}) custom-call(bf16[2,768,1024]{2,1,0:T(8,128)(2,1)} %get-tuple-element.103.refs_0_, bf16[2,768,1024]{2,1,0:T(8,128)(2,1)} %get-tuple-element.77.refs_7_.refs_1_, f32[2,8,768]{2,1,0:T(8,128)} %get-tuple-element.131.refs_0_.refs_4_.refs_2_, ...), custom_call_target="tpu_custom_call" | custom-call | flops 1000000 | bytes 10000000 | tf_op jit(solution)/shard_map/edge/pallas_call | solution.py:358
  694.7 0.8 broadcast_in_dim.56
  695.6 3.5 all-to-all-start.4
  699.0 9.6 %add_convert_fusion = bf16[2,3,768,768]{3,2,1,0:T(8,128)(2,1)} fusion(bf16[2,3,768,768]{3,2,1,0:T(8,128)(2,1)} %collective-permute-done.10, bf16[2,3,768,768]{3,2,1,0:T(8,128)(2,1)} %get-tuple-element.124), kind=kLoop, calls=%fused_computation | loop fusion | flops 14155776 | bytes 21233664 | tf_op jit(solution)/shard_map/convert_element_type | solution.py:577
  708.6 4.0 slice_bitcast_fusion
  712.6 2.0 collective-permute-start.11
  714.6 7.0 add_convert_fusion.1
  721.6 4.7 all-to-all-start.3
  726.3 3.4 slice_bitcast_fusion.2
  729.7 2.0 collective-permute-start.7
  731.6 2.4 add_convert_fusion.2
  734.0 1.4 copy-done.2
  735.4 1.1 slice_bitcast_fusion.6
  739.4 7.7 wmod_grad.1
  749.0 77.1 %all-to-all-done.3 = bf16[4,2,256,768]{3,2,1,0:T(8,128)(2,1)} async-done(((bf16[4,2,256,768]{3,2,1,0:T(8,128)(2,1)}), bf16[4,2,256,768]{3,2,1,0:T(8,128)(2,1)}, u32[]{:S(2)}, u32[]{:S(2)}) %all-to-all-start.3) | async-done | bytes 3145760 | tf_op jit(solution)/shard_map/all_to_all | solution.py:505
  826.0 75.3 %collective-permute-done.9 = bf16[1,768,768]{2,1,0:T(8,128)(2,1)} collective-permute-done((bf16[1,768,768]{2,1,0:T(8,128)(2,1)}, bf16[1,768,768]{2,1,0:T(8,128)(2,1)}, u32[]{:S(2)}, u32[]{:S(2)}) %collective-permute-start.9) | collective-permute-done | bytes 1179680 | tf_op jit(solution)/shard_map/ppermute | solution.py:578
  901.4 2.1 fusion.9
  903.5 3.1 fusion.1
  906.9 3.1 fusion.5
  910.0 1.8 pad_maximum_fusion.2
  911.8 4.0 convert_bitcast_fusion
  915.8 3.8 copy.90
  919.5 3.8 copy.91
  (148 shorter events, 20.8 us)
Async XLA Ops:
  0.6 1.6 copy-start
  3.6 11.1 %copy-start.5 = (bf16[448,448,1]{1,0,2:T(8,128)(2,1)S(1)}, bf16[448,448,1]{1,0,2:T(8,128)(2,1)}, u32[]{:S(2)}) copy-start(bf16[448,448,1]{1,0,2:T(8,128)(2,1)} %constant.273) | copy-start | bytes 1204228
  3.6 11.1 %copy-start.17 = (bf16[2,768,3,448]{1,3,2,0:T(8,128)(2,1)S(1)}, bf16[2,768,3,448]{1,3,2,0:T(8,128)(2,1)}, u32[]{:S(2)}) copy-start(bf16[2,768,3,448]{1,3,2,0:T(8,128)(2,1)} %param.20) | copy-start | bytes 12386308
  18.0 5.3 copy-start.12
  18.0 5.3 copy-start.11
  18.0 45.5 %collective-permute-start.1 = (bf16[3,768,768]{2,1,0:T(8,128)(2,1)}, bf16[3,768,768]{2,1,0:T(8,128)(2,1)}, u32[]{:S(2)}, u32[]{:S(2)}) collective-permute-start(bf16[3,768,768]{2,1,0:T(8,128)(2,1)} %pad_maximum_fusion.1.refs_1_.wa0_ref), channel_id=1, source_target_pairs={{0,1},{1,0},{2,3},{3,2},{4,5},{5,4},{6,7},{7,6},{8,9},{9,8},{10,11... | collective-permute-start | bytes 10616840 | tf_op jit(solution)/shard_map/ppermute | solution.py:528
  18.3 41.9 %all-to-all-start = ((bf16[4,2,256,768]{3,2,1,0:T(8,128)(2,1)}), bf16[4,2,256,768]{3,2,1,0:T(8,128)(2,1)}, u32[]{:S(2)}, u32[]{:S(2)}) async-start(bf16[4,2,256,768]{3,2,1,0:T(8,128)(2,1)} %bitcast.10), calls=%async_computation | async-start | bytes 6291456 | tf_op jit(solution)/shard_map/all_to_all | solution.py:505
  23.4 4.1 copy-start.9
  23.4 38.8 %copy-start.15 = (bf16[2,64]{1,0:T(2,128)(2,1)S(1)}, bf16[2,64]{1,0:T(2,128)(2,1)}, u32[]{:S(2)}) copy-start(bf16[2,64]{1,0:T(2,128)(2,1)} %param.22) | copy-start | bytes 772
  23.4 39.0 %copy-start.16 = (bf16[2,64]{1,0:T(2,128)(2,1)S(1)}, bf16[2,64]{1,0:T(2,128)(2,1)}, u32[]{:S(2)}) copy-start(bf16[2,64]{1,0:T(2,128)(2,1)} %param.23) | copy-start | bytes 772
  23.4 39.4 %copy-start.14 = (bf16[2,768]{1,0:T(2,128)(2,1)S(1)}, bf16[2,768]{1,0:T(2,128)(2,1)}, u32[]{:S(2)}) copy-start(bf16[2,768]{1,0:T(2,128)(2,1)} %param.25) | copy-start | bytes 9220
  60.2 78.3 %collective-permute-start = (bf16[3,768,768]{2,1,0:T(8,128)(2,1)}, bf16[3,768,768]{2,1,0:T(8,128)(2,1)}, u32[]{:S(2)}, u32[]{:S(2)}) collective-permute-start(bf16[3,768,768]{2,1,0:T(8,128)(2,1)} %pad_maximum_fusion.1.refs_1_.wa0_ref), channel_id=1, source_target_pairs={{0,2},{1,3},{2,0},{3,1},{4,6},{5,7},{6,4},{7,5},{8,10},{9,11},{10,... | collective-permute-start | bytes 10616840 | tf_op jit(solution)/shard_map/ppermute | solution.py:550
  114.4 26.9 %copy-start.3 = (bf16[3,320,768]{2,1,0:T(8,128)(2,1)S(1)}, bf16[3,320,768]{2,1,0:T(8,128)(2,1)}, u32[]{:S(2)}) copy-start(bf16[3,320,768]{2,1,0:T(8,128)(2,1)} %get-tuple-element.127) | copy-start | bytes 4423684
  138.5 6.6 collective-permute-start.4
  143.3 52.2 %collective-permute-start.3 = (bf16[3,768,768]{2,1,0:T(8,128)(2,1)}, bf16[3,768,768]{2,1,0:T(8,128)(2,1)}, u32[]{:S(2)}, u32[]{:S(2)}) collective-permute-start(bf16[3,768,768]{2,1,0:T(8,128)(2,1)} %pad_maximum_fusion.refs_1_.wa0_ref), channel_id=1, source_target_pairs={{0,1},{1,0},{2,3},{3,2},{4,5},{5,4},{6,7},{7,6},{8,9},{9,8},{10,11... | collective-permute-start | bytes 10616840 | tf_op jit(solution)/shard_map/ppermute | solution.py:528
  143.9 102.0 %collective-permute-start.2 = (bf16[3,768,768]{2,1,0:T(8,128)(2,1)}, bf16[3,768,768]{2,1,0:T(8,128)(2,1)}, u32[]{:S(2)}, u32[]{:S(2)}) collective-permute-start(bf16[3,768,768]{2,1,0:T(8,128)(2,1)} %pad_maximum_fusion.refs_1_.wa0_ref), channel_id=1, source_target_pairs={{0,2},{1,3},{2,0},{3,1},{4,6},{5,7},{6,4},{7,5},{8,10},{9,11},{10,... | collective-permute-start | bytes 10616840 | tf_op jit(solution)/shard_map/ppermute | solution.py:550
  246.0 6.6 collective-permute-start.5
  246.2 56.7 %all-to-all-start.1 = ((bf16[4,2,256,768]{3,2,1,0:T(8,128)(2,1)}), bf16[4,2,256,768]{3,2,1,0:T(8,128)(2,1)}, u32[]{:S(2)}, u32[]{:S(2)}) async-start(bf16[4,2,256,768]{3,2,1,0:T(8,128)(2,1)} %bitcast.140), calls=%async_computation.1 | async-start | bytes 6291456 | tf_op jit(solution)/shard_map/all_to_all | solution.py:505
  302.9 198.4 %all-to-all-start.2 = ((bf16[4,2,256,768]{3,2,1,0:T(8,128)(2,1)}), bf16[4,2,256,768]{3,2,1,0:T(8,128)(2,1)}, u32[]{:S(2)}, u32[]{:S(2)}) async-start(bf16[4,2,256,768]{3,2,1,0:T(8,128)(2,1)} %get-tuple-element.101), calls=%async_computation.2 | async-start | bytes 6291456 | tf_op jit(solution)/shard_map/all_to_all | solution.py:505
  481.2 217.8 %collective-permute-start.10 = (bf16[2,3,768,768]{3,2,1,0:T(8,128)(2,1)}, bf16[2,3,768,768]{3,2,1,0:T(8,128)(2,1)}, u32[]{:S(2)}, u32[]{:S(2)}) collective-permute-start(bf16[2,3,768,768]{3,2,1,0:T(8,128)(2,1)} %get-tuple-element.125), channel_id=1, source_target_pairs={{0,1},{1,0},{2,3},{3,2},{4,5},{5,4},{6,7},{7,6},{8,9},{9,8},{10,11... | collective-permute-start | bytes 21233672 | tf_op jit(solution)/shard_map/ppermute | solution.py:577
  482.6 17.6 %copy-start.7 = (f32[2,64,1]{2,1,0:T(8,128)S(1)}, f32[2,64,1]{2,1,0:T(8,128)}, u32[]{:S(2)}) copy-start(f32[2,64,1]{2,1,0:T(8,128)} %get-tuple-element.118) | copy-start | bytes 1540
  614.4 100.2 %collective-permute-start.6 = (bf16[2,2,768,768]{3,2,1,0:T(8,128)(2,1)}, bf16[2,2,768,768]{3,2,1,0:T(8,128)(2,1)}, u32[]{:S(2)}, u32[]{:S(2)}) collective-permute-start(bf16[2,2,768,768]{3,2,1,0:T(8,128)(2,1)} %get-tuple-element.121), channel_id=1, source_target_pairs={{0,1},{1,0},{2,3},{3,2},{4,5},{5,4},{6,7},{7,6},{8,9},{9,8},{10,11... | collective-permute-start | bytes 14155784 | tf_op jit(solution)/shard_map/ppermute | solution.py:577
  678.5 53.1 %collective-permute-start.8 = (bf16[2,1,768,768]{3,2,1,0:T(8,128)(2,1)}, bf16[2,1,768,768]{3,2,1,0:T(8,128)(2,1)}, u32[]{:S(2)}, u32[]{:S(2)}) collective-permute-start(bf16[2,1,768,768]{3,2,1,0:T(8,128)(2,1)} %get-tuple-element.123), channel_id=1, source_target_pairs={{0,1},{1,0},{2,3},{3,2},{4,5},{5,4},{6,7},{7,6},{8,9},{9,8},{10,11... | collective-permute-start | bytes 7077896 | tf_op jit(solution)/shard_map/ppermute | solution.py:577
  679.0 14.8 %copy-start.6 = (f32[2,64,1]{2,1,0:T(8,128)S(1)}, f32[2,64,1]{2,1,0:T(8,128)}, u32[]{:S(2)}) copy-start(f32[2,64,1]{2,1,0:T(8,128)} %get-tuple-element.113) | copy-start | bytes 1540
  679.0 14.8 %copy-start.8 = (f32[2,64,1]{2,1,0:T(8,128)S(1)}, f32[2,64,1]{2,1,0:T(8,128)}, u32[]{:S(2)}) copy-start(f32[2,64,1]{2,1,0:T(8,128)} %get-tuple-element.114) | copy-start | bytes 1540
  679.0 15.0 %copy-start.10 = (f32[2,2,2,1,448]{4,3,2,1,0:T(1,128)S(1)}, f32[2,2,2,1,448]{4,3,2,1,0:T(1,128)}, u32[]{:S(2)}) copy-start(f32[2,2,2,1,448]{4,3,2,1,0:T(1,128)} %get-tuple-element.115) | copy-start | bytes 43012
  679.0 15.0 %copy-start.13 = (f32[2,2,1,1,448]{4,3,2,1,0:T(1,128)S(1)}, f32[2,2,1,1,448]{4,3,2,1,0:T(1,128)}, u32[]{:S(2)}) copy-start(f32[2,2,1,1,448]{4,3,2,1,0:T(1,128)} %get-tuple-element.116) | copy-start | bytes 21508
  695.6 26.0 %all-to-all-start.4 = ((f32[4,2,10880]{2,1,0:T(2,128)}), f32[4,2,10880]{2,1,0:T(2,128)S(1)}, u32[]{:S(2)}, u32[]{:S(2)}) async-start(f32[4,2,10880]{2,1,0:T(2,128)} %broadcast_in_dim.56), calls=%async_computation.4 | async-start | bytes 696320 | tf_op jit(solution)/shard_map/all_to_all | solution.py:505
  712.6 194.2 %collective-permute-start.11 = (bf16[3,768,768]{2,1,0:T(8,128)(2,1)}, bf16[3,768,768]{2,1,0:T(8,128)(2,1)}, u32[]{:S(2)}, u32[]{:S(2)}) collective-permute-start(bf16[3,768,768]{2,1,0:T(8,128)(2,1)} %slice_bitcast_fusion), channel_id=1, source_target_pairs={{0,2},{1,3},{2,0},{3,1},{4,6},{5,7},{6,4},{7,5},{8,10},{9,11},{10,... | collective-permute-start | bytes 10616840 | tf_op jit(solution)/shard_map/ppermute | solution.py:578
  721.6 104.4 %all-to-all-start.3 = ((bf16[4,2,256,768]{3,2,1,0:T(8,128)(2,1)}), bf16[4,2,256,768]{3,2,1,0:T(8,128)(2,1)}, u32[]{:S(2)}, u32[]{:S(2)}) async-start(bf16[4,2,256,768]{3,2,1,0:T(8,128)(2,1)} %get-tuple-element.110), calls=%async_computation.3 | async-start | bytes 6291456 | tf_op jit(solution)/shard_map/all_to_all | solution.py:505
  726.3 5.4 copy-start.4
  729.7 173.8 %collective-permute-start.7 = (bf16[2,768,768]{2,1,0:T(8,128)(2,1)}, bf16[2,768,768]{2,1,0:T(8,128)(2,1)}, u32[]{:S(2)}, u32[]{:S(2)}) collective-permute-start(bf16[2,768,768]{2,1,0:T(8,128)(2,1)} %slice_bitcast_fusion.2), channel_id=1, source_target_pairs={{0,2},{1,3},{2,0},{3,1},{4,6},{5,7},{6,4},{7,5},{8,10},{9,11},{10,... | collective-permute-start | bytes 7077896 | tf_op jit(solution)/shard_map/ppermute | solution.py:578
  734.0 1.4 copy-start.2
  736.5 164.9 %collective-permute-start.9 = (bf16[1,768,768]{2,1,0:T(8,128)(2,1)}, bf16[1,768,768]{2,1,0:T(8,128)(2,1)}, u32[]{:S(2)}, u32[]{:S(2)}) collective-permute-start(bf16[1,768,768]{2,1,0:T(8,128)(2,1)} %slice_bitcast_fusion.6), channel_id=1, source_target_pairs={{0,2},{1,3},{2,0},{3,1},{4,6},{5,7},{6,4},{7,5},{8,10},{9,11},{10,... | collective-permute-start | bytes 3538952 | tf_op jit(solution)/shard_map/ppermute | solution.py:578
  901.4 5.5 slice-start
  903.4 3.4 slice-start.1
  910.0 1.8 copy-start.18
  915.8 7.5 copy-start.1

commit v4 on v3

--- a/solution.py
+++ b/solution.py
@@ -13,12 +13,11 @@
 GELU_A = 0.044715
 F32 = jnp.float32
 BF16 = jnp.bfloat16
-CHUNK = 256
+CHUNK = 512
 VMEM = 63 * 1024 * 1024
-SPLIT = 4
+SPLIT = 2
 SQ = pl.squeezed
 FULL = ...
-SMALL_FIRST = False
 
 
 def dot_nn(a, b):
@@ -291,7 +290,7 @@
             gt_ref = take(0)
         dbr_ref = take(0)
     sum_ref = take(0)
-    grad = g_ref[FULL].astype(F32).T if token_g else g_ref[FULL].astype(F32)
+    grad = from_tokens(g_ref) if token_g else g_ref[FULL].astype(F32)
     parts = []
     if n_exit:
         d_h = dh_refs[0][FULL]
@@ -306,7 +305,9 @@
         d_x = inv * (d_hat - jnp.mean(d_hat, axis=0, keepdims=True) - hat * jnp.mean(d_hat * hat, axis=0, keepdims=True))
         grad = grad + d_x
         if token_out:
-            gx_ref[FULL] = grad.T.astype(BF16)
+            s_t = gx_ref.shape[1]
+            for t in range(gx_ref.shape[0]):
+                gx_ref[t] = grad[:, t * s_t:(t + 1) * s_t].T.astype(BF16)
         else:
             gx_ref[FULL] = grad.astype(BF16)
             grad = grad.astype(BF16).astype(F32)
@@ -337,11 +338,11 @@
     if token_g:
         n_t, n_b, s_t, dim = grad.shape
     else:
-        n_t, (n_b, dim, s_t) = SPLIT, grad.shape
+        n_t, (n_b, dim, s_t) = token_out or SPLIT, grad.shape
         s_t = s_t // n_t
-    act = pl.BlockSpec((SQ, dim, s_t), lambda b, t: (b, 0, t))
+    act = pl.BlockSpec((SQ, dim, n_t * s_t // SPLIT), lambda b, t: (b, 0, t))
     rows = pl.BlockSpec((SQ, 8, dim), lambda b, t: (b, 0, 0))
-    tok = pl.BlockSpec((SQ, SQ, s_t, dim), lambda b, t: (t, b, 0, 0))
+    tok = pl.BlockSpec((n_t // SPLIT, SQ, s_t, dim), lambda b, t: (t, b, 0, 0))
     shape_act = shape_of(BF16, n_b, dim, n_t * s_t)
     args, in_specs, out_specs, out_shape = [grad], [tok if token_g else act], [], []
     if exit_args:
@@ -357,7 +358,7 @@
         out_shape += [shape_act] * (1 + token_g)
     return pl.pallas_call(
         functools.partial(edge_kernel, len(exit_args[2]) if exit_args else 0, bool(entry_args), token_g, token_out),
-        grid=(n_b, n_t), in_specs=in_specs, out_specs=out_specs + [rows], out_shape=out_shape + [shape_of(F32, n_b, 8, dim)],
+        grid=(n_b, SPLIT), in_specs=in_specs, out_specs=out_specs + [rows], out_shape=out_shape + [shape_of(F32, n_b, 8, dim)],
         compiler_params=params(2),
         cost_estimate=pl.CostEstimate(flops=10 ** 6, bytes_accessed=10 ** 7, transcendentals=0),
         name="edge",
@@ -518,8 +519,6 @@
         b_perm = jnp.einsum("ec,lhc->lhe", perm_mat, b_in, preferred_element_type=F32)
         small_in = jnp.concatenate([rope_cos.T.reshape(-1), rope_sin.T.reshape(-1), b_perm.reshape(-1)])
         small_all = lax.all_gather(small_in, "tp", axis=0, tiled=False)
-        small_all, x_in, w_in, w_out = lax.optimization_barrier((small_all, x_in, w_in, w_out))
-
         tie = swap(x_in.reshape(n_tp, n_b, s_own, dim))
         w_local = []
         for l in range(n_l):
@@ -562,7 +561,7 @@
 
         grads, small = [None] * n_l, [None] * n_l
         top = n_l - 1
-        g_t, d_br, sums_in = edge(g_tok, (), (mod_rows[top], saved[top][5]), True, False)
+        g_t, d_br, sums_in = edge(g_tok, (), (mod_rows[top], saved[top][5]), True, 0)
         d_gate, d_bias = sums_in[:, 0], sums_in[:, 1]
         for l in reversed(range(n_l)):
             x_t, y, o, lse, h_t, branch = saved[l]
@@ -574,11 +573,12 @@
                 d_hs.append(dh_j)
                 d_qk = d_qk + dqk_j
                 gb.append(gb_j)
-                chip_sum = (keep.astype(F32) + lax.ppermute(send, "tp", peer_core).astype(F32)).astype(BF16)
-                from_chip = lax.ppermute(chip_sum[1], "tp", across)
-                gw.append((chip_sum[0].astype(F32) + from_chip.astype(F32)).astype(BF16))
+                near = lax.ppermute(send, "tp", peer_core)
+                leaving = (keep[1].astype(F32) + near[1].astype(F32)).astype(BF16)
+                far = lax.ppermute(leaving, "tp", across)
+                gw.append((keep[0].astype(F32) + near[0].astype(F32) + far.astype(F32)).astype(BF16))
             entry = (mod_rows[l - 1], saved[l - 1][5]) if l > 0 else ()
-            edge_out = edge(g_t, (x_t, mod_rows[l], d_hs), entry, False, l == 0)
+            edge_out = edge(g_t, (x_t, mod_rows[l], d_hs), entry, False, n_tp * (l == 0))
             g_t, sums = edge_out[0], edge_out[-1]
             grads[l] = jnp.concatenate(gw)
             d_mod = jnp.stack([sums[:, 0], sums[:, 1], d_gate], axis=1)
@@ -590,7 +590,6 @@
                 d_gate, d_bias = sums[:, 2], sums[:, 3]
 
         gathered = swap(jnp.broadcast_to(jnp.stack(small), (n_tp, n_l, small[0].shape[0])))
-        g_t, gathered = lax.optimization_barrier((g_t, gathered)) if SMALL_FIRST else (g_t, gathered)
         grad_x = swap(g_t)
         n_mod = n_b * 3 * dim
         d_mod = jnp.moveaxis(gathered[:, :, :n_mod].reshape(n_tp, n_l, n_b, 3 * dim), 1, 0).reshape(n_l, n_all, 3 * dim)

time: 928 us -> 908 us (0.978)
  blocking collectives: 7.82 us -> 39.7 us
  waiting for transfers between devices: 211 us -> 190 us
  Pallas kernels: 587 us -> 567 us
  local copies, waits for them, and re-layouts: 34.7 us -> 23.6 us
    all_gather x1, blocking collectives: 7.82 us -> 39.7 us  [device_step(): small_all = lax.all_gather(small_in, 'tp', axis=0, tiled=False)]
    all_to_all x5, waiting for transfers between devices: 110 us -> 85.2 us  [swap(): return lax.all_to_all(arr, 'tp', 0, 0)]
  transfers between devices with their start and end apart: 17 -> 17, of which waited for: 6 -> 5; matrix products, arithmetic and copies ran while one was open for 6% -> 5% of each run, Pallas kernels for 64% -> 63%
where the time goes in v4:
time: 908 us; the launch traced here: 898 us
  Pallas kernels  567 us (62%)
  waiting for transfers between devices  190 us (21%)
  blocking collectives  39.7 us (4%)
  other arithmetic  34.6 us (4%)
  starting transfers between devices  29.4 us (3%)
  local copies, waits for them, and re-layouts  23.6 us (3%)
  matrix products  12.3 us (1%)
    pallas_call x3, Pallas kernels, block_backward(): pl.pallas_call(functools.partial(bwd_kernel, e), grid=(n + 1,), in_specs=...  335 us
    pallas_call x4, Pallas kernels, block_forward(): pl.pallas_call(functools.partial(fwd_kernel, e, first, last, token_in, to...  191 us
    all_to_all x5, waiting for transfers between devices, swap(): return lax.all_to_all(arr, 'tp', 0, 0)  85.2 us
    ppermute x3, waiting for transfers between devices, device_step(): far = lax.ppermute(leaving, 'tp', across)  75.3 us
    all_gather x1, blocking collectives, device_step(): small_all = lax.all_gather(small_in, 'tp', axis=0, tiled=False)  39.7 us
    pallas_call x3, Pallas kernels, edge(): pl.pallas_call(functools.partial(edge_kernel, len(exit_args[2]) if exit_a...  33.3 us
    ppermute x2, waiting for transfers between devices, device_step(): got = lax.ppermute(mine, 'tp', across)  26.9 us
    all_to_all x5, starting transfers between devices, swap(): return lax.all_to_all(arr, 'tp', 0, 0)  22.6 us
  transfers between devices with their start and end apart: 17, of which 5 were waited for; matrix products, arithmetic and copies ran while one was open for 5% of the time, Pallas kernels for 63%

profile of v4, /device:TPU:0, one launch (start us, length us, event | category | flops | bytes accessed | tf_op | source)
XLA Modules:
  0.0 897.9 jit_solution(1923707350645302842)
XLA Ops:
  0.7 3.3 slice_bitcast_fusion
  4.1 1.2 convert_bitcast_fusion.1
  5.3 2.0 pad_maximum_fusion.1.refs_1_.wa0_ref
  7.3 0.7 collective-permute-start.1
  8.1 4.8 all-to-all-start
  13.3 39.7 %all-gather.1 = f32[4,1,19072]{2,1,0:T(1,128)S(1)} all-gather(f32[1,1,19072]{2,1,0:T(1,128)S(1)} %reshape.235), channel_id=2, replica_groups=mesh['dp'=4,'tp'=4] {'tp'}, dimensions={0}, use_global_device_ids=true | all-gather | bytes 381440 | tf_op jit(solution)/shard_map/all_gather | solution.py:521
  53.3 4.0 fusion.7
  61.5 48.1 %block_fwd.4 = (f32[2,2,2,3,448,1024]{5,4,3,2,1,0:T(8,128)}, bf16[2,2,2,3,64,1024]{5,4,3,2,1,0:T(8,128)(2,1)}, f32[2,2,3,2,1024]{4,3,2,1,0:T(2,128)}, bf16[2,768...) custom-call(f32[2,8,768]{2,1,0:T(8,128)} %get-tuple-element.123.refs_0_.refs_4_.refs_2_, ...), custom_call_target="tpu_custom_call" | custom-call | flops 27380416512 | bytes 10000000 | tf_op jit(solution)/shard_map/block_fwd/pallas_call | solution.py:429
  109.6 26.9 %collective-permute-done.refs_1_.wa1_ref = bf16[3,768,768]{2,1,0:T(8,128)(2,1)} collective-permute-done((bf16[3,768,768]{2,1,0:T(8,128)(2,1)}, bf16[3,768,768]{2,1,0:T(8,128)(2,1)}, u32[]{:S(2)}, u32[]{:S(2)}) %collective-permute-start) | collective-permute-done | bytes 3538976 | tf_op jit(solution)/shard_map/ppermute | solution.py:549
  136.4 2.8 convert_bitcast_fusion.2
  139.3 2.0 pad_maximum_fusion.refs_1_.wa0_ref
  142.2 0.8 collective-permute-done.4.refs_2_.wb1_ref
  143.7 47.8 %block_fwd.5 = (f32[2,2,2,3,448,1024]{5,4,3,2,1,0:T(8,128)}, bf16[2,2,2,3,64,1024]{5,4,3,2,1,0:T(8,128)(2,1)}, f32[2,2,3,2,1024]{4,3,2,1,0:T(2,128)}, f32[2,768,1024]{2,1,0:T(8,128)}, bf16[2,768,1024]{2,1,0:T(8,128)(2,1)}) custom-call(f32[2,8,768]{2,1,0:T(8,128)} %get-tuple-element.123.refs_0_.refs_4_.r, ...), custom_call_target="tpu_custom_call", output_to_operand_aliasing={{0}: (10, {}), {1}: (11, {}), {2}: (12, {})} | custom-call | flops 27380416512 | bytes 10000000 | tf_op jit(solution)/shard_map/block_fwd/pallas_call | solution.py:429
  192.7 47.6 %block_fwd.6 = (f32[2,2,2,3,448,1024]{5,4,3,2,1,0:T(8,128)}, bf16[2,2,2,3,64,1024]{5,4,3,2,1,0:T(8,128)(2,1)}, f32[2,2,3,2,1024]{4,3,2,1,0:T(2,128)}, bf16[2,768,1024]{2,1,0:T(8,128)(2,1)}, f32[2,768,1024]{2,1,0:T(8,128)}) custom-call(f32[2,8,768]{2,1,0:T(8,128)} %get-tuple-element.122.refs_0_.refs_1_.refs_2_, ...), custom_call_target="tpu_custom_call" | custom-call | flops 27380416512 | bytes 10000000 | tf_op jit(solution)/shard_map/block_fwd/pallas_call | solution.py:429
  240.5 5.1 all-to-all-start.1
  245.6 1.3 collective-permute-done.5.refs_2_.wb1_ref
  247.5 47.9 %block_fwd.7 = (f32[2,2,2,3,448,1024]{5,4,3,2,1,0:T(8,128)}, bf16[2,2,2,3,64,1024]{5,4,3,2,1,0:T(8,128)(2,1)}, f32[2,2,3,2,1024]{4,3,2,1,0:T(2,128)}, f32[2,768,1024]{2,1,0:T(8,128)}, bf16[4,2,256,768]{3,2,1,0:T(8,128)(2,1)}) custom-call(f32[2,8,768]{2,1,0:T(8,128)} %get-tuple-element.122.refs_0_.refs_1, ...), custom_call_target="tpu_custom_call", output_to_operand_aliasing={{0}: (10, {}), {1}: (11, {}), {2}: (12, {})} | custom-call | flops 27380416512 | bytes 10000000 | tf_op jit(solution)/shard_map/block_fwd/pallas_call | solution.py:429
  295.5 4.7 all-to-all-start.2
  300.2 8.4 edge.3
  308.6 160.0 %block_bwd.3 = (bf16[2,3,768,768]{3,2,1,0:T(8,128)(2,1)}, bf16[2,3,768,768]{3,2,1,0:T(8,128)(2,1)}, f32[2,2,3,1,448]{4,3,2,1,0:T(1,128)}, f32[2,64,1]{2,1,0:T(8,128)}, f32[2,768,1024]{2,1,0:T(8,128)}) custom-call(bf16[2,768,1024]{2,1,0:T(8,128)(2,1)} %get-tuple-element.86.dbr_ref, bf16[2,768,1024]{2,1,0:T(8,128)(2,1)} %get-tuple-element.79.refs_8_.h_ref, ...), custom_call_target="tpu_custom_call" | custom-call | flops 122406567936 | bytes 10000000 | tf_op jit(solution)/shard_map/block_bwd/pallas_call | solution.py:454
  469.1 0.8 reduce.6
  470.0 12.8 %edge.4 = (bf16[2,768,1024]{2,1,0:T(8,128)(2,1)}, bf16[2,768,1024]{2,1,0:T(8,128)(2,1)}, f32[2,8,768]{2,1,0:T(8,128)}) custom-call(bf16[2,768,1024]{2,1,0:T(8,128)(2,1)} %get-tuple-element.85.refs_0_, bf16[2,768,1024]{2,1,0:T(8,128)(2,1)} %get-tuple-element.75.refs_7_.refs_1_, f32[2,8,768]{2,1,0:T(8,128)} %get-tuple-element.122.refs_0_.refs_1_.refs_2_, ...), custom_call_target="tpu_custom_call" | custom-call | flops 1000000 | bytes 10000000 | tf_op jit(solution)/shard_map/edge/pallas_call | solution.py:359
  482.8 0.8 slice.186
  483.6 0.9 fusion.37
  484.8 0.9 fusion.36
  485.7 111.5 %block_bwd.4 = (bf16[2,2,768,768]{3,2,1,0:T(8,128)(2,1)}, bf16[2,2,768,768]{3,2,1,0:T(8,128)(2,1)}, f32[2,2,2,1,448]{4,3,2,1,0:T(1,128)}, f32[2,64,1]{2,1,0:T(8,128)}, f32[2,768,1024]{2,1,0:T(8,128)}) custom-call(bf16[2,768,1024]{2,1,0:T(8,128)(2,1)} %get-tuple-element.96.dbr_ref, bf16[2,768,1024]{2,1,0:T(8,128)(2,1)} %get-tuple-element.70.refs_8_.h_ref, ...), custom_call_target="tpu_custom_call" | custom-call | flops 81604378624 | bytes 10000000 | tf_op jit(solution)/shard_map/block_bwd/pallas_call | solution.py:454
  597.3 63.0 %block_bwd.5 = (bf16[2,1,768,768]{3,2,1,0:T(8,128)(2,1)}, bf16[2,1,768,768]{3,2,1,0:T(8,128)(2,1)}, f32[2,2,1,1,448]{4,3,2,1,0:T(1,128)}, f32[2,64,1]{2,1,0:T(8,128)}, f32[2,768,1024]{2,1,0:T(8,128)}) custom-call(bf16[2,768,1024]{2,1,0:T(8,128)(2,1)} %get-tuple-element.96.dbr_ref, bf16[2,768,1024]{2,1,0:T(8,128)(2,1)} %get-tuple-element.70.refs_8_.h_ref, ...), custom_call_target="tpu_custom_call" | custom-call | flops 40802189312 | bytes 10000000 | tf_op jit(solution)/shard_map/block_bwd/pallas_call | solution.py:454
  660.8 12.1 %edge.5 = (bf16[4,2,256,768]{3,2,1,0:T(8,128)(2,1)}, f32[2,8,768]{2,1,0:T(8,128)}) custom-call(bf16[2,768,1024]{2,1,0:T(8,128)(2,1)} %get-tuple-element.95.refs_0_, bf16[2,768,1024]{2,1,0:T(8,128)(2,1)} %get-tuple-element.69.refs_7_.refs_1_, f32[2,8,768]{2,1,0:T(8,128)} %get-tuple-element.123.refs_0_.refs_4_.refs_2_, ...), custom_call_target="tpu_custom_call" | custom-call | flops 1000000 | bytes 10000000 | tf_op jit(solution)/shard_map/edge/pallas_call | solution.py:359
  672.9 0.8 slice.183
  674.7 0.8 broadcast_in_dim.56
  675.5 3.5 all-to-all-start.4
  679.0 5.7 fusion.5
  684.6 2.0 collective-permute-start.11
  686.6 4.7 all-to-all-start.3
  691.3 4.5 fusion.10
  695.8 2.0 collective-permute-start.7
  697.7 2.6 fusion.22
  702.2 0.8 reshape.227.d_ref
  703.3 7.7 wmod_grad.1
  712.9 85.2 %all-to-all-done.3 = bf16[4,2,256,768]{3,2,1,0:T(8,128)(2,1)} async-done(((bf16[4,2,256,768]{3,2,1,0:T(8,128)(2,1)}), bf16[4,2,256,768]{3,2,1,0:T(8,128)(2,1)}, u32[]{:S(2)}, u32[]{:S(2)}) %all-to-all-start.3) | async-done | bytes 3145760 | tf_op jit(solution)/shard_map/all_to_all | solution.py:506
  798.0 75.3 %collective-permute-done.9 = bf16[1,768,768]{2,1,0:T(8,128)(2,1)} collective-permute-done((bf16[1,768,768]{2,1,0:T(8,128)(2,1)}, bf16[1,768,768]{2,1,0:T(8,128)(2,1)}, u32[]{:S(2)}, u32[]{:S(2)}) %collective-permute-start.9) | collective-permute-done | bytes 1179680 | tf_op jit(solution)/shard_map/ppermute | solution.py:578
  873.4 2.6 fusion.11
  876.0 4.1 fusion.1
  880.4 3.8 fusion.6
  884.2 1.8 pad_maximum_fusion.2
  886.0 4.0 convert_bitcast_fusion
  890.0 3.8 copy.90
  893.8 3.8 copy.91
  (147 shorter events, 15.0 us)
Async XLA Ops:
  0.6 12.3 %copy-start = (bf16[2,3,448]{2,0,1:T(2,128)(2,1)S(1)}, bf16[2,3,448]{2,0,1:T(2,128)(2,1)}, u32[]{:S(2)}) copy-start(bf16[2,3,448]{2,0,1:T(2,128)(2,1)} %param.21) | copy-start | bytes 16132
  0.7 3.3 copy-start.4
  0.7 3.4 copy-start.18
  7.3 5.5 copy-start.9
  7.3 5.5 copy-start.10
  7.3 52.9 %collective-permute-start.1 = (bf16[3,768,768]{2,1,0:T(8,128)(2,1)}, bf16[3,768,768]{2,1,0:T(8,128)(2,1)}, u32[]{:S(2)}, u32[]{:S(2)}) collective-permute-start(bf16[3,768,768]{2,1,0:T(8,128)(2,1)} %pad_maximum_fusion.1.refs_1_.wa0_ref), channel_id=1, source_target_pairs={{0,1},{1,0},{2,3},{3,2},{4,5},{5,4},{6,7},{7,6},{8,9},{9,8},{10,11... | collective-permute-start | bytes 10616840 | tf_op jit(solution)/shard_map/ppermute | solution.py:527
  8.1 45.1 %copy-start.13 = (bf16[2,2304]{1,0:T(2,128)(2,1)S(1)}, bf16[2,2304]{1,0:T(2,128)(2,1)}, u32[]{:S(2)}) copy-start(bf16[2,2304]{1,0:T(2,128)(2,1)} %param.19) | copy-start | bytes 27652
  8.1 45.1 %copy-start.12 = (bf16[8,768]{1,0:T(8,128)(2,1)S(1)}, bf16[8,768]{1,0:T(8,128)(2,1)}, u32[]{:S(2)}) copy-start(bf16[8,768]{1,0:T(8,128)(2,1)} %param.15) | copy-start | bytes 36868
  8.1 49.2 %all-to-all-start = ((bf16[4,2,256,768]{3,2,1,0:T(8,128)(2,1)}), bf16[4,2,256,768]{3,2,1,0:T(8,128)(2,1)}, u32[]{:S(2)}, u32[]{:S(2)}) async-start(bf16[4,2,256,768]{3,2,1,0:T(8,128)(2,1)} %bitcast.7), calls=%async_computation | async-start | bytes 6291456 | tf_op jit(solution)/shard_map/all_to_all | solution.py:506
  53.2 4.1 copy-start.8
  53.2 5.7 copy-start.16
  53.2 5.9 copy-start.17
  53.2 6.3 copy-start.15
  57.3 79.1 %collective-permute-start = (bf16[3,768,768]{2,1,0:T(8,128)(2,1)}, bf16[3,768,768]{2,1,0:T(8,128)(2,1)}, u32[]{:S(2)}, u32[]{:S(2)}) collective-permute-start(bf16[3,768,768]{2,1,0:T(8,128)(2,1)} %pad_maximum_fusion.1.refs_1_.wa0_ref), channel_id=1, source_target_pairs={{0,2},{1,3},{2,0},{3,1},{4,6},{5,7},{6,4},{7,5},{8,10},{9,11},{10,... | collective-permute-start | bytes 10616840 | tf_op jit(solution)/shard_map/ppermute | solution.py:549
  109.5 29.7 %copy-start.2 = (bf16[3,320,768]{2,1,0:T(8,128)(2,1)S(1)}, bf16[3,320,768]{2,1,0:T(8,128)(2,1)}, u32[]{:S(2)}) copy-start(bf16[3,320,768]{2,1,0:T(8,128)(2,1)} %get-tuple-element.119) | copy-start | bytes 4423684
  136.4 6.6 collective-permute-start.4
  141.3 50.1 %collective-permute-start.3 = (bf16[3,768,768]{2,1,0:T(8,128)(2,1)}, bf16[3,768,768]{2,1,0:T(8,128)(2,1)}, u32[]{:S(2)}, u32[]{:S(2)}) collective-permute-start(bf16[3,768,768]{2,1,0:T(8,128)(2,1)} %pad_maximum_fusion.refs_1_.wa0_ref), channel_id=1, source_target_pairs={{0,1},{1,0},{2,3},{3,2},{4,5},{5,4},{6,7},{7,6},{8,9},{9,8},{10,11... | collective-permute-start | bytes 10616840 | tf_op jit(solution)/shard_map/ppermute | solution.py:527
  141.9 98.4 %collective-permute-start.2 = (bf16[3,768,768]{2,1,0:T(8,128)(2,1)}, bf16[3,768,768]{2,1,0:T(8,128)(2,1)}, u32[]{:S(2)}, u32[]{:S(2)}) collective-permute-start(bf16[3,768,768]{2,1,0:T(8,128)(2,1)} %pad_maximum_fusion.refs_1_.wa0_ref), channel_id=1, source_target_pairs={{0,2},{1,3},{2,0},{3,1},{4,6},{5,7},{6,4},{7,5},{8,10},{9,11},{10,... | collective-permute-start | bytes 10616840 | tf_op jit(solution)/shard_map/ppermute | solution.py:549
  240.3 6.6 collective-permute-start.5
  240.5 55.0 %all-to-all-start.1 = ((bf16[4,2,256,768]{3,2,1,0:T(8,128)(2,1)}), bf16[4,2,256,768]{3,2,1,0:T(8,128)(2,1)}, u32[]{:S(2)}, u32[]{:S(2)}) async-start(bf16[4,2,256,768]{3,2,1,0:T(8,128)(2,1)} %bitcast.139), calls=%async_computation.1 | async-start | bytes 6291456 | tf_op jit(solution)/shard_map/all_to_all | solution.py:506
  295.5 190.2 %all-to-all-start.2 = ((bf16[4,2,256,768]{3,2,1,0:T(8,128)(2,1)}), bf16[4,2,256,768]{3,2,1,0:T(8,128)(2,1)}, u32[]{:S(2)}, u32[]{:S(2)}) async-start(bf16[4,2,256,768]{3,2,1,0:T(8,128)(2,1)} %get-tuple-element.93), calls=%async_computation.2 | async-start | bytes 6291456 | tf_op jit(solution)/shard_map/all_to_all | solution.py:506
  468.6 210.3 %collective-permute-start.10 = (bf16[2,3,768,768]{3,2,1,0:T(8,128)(2,1)}, bf16[2,3,768,768]{3,2,1,0:T(8,128)(2,1)}, u32[]{:S(2)}, u32[]{:S(2)}) collective-permute-start(bf16[2,3,768,768]{3,2,1,0:T(8,128)(2,1)} %get-tuple-element.117), channel_id=1, source_target_pairs={{0,1},{1,0},{2,3},{3,2},{4,5},{5,4},{6,7},{7,6},{8,9},{9,8},{10,11... | collective-permute-start | bytes 21233672 | tf_op jit(solution)/shard_map/ppermute | solution.py:576
  470.0 14.6 %copy-start.6 = (f32[2,64,1]{2,1,0:T(8,128)S(1)}, f32[2,64,1]{2,1,0:T(8,128)}, u32[]{:S(2)}) copy-start(f32[2,64,1]{2,1,0:T(8,128)} %get-tuple-element.110) | copy-start | bytes 1540
  597.2 94.0 %collective-permute-start.6 = (bf16[2,2,768,768]{3,2,1,0:T(8,128)(2,1)}, bf16[2,2,768,768]{3,2,1,0:T(8,128)(2,1)}, u32[]{:S(2)}, u32[]{:S(2)}) collective-permute-start(bf16[2,2,768,768]{3,2,1,0:T(8,128)(2,1)} %get-tuple-element.113), channel_id=1, source_target_pairs={{0,1},{1,0},{2,3},{3,2},{4,5},{5,4},{6,7},{7,6},{8,9},{9,8},{10,11... | collective-permute-start | bytes 14155784 | tf_op jit(solution)/shard_map/ppermute | solution.py:576
  660.4 37.4 %collective-permute-start.8 = (bf16[2,1,768,768]{3,2,1,0:T(8,128)(2,1)}, bf16[2,1,768,768]{3,2,1,0:T(8,128)(2,1)}, u32[]{:S(2)}, u32[]{:S(2)}) collective-permute-start(bf16[2,1,768,768]{3,2,1,0:T(8,128)(2,1)} %get-tuple-element.115), channel_id=1, source_target_pairs={{0,1},{1,0},{2,3},{3,2},{4,5},{5,4},{6,7},{7,6},{8,9},{9,8},{10,11... | collective-permute-start | bytes 7077896 | tf_op jit(solution)/shard_map/ppermute | solution.py:576
  660.8 13.0 %copy-start.5 = (f32[2,64,1]{2,1,0:T(8,128)S(1)}, f32[2,64,1]{2,1,0:T(8,128)}, u32[]{:S(2)}) copy-start(f32[2,64,1]{2,1,0:T(8,128)} %get-tuple-element.105) | copy-start | bytes 1540
  660.8 13.0 %copy-start.7 = (f32[2,64,1]{2,1,0:T(8,128)S(1)}, f32[2,64,1]{2,1,0:T(8,128)}, u32[]{:S(2)}) copy-start(f32[2,64,1]{2,1,0:T(8,128)} %get-tuple-element.106) | copy-start | bytes 1540
  660.8 13.2 %copy-start.11 = (f32[2,2,2,1,448]{4,3,2,1,0:T(1,128)S(1)}, f32[2,2,2,1,448]{4,3,2,1,0:T(1,128)}, u32[]{:S(2)}) copy-start(f32[2,2,2,1,448]{4,3,2,1,0:T(1,128)} %get-tuple-element.107) | copy-start | bytes 43012
  660.8 13.2 %copy-start.14 = (f32[2,2,1,1,448]{4,3,2,1,0:T(1,128)S(1)}, f32[2,2,1,1,448]{4,3,2,1,0:T(1,128)}, u32[]{:S(2)}) copy-start(f32[2,2,1,1,448]{4,3,2,1,0:T(1,128)} %get-tuple-element.108) | copy-start | bytes 21508
  675.5 11.1 %all-to-all-start.4 = ((f32[4,2,10880]{2,1,0:T(2,128)}), f32[4,2,10880]{2,1,0:T(2,128)S(1)}, u32[]{:S(2)}, u32[]{:S(2)}) async-start(f32[4,2,10880]{2,1,0:T(2,128)} %broadcast_in_dim.56), calls=%async_computation.4 | async-start | bytes 696320 | tf_op jit(solution)/shard_map/all_to_all | solution.py:506
  684.6 195.7 %collective-permute-start.11 = (bf16[3,768,768]{2,1,0:T(8,128)(2,1)}, bf16[3,768,768]{2,1,0:T(8,128)(2,1)}, u32[]{:S(2)}, u32[]{:S(2)}) collective-permute-start(bf16[3,768,768]{2,1,0:T(8,128)(2,1)} %fusion.5), channel_id=1, source_target_pairs={{0,2},{1,3},{2,0},{3,1},{4,6},{5,7},{6,4},{7,5},{8,10},{9,11},{10,... | collective-permute-start | bytes 10616840 | tf_op jit(solution)/shard_map/ppermute | solution.py:578
  686.6 111.4 %all-to-all-start.3 = ((bf16[4,2,256,768]{3,2,1,0:T(8,128)(2,1)}), bf16[4,2,256,768]{3,2,1,0:T(8,128)(2,1)}, u32[]{:S(2)}, u32[]{:S(2)}) async-start(bf16[4,2,256,768]{3,2,1,0:T(8,128)(2,1)} %get-tuple-element.102), calls=%async_computation.3 | async-start | bytes 6291456 | tf_op jit(solution)/shard_map/all_to_all | solution.py:506
  691.3 6.5 copy-start.3
  695.8 180.2 %collective-permute-start.7 = (bf16[2,768,768]{2,1,0:T(8,128)(2,1)}, bf16[2,768,768]{2,1,0:T(8,128)(2,1)}, u32[]{:S(2)}, u32[]{:S(2)}) collective-permute-start(bf16[2,768,768]{2,1,0:T(8,128)(2,1)} %fusion.10), channel_id=1, source_target_pairs={{0,2},{1,3},{2,0},{3,1},{4,6},{5,7},{6,4},{7,5},{8,10},{9,11},{10,... | collective-permute-start | bytes 7077896 | tf_op jit(solution)/shard_map/ppermute | solution.py:578
  700.4 173.0 %collective-permute-start.9 = (bf16[1,768,768]{2,1,0:T(8,128)(2,1)}, bf16[1,768,768]{2,1,0:T(8,128)(2,1)}, u32[]{:S(2)}, u32[]{:S(2)}) collective-permute-start(bf16[1,768,768]{2,1,0:T(8,128)(2,1)} %fusion.22), channel_id=1, source_target_pairs={{0,2},{1,3},{2,0},{3,1},{4,6},{5,7},{6,4},{7,5},{8,10},{9,11},{10,... | collective-permute-start | bytes 3538952 | tf_op jit(solution)/shard_map/ppermute | solution.py:578
  873.4 7.0 slice-start
  875.9 4.5 slice-start.1
  884.2 1.8 copy-start.19
  890.0 7.5 copy-start.1

commit v5 on v4

--- a/solution.py
+++ b/solution.py
@@ -385,18 +385,18 @@
     )(silu_all, d_mod)
 
 
-def block_forward(slot, x_in, mod_rows, w_pair, b_rows, qk, cos_t, sin_t, prev, token_in, token_out):
-    first, last = slot == 0, slot == 1
+def block_forward(slot, j_lo, last, x_in, mod_rows, w_pair, b_rows, qk, cos_t, sin_t, prev, token_in, token_out):
+    first = slot == 0
     token_in = token_in and first
-    n_j, dim = w_pair[0].shape[:2]
-    n_c = len(w_pair)
+    j_n, dim = w_pair[0].shape[:2]
+    n_c, n_j = b_rows.shape[:2]
     cols = b_rows.shape[-1]
     e = qk.shape[-1]
     s_len = cos_t.shape[1]
     n_b = mod_rows.shape[0]
-    final = n_j - 1
+    final = j_n - 1
     full = lambda *shape: pl.BlockSpec(shape, lambda g, b: (0,) * len(shape))
-    head6 = lambda n, m: pl.BlockSpec((SQ, SQ, n_c, SQ, n, m), lambda g, b: (b, slot, 0, g, 0, 0))
+    head6 = lambda n, m: pl.BlockSpec((SQ, SQ, n_c, SQ, n, m), lambda g, b: (b, slot, 0, j_lo + g, 0, 0))
     act = lambda idx: pl.BlockSpec((SQ, dim, s_len), lambda g, b: (idx(g, b), 0, 0))
     at_start = lambda g, b: jnp.where(g == 0, b, n_b - 1)
     at_end = lambda g, b: jnp.where(g == final, b, 0)
@@ -405,7 +405,7 @@
     args = [mod_rows, *w_pair, b_rows, qk, cos_t, sin_t, x_in]
     in_specs = [
         pl.BlockSpec((SQ, 8, dim), lambda g, b: (b, 0, 0)), weight, weight,
-        pl.BlockSpec((n_c, SQ, 8, cols), lambda g, b: (0, g, 0, 0)),
+        pl.BlockSpec((n_c, SQ, 8, cols), lambda g, b: (0, j_lo + g, 0, 0)),
         full(2, 8, e), full(e // 2, s_len), full(e // 2, s_len),
         tok(x_in.shape[0], at_start) if token_in else act(at_start if first else at_end),
     ]
@@ -415,7 +415,7 @@
         in_specs += [act(at_start), act(at_start)] + [pl.BlockSpec(memory_space=pl.ANY)] * 3
         aliases = {len(args) - 3 + i: i for i in range(3)}
     shape16, shape32 = shape_of(BF16, n_b, dim, s_len), shape_of(F32, n_b, dim, s_len)
-    out_specs = [head6(cols, s_len), head6(e, s_len), pl.BlockSpec((SQ, SQ, SQ, n_c, s_len), lambda g, b: (b, slot, g, 0, 0))]
+    out_specs = [head6(cols, s_len), head6(e, s_len), pl.BlockSpec((SQ, SQ, SQ, n_c, s_len), lambda g, b: (b, slot, j_lo + g, 0, 0))]
     out_shape = [shape_of(F32, n_b, 2, n_c, n_j, cols, s_len), shape_of(BF16, n_b, 2, n_c, n_j, e, s_len), shape_of(F32, n_b, 2, n_j, n_c, s_len)]
     if first:
         out_specs += [act(at_start)] * (1 + token_in)
@@ -425,10 +425,10 @@
     if last:
         out_specs.append(tok(token_out, at_end) if token_out else act(at_end))
         out_shape.append(shape_of(BF16, token_out, n_b, s_len // token_out, dim) if token_out else shape16)
-    heads = n_c * n_j * n_b
+    heads = n_c * j_n * n_b
     return pl.pallas_call(
         functools.partial(fwd_kernel, e, first, last, token_in, token_out),
-        grid=(n_j, n_b), in_specs=in_specs, out_specs=out_specs, out_shape=out_shape,
+        grid=(j_n, n_b), in_specs=in_specs, out_specs=out_specs, out_shape=out_shape,
         input_output_aliases=aliases,
         scratch_shapes=[pltpu.VMEM((n_b, dim, s_len), F32), pltpu.VMEM((n_b, dim, s_len), BF16), pltpu.VMEM((dim, 2 * (dim - cols)), BF16)],
         compiler_params=params(2),
@@ -448,14 +448,18 @@
     once = pl.Buffered(1)
     full = lambda *shape: pl.BlockSpec(shape, lambda s: (0,) * len(shape), pipeline_mode=once)
     head6 = lambda n_r, m: pl.BlockSpec((SQ, SQ, n_c, SQ, n_r, m), lambda s: (jnp.minimum(s, n - 1) % n_b, group(s) % 2, 0, j_lo + group(s) // 2, 0, 0))
-    weight = pl.BlockSpec((SQ, dim, dim), lambda s: (j_lo + group(s) // 2, 0, 0))
+
+    def weight(w):
+        base = 0 if w.shape[0] == j_n else j_lo
+        return pl.BlockSpec((SQ, dim, dim), lambda s: (base + group(s) // 2, 0, 0))
+
     grad = pl.BlockSpec((SQ, SQ, dim, dim), lambda s: (before(s) % 2, before(s) // 2, 0, 0))
     heads = 2 * n_c * j_n * n_b
     return pl.pallas_call(
         functools.partial(bwd_kernel, e),
         grid=(n + 1,),
         in_specs=[
-            full(n_b, dim, s_len), full(n_b, dim, s_len), weight, weight, weight, weight,
+            full(n_b, dim, s_len), full(n_b, dim, s_len), *[weight(w) for w in ws],
             full(2, 8, e), full(e // 2, s_len), full(e // 2, s_len),
             head6(cols, s_len), head6(e, s_len),
             pl.BlockSpec((SQ, SQ, SQ, n_c, s_len), lambda s: (jnp.minimum(s, n - 1) % n_b, group(s) % 2, j_lo + group(s) // 2, 0, 0)),
@@ -518,6 +522,13 @@
         n_rope = e * s_own
         b_perm = jnp.einsum("ec,lhc->lhe", perm_mat, b_in, preferred_element_type=F32)
         small_in = jnp.concatenate([rope_cos.T.reshape(-1), rope_sin.T.reshape(-1), b_perm.reshape(-1)])
+        silu_all = jax.nn.silu(cond_vec.astype(F32)).astype(BF16)
+        silu_own = lax.dynamic_slice_in_dim(silu_all, me * n_b, n_b, 0)
+        mod_sum = jnp.einsum("bd,ldm->lbm", silu_own, w_mod, preferred_element_type=F32)
+        mod = mod_sum + b_mod.astype(F32)[:, None]
+        bias = jnp.broadcast_to(b_out.astype(F32)[:, None, None], (n_l, n_b, 5, dim))
+        mod_rows = jnp.concatenate([mod.reshape(n_l, n_b, 3, dim), bias], axis=2)
+        small_in, mod_rows = lax.optimization_barrier((small_in, mod_rows))
         small_all = lax.all_gather(small_in, "tp", axis=0, tiled=False)
         tie = swap(x_in.reshape(n_tp, n_b, s_own, dim))
         w_local = []
@@ -532,11 +543,6 @@
         b_rel = jnp.stack([lax.dynamic_index_in_dim(b_all, me ^ i, 0, keepdims=False) for i in range(n_tp)])
         b_rel = jnp.broadcast_to(b_rel, (n_tp, n_l, n_j, 8, cols))
 
-        silu_all = jax.nn.silu(cond_vec.astype(F32)).astype(BF16)
-        silu_own = lax.dynamic_slice_in_dim(silu_all, me * n_b, n_b, 0)
-        mod = jnp.einsum("bd,ldm->lbm", silu_own, w_mod, preferred_element_type=F32) + b_mod.astype(F32)[:, None]
-        bias = jnp.broadcast_to(b_out.astype(F32)[:, None, None], (n_l, n_b, 5, dim))
-        mod_rows = jnp.concatenate([mod.reshape(n_l, n_b, 3, dim), bias], axis=2)
         qk = even_first(jnp.stack([q_scale, k_scale], axis=1).astype(F32), e)
         qk = jnp.broadcast_to(qk[:, :, None], (n_l, 2, 8, e))
 
@@ -546,15 +552,24 @@
             mine, tie = lax.optimization_barrier((w_local[l], tie))
             if l == 0:
                 x_cur = tie
-            got = lax.ppermute(mine, "tp", across)
-            half = block_forward(0, x_cur, mod_rows[l], w_own[l], b_rel[:2, l], *consts, (), l == 0, 0)
+            cuts = (0, n_j - 1, n_j) if l == 0 else (0, n_j)
+            bounds = list(zip(cuts[:-1], cuts[1:]))
+            arriving = [lax.ppermute(mine[lo:hi], "tp", across) for lo, hi in bounds]
+            half = block_forward(0, 0, False, x_cur, mod_rows[l], w_own[l], b_rel[:2, l], *consts, (), l == 0, 0)
             x_t = half[4] if l == 0 else x_cur
-            got, h_t = lax.optimization_barrier((got, half[3]))
-            tie = got
-            w_other = (got, lax.ppermute(got, "tp", peer_core))
-            y, o, lse, branch, x_cur = block_forward(1, x_t, mod_rows[l], w_other, b_rel[2:, l], *consts, (*half[:3], h_t, half[-1]), False, n_tp * (l == n_l - 1))
+            y, o, lse, h_t = half[:4]
+            z = half[-1]
+            others = []
+            for got, (lo, hi) in zip(arriving, bounds):
+                end = hi == n_j
+                got, z = lax.optimization_barrier((got, z))
+                tie = got
+                others.append((lo, hi - lo, (got, lax.ppermute(got, "tp", peer_core))))
+                out = block_forward(1, lo, end, x_t, mod_rows[l], others[-1][-1], b_rel[2:, l], *consts, (y, o, lse, h_t, z), False, n_tp * (end and l == n_l - 1))
+                y, o, lse, z = out[:4]
+            branch, x_cur = out[3:]
             saved.append((x_t, y, o, lse, h_t, branch))
-            ws.append((*w_own[l], *w_other))
+            ws.append(others)
         d_late, tie = lax.optimization_barrier((d_out, tie))
         g_tok = swap(d_late.reshape(n_tp, n_b, s_own, dim))
         x_out = swap(x_cur)
@@ -568,8 +583,8 @@
             if l == 0:
                 d_br, x_out = lax.optimization_barrier((d_br, x_out))
             d_hs, d_qk, gb, gw = [], 0.0, [], []
-            for j, width in ((0, n_j),) if l else ((0, n_j - 1), (n_j - 1, 1)):
-                keep, send, gb_j, dqk_j, dh_j = block_backward(j, width, d_br, h_t, ws[l], qk[l], cos_t, sin_t, y, o, lse)
+            for j, width, w_other in ws[l]:
+                keep, send, gb_j, dqk_j, dh_j = block_backward(j, width, d_br, h_t, (*w_own[l], *w_other), qk[l], cos_t, sin_t, y, o, lse)
                 d_hs.append(dh_j)
                 d_qk = d_qk + dqk_j
                 gb.append(gb_j)

time: 908 us -> 896 us (0.987)
  waiting for transfers between devices: 190 us -> 175 us
    ppermute x4 -> x6, waiting for transfers between devices: 29 us -> 14.5 us  [the longest x3 11.3 us: device_step(): arriving = [lax.ppermute(mine[lo:hi], 'tp', across) for lo, hi in bounds]]
    pallas_call x4 -> x5, Pallas kernels: 191 us -> 198 us  [block_forward(): pl.pallas_call(functools.partial(fwd_kernel, e, first, last, token_in, to...]
  transfers between devices with their start and end apart: 17 -> 19, of which waited for: 5 -> 6; matrix products, arithmetic and copies ran while one was open for 5% -> 6% of each run, Pallas kernels for 63% -> 64%
where the time goes in v5:
time: 896 us; the launch traced here: 892 us
  Pallas kernels  574 us (64%)
  waiting for transfers between devices  175 us (20%)
  blocking collectives  34.9 us (4%)
  other arithmetic  33.9 us (4%)
  starting transfers between devices  30.5 us (3%)
  local copies, waits for them, and re-layouts  30.4 us (3%)
  matrix products  12.3 us (1%)
    pallas_call x3, Pallas kernels, block_backward(): pl.pallas_call(functools.partial(bwd_kernel, e), grid=(n + 1,), in_specs=...  335 us
    pallas_call x5, Pallas kernels, block_forward(): pl.pallas_call(functools.partial(fwd_kernel, e, first, last, token_in, to...  198 us
    all_to_all x5, waiting for transfers between devices, swap(): return lax.all_to_all(arr, 'tp', 0, 0)  85.2 us
    ppermute x3, waiting for transfers between devices, device_step(): far = lax.ppermute(leaving, 'tp', across)  75.3 us
    all_gather x1, blocking collectives, device_step(): small_all = lax.all_gather(small_in, 'tp', axis=0, tiled=False)  34.9 us
    pallas_call x3, Pallas kernels, edge(): pl.pallas_call(functools.partial(edge_kernel, len(exit_args[2]) if exit_a...  33.4 us
    all_to_all x5, starting transfers between devices, swap(): return lax.all_to_all(arr, 'tp', 0, 0)  22.1 us
  transfers between devices with their start and end apart: 19, of which 6 were waited for; matrix products, arithmetic and copies ran while one was open for 6% of the time, Pallas kernels for 64%

profile of v5, /device:TPU:0, one launch (start us, length us, event | category | flops | bytes accessed | tf_op | source)
XLA Modules:
  0.0 892.3 jit_solution(8375911096457753547)
XLA Ops:
  0.7 3.3 slice_bitcast_fusion
  4.1 1.2 convert_bitcast_fusion.1
  5.3 2.0 pad_maximum_fusion.1.refs_1_.wa0_ref
  8.1 4.7 all-to-all-start
  13.4 4.0 fusion.7
  18.0 34.9 %all-gather.1 = f32[4,1,19072]{2,1,0:T(1,128)S(1)} all-gather(f32[1,1,19072]{2,1,0:T(1,128)S(1)} %reshape.235), channel_id=2, replica_groups=mesh['dp'=4,'tp'=4] {'tp'}, dimensions={0}, use_global_device_ids=true | all-gather | bytes 381440 | tf_op jit(solution)/shard_map/all_gather | solution.py:532
  55.8 3.2 slice.179
  60.2 48.1 %block_fwd.5 = (f32[2,2,2,3,448,1024]{5,4,3,2,1,0:T(8,128)}, bf16[2,2,2,3,64,1024]{5,4,3,2,1,0:T(8,128)(2,1)}, f32[2,2,3,2,1024]{4,3,2,1,0:T(2,128)}, bf16[2,768...) custom-call(f32[2,8,768]{2,1,0:T(8,128)} %get-tuple-element.139.refs_0_.refs_4_.refs_2_, ...), custom_call_target="tpu_custom_call" | custom-call | flops 27380416512 | bytes 10000000 | tf_op jit(solution)/shard_map/block_fwd/pallas_call | solution.py:429
  108.3 4.5 collective-permute-done.1.refs_1_.wa1_ref
  112.8 2.8 convert_bitcast_fusion.2
  115.7 2.0 pad_maximum_fusion.refs_1_.wa0_ref
  118.2 2.4 slice.177
  121.5 33.8 %block_fwd.6 = (f32[2,2,2,3,448,1024]{5,4,3,2,1,0:T(8,128)}, bf16[2,2,2,3,64,1024]{5,4,3,2,1,0:T(8,128)(2,1)}, f32[2,2,3,2,1024]{4,3,2,1,0:T(2,128)}, f32[2,768,1024]{2,1,0:T(8,128)}) custom-call(f32[2,8,768]{2,1,0:T(8,128)} %get-tuple-element.139.refs_0_.refs_4_.refs_2_, ...), custom_call_target="tpu_custom_call", output_to_operand_aliasing={{0}: (10, {}), {1}: (11, {}), {2}: (12, {})} | custom-call | flops 18253611008 | bytes 10000000 | tf_op jit(solution)/shard_map/block_fwd/pallas_call | solution.py:429
  155.3 1.8 collective-permute-start.4
  157.2 1.3 collective-permute-done.6.refs_2_.wb1_ref
  158.5 20.5 %block_fwd.7 = (f32[2,2,2,3,448,1024]{5,4,3,2,1,0:T(8,128)}, bf16[2,2,2,3,64,1024]{5,4,3,2,1,0:T(8,128)(2,1)}, f32[2,2,3,2,1024]{4,3,2,1,0:T(2,128)}, f32[2,768,1024]{2,1,0:T(8,128)}, bf16[2,768,1024]{2,1,0:T(8,128)(2,1)}) custom-call(f32[2,8,768]{2,1,0:T(8,128)} %get-tuple-element.139.refs_0_.refs_4_.r, ...), custom_call_target="tpu_custom_call", output_to_operand_aliasing={{0}: (10, {}), {1}: (11, {}), {2}: (12, {})} | custom-call | flops 9126805504 | bytes 10000000 | tf_op jit(solution)/shard_map/block_fwd/pallas_call | solution.py:429
  180.3 47.5 %block_fwd.8 = (f32[2,2,2,3,448,1024]{5,4,3,2,1,0:T(8,128)}, bf16[2,2,2,3,64,1024]{5,4,3,2,1,0:T(8,128)(2,1)}, f32[2,2,3,2,1024]{4,3,2,1,0:T(2,128)}, bf16[2,768,1024]{2,1,0:T(8,128)(2,1)}, f32[2,768,1024]{2,1,0:T(8,128)}) custom-call(f32[2,8,768]{2,1,0:T(8,128)} %get-tuple-element.138.refs_0_.refs_1_.refs_2_, ...), custom_call_target="tpu_custom_call" | custom-call | flops 27380416512 | bytes 10000000 | tf_op jit(solution)/shard_map/block_fwd/pallas_call | solution.py:429
  227.8 6.8 collective-permute-done.4.refs_1_.wa1_ref
  234.6 4.6 all-to-all-start.1
  239.3 1.9 collective-permute-done.7.refs_2_.wb1_ref
  241.8 48.0 %block_fwd.9 = (f32[2,2,2,3,448,1024]{5,4,3,2,1,0:T(8,128)}, bf16[2,2,2,3,64,1024]{5,4,3,2,1,0:T(8,128)(2,1)}, f32[2,2,3,2,1024]{4,3,2,1,0:T(2,128)}, f32[2,768,1024]{2,1,0:T(8,128)}, bf16[4,2,256,768]{3,2,1,0:T(8,128)(2,1)}) custom-call(f32[2,8,768]{2,1,0:T(8,128)} %get-tuple-element.138.refs_0_.refs_1, ...), custom_call_target="tpu_custom_call", output_to_operand_aliasing={{0}: (10, {}), {1}: (11, {}), {2}: (12, {})} | custom-call | flops 27380416512 | bytes 10000000 | tf_op jit(solution)/shard_map/block_fwd/pallas_call | solution.py:429
  289.8 4.7 all-to-all-start.2
  294.5 8.4 edge.3
  303.0 160.3 %block_bwd.3 = (bf16[2,3,768,768]{3,2,1,0:T(8,128)(2,1)}, bf16[2,3,768,768]{3,2,1,0:T(8,128)(2,1)}, f32[2,2,3,1,448]{4,3,2,1,0:T(1,128)}, f32[2,64,1]{2,1,0:T(8,128)}, f32[2,768,1024]{2,1,0:T(8,128)}) custom-call(bf16[2,768,1024]{2,1,0:T(8,128)(2,1)} %get-tuple-element.102.dbr_ref, bf16[2,768,1024]{2,1,0:T(8,128)(2,1)} %get-tuple-element.95.refs_8_.h_ref, ...), custom_call_target="tpu_custom_call" | custom-call | flops 122406567936 | bytes 10000000 | tf_op jit(solution)/shard_map/block_bwd/pallas_call | solution.py:458
  464.6 12.8 %edge.4 = (bf16[2,768,1024]{2,1,0:T(8,128)(2,1)}, bf16[2,768,1024]{2,1,0:T(8,128)(2,1)}, f32[2,8,768]{2,1,0:T(8,128)}) custom-call(bf16[2,768,1024]{2,1,0:T(8,128)(2,1)} %get-tuple-element.101.refs_0_, bf16[2,768,1024]{2,1,0:T(8,128)(2,1)} %get-tuple-element.91.refs_7_.refs_1_, f32[2,8,768]{2,1,0:T(8,128)} %get-tuple-element.138.refs_0_.refs_1_.refs_2_, ...), custom_call_target="tpu_custom_call" | custom-call | flops 1000000 | bytes 10000000 | tf_op jit(solution)/shard_map/edge/pallas_call | solution.py:359
  478.2 0.9 fusion.34
  479.4 0.9 fusion.33
  480.3 111.3 %block_bwd.4 = (bf16[2,2,768,768]{3,2,1,0:T(8,128)(2,1)}, bf16[2,2,768,768]{3,2,1,0:T(8,128)(2,1)}, f32[2,2,2,1,448]{4,3,2,1,0:T(1,128)}, f32[2,64,1]{2,1,0:T(8,128)}, f32[2,768,1024]{2,1,0:T(8,128)}) custom-call(bf16[2,768,1024]{2,1,0:T(8,128)(2,1)} %get-tuple-element.112.dbr_ref, bf16[2,768,1024]{2,1,0:T(8,128)(2,1)} %get-tuple-element.79.refs_8_.h_ref, ...), custom_call_target="tpu_custom_call" | custom-call | flops 81604378624 | bytes 10000000 | tf_op jit(solution)/shard_map/block_bwd/pallas_call | solution.py:458
  591.7 63.3 %block_bwd.5 = (bf16[2,1,768,768]{3,2,1,0:T(8,128)(2,1)}, bf16[2,1,768,768]{3,2,1,0:T(8,128)(2,1)}, f32[2,2,1,1,448]{4,3,2,1,0:T(1,128)}, f32[2,64,1]{2,1,0:T(8,128)}, f32[2,768,1024]{2,1,0:T(8,128)}) custom-call(bf16[2,768,1024]{2,1,0:T(8,128)(2,1)} %get-tuple-element.112.dbr_ref, bf16[2,768,1024]{2,1,0:T(8,128)(2,1)} %get-tuple-element.79.refs_8_.h_ref, ...), custom_call_target="tpu_custom_call" | custom-call | flops 40802189312 | bytes 10000000 | tf_op jit(solution)/shard_map/block_bwd/pallas_call | solution.py:458
  655.5 12.1 %edge.5 = (bf16[4,2,256,768]{3,2,1,0:T(8,128)(2,1)}, f32[2,8,768]{2,1,0:T(8,128)}) custom-call(bf16[2,768,1024]{2,1,0:T(8,128)(2,1)} %get-tuple-element.111.refs_0_, bf16[2,768,1024]{2,1,0:T(8,128)(2,1)} %get-tuple-element.78.refs_7_.refs_1_, f32[2,8,768]{2,1,0:T(8,128)} %get-tuple-element.139.refs_0_.refs_4_.refs_2_, ...), custom_call_target="tpu_custom_call" | custom-call | flops 1000000 | bytes 10000000 | tf_op jit(solution)/shard_map/edge/pallas_call | solution.py:359
  669.3 0.8 broadcast_in_dim.56
  670.1 3.5 all-to-all-start.4
  673.6 5.7 fusion.5
  679.3 2.0 collective-permute-start.13
  681.3 4.7 all-to-all-start.3
  685.9 4.5 fusion.10
  690.4 2.0 collective-permute-start.9
  692.4 2.6 fusion.22
  698.0 7.7 wmod_grad.1
  707.5 85.1 %all-to-all-done.3 = bf16[4,2,256,768]{3,2,1,0:T(8,128)(2,1)} async-done(((bf16[4,2,256,768]{3,2,1,0:T(8,128)(2,1)}), bf16[4,2,256,768]{3,2,1,0:T(8,128)(2,1)}, u32[]{:S(2)}, u32[]{:S(2)}) %all-to-all-start.3) | async-done | bytes 3145760 | tf_op jit(solution)/shard_map/all_to_all | solution.py:510
  792.7 75.3 %collective-permute-done.11 = bf16[1,768,768]{2,1,0:T(8,128)(2,1)} collective-permute-done((bf16[1,768,768]{2,1,0:T(8,128)(2,1)}, bf16[1,768,768]{2,1,0:T(8,128)(2,1)}, u32[]{:S(2)}, u32[]{:S(2)}) %collective-permute-start.11) | collective-permute-done | bytes 1179680 | tf_op jit(solution)/shard_map/ppermute | solution.py:593
  868.0 2.6 fusion.11
  870.6 4.1 fusion.1
  875.0 3.8 fusion.6
  878.8 1.8 pad_maximum_fusion.2
  880.6 4.0 convert_bitcast_fusion
  884.6 3.8 copy.96
  888.4 3.8 copy.97
  (155 shorter events, 19.2 us)
Async XLA Ops:
  0.6 16.9 %copy-start = (bf16[2,3,448]{2,0,1:T(2,128)(2,1)S(1)}, bf16[2,3,448]{2,0,1:T(2,128)(2,1)}, u32[]{:S(2)}) copy-start(bf16[2,3,448]{2,0,1:T(2,128)(2,1)} %param.21) | copy-start | bytes 16132
  0.7 3.3 copy-start.4
  0.7 3.4 copy-start.18
  7.3 5.4 copy-start.13
  7.3 5.4 copy-start.12
  7.3 51.7 %collective-permute-start.2 = (bf16[3,768,768]{2,1,0:T(8,128)(2,1)}, bf16[3,768,768]{2,1,0:T(8,128)(2,1)}, u32[]{:S(2)}, u32[]{:S(2)}) collective-permute-start(bf16[3,768,768]{2,1,0:T(8,128)(2,1)} %pad_maximum_fusion.1.refs_1_.wa0_ref), channel_id=1, source_target_pairs={{0,1},{1,0},{2,3},{3,2},{4,5},{5,4},{6,7},{7,6},{8,9},{9,8},{10,11... | collective-permute-start | bytes 10616840 | tf_op jit(solution)/shard_map/ppermute | solution.py:538
  8.1 47.7 %all-to-all-start = ((bf16[4,2,256,768]{3,2,1,0:T(8,128)(2,1)}), bf16[4,2,256,768]{3,2,1,0:T(8,128)(2,1)}, u32[]{:S(2)}, u32[]{:S(2)}) async-start(bf16[4,2,256,768]{3,2,1,0:T(8,128)(2,1)} %bitcast.7), calls=%async_computation | async-start | bytes 6291456 | tf_op jit(solution)/shard_map/all_to_all | solution.py:510
  12.8 0.6 copy-start.8
  13.4 4.1 copy-start.9
  13.4 4.1 copy-start.10
  13.4 4.5 copy-start.15
  17.4 37.1 %copy-start.16 = (bf16[2,64]{1,0:T(2,128)(2,1)S(1)}, bf16[2,64]{1,0:T(2,128)(2,1)}, u32[]{:S(2)}) copy-start(bf16[2,64]{1,0:T(2,128)(2,1)} %param.22) | copy-start | bytes 772
  17.4 37.3 %copy-start.17 = (bf16[2,64]{1,0:T(2,128)(2,1)S(1)}, bf16[2,64]{1,0:T(2,128)(2,1)}, u32[]{:S(2)}) copy-start(bf16[2,64]{1,0:T(2,128)(2,1)} %param.23) | copy-start | bytes 772
  59.0 53.8 %collective-permute-start.1 = (bf16[2,768,768]{2,1,0:T(8,128)(2,1)}, bf16[2,768,768]{2,1,0:T(8,128)(2,1)}, u32[]{:S(2)}, u32[]{:S(2)}) collective-permute-start(bf16[2,768,768]{2,1,0:T(8,128)(2,1)} %slice.179), channel_id=1, source_target_pairs={{0,2},{1,3},{2,0},{3,1},{4,6},{5,7},{6,4},{7,5},{8,10},{9,11},{10,... | collective-permute-start | bytes 7077896 | tf_op jit(solution)/shard_map/ppermute | solution.py:557
  108.3 7.3 copy-start.2
  112.8 8.0 collective-permute-start.3
  117.7 61.4 %collective-permute-start.5 = (bf16[3,768,768]{2,1,0:T(8,128)(2,1)}, bf16[3,768,768]{2,1,0:T(8,128)(2,1)}, u32[]{:S(2)}, u32[]{:S(2)}) collective-permute-start(bf16[3,768,768]{2,1,0:T(8,128)(2,1)} %pad_maximum_fusion.refs_1_.wa0_ref), channel_id=1, source_target_pairs={{0,1},{1,0},{2,3},{3,2},{4,5},{5,4},{6,7},{7,6},{8,9},{9,8},{10,11... | collective-permute-start | bytes 10616840 | tf_op jit(solution)/shard_map/ppermute | solution.py:538
  120.5 34.7 %collective-permute-start = (bf16[1,768,768]{2,1,0:T(8,128)(2,1)}, bf16[1,768,768]{2,1,0:T(8,128)(2,1)}, u32[]{:S(2)}, u32[]{:S(2)}) collective-permute-start(bf16[1,768,768]{2,1,0:T(8,128)(2,1)} %slice.177), channel_id=1, source_target_pairs={{0,2},{1,3},{2,0},{3,1},{4,6},{5,7},{6,4},{7,5},{8,10},{9,11},{10,... | collective-permute-start | bytes 3538952 | tf_op jit(solution)/shard_map/ppermute | solution.py:557
  155.3 3.2 collective-permute-start.6
  155.3 79.3 %collective-permute-start.4 = (bf16[3,768,768]{2,1,0:T(8,128)(2,1)}, bf16[3,768,768]{2,1,0:T(8,128)(2,1)}, u32[]{:S(2)}, u32[]{:S(2)}) collective-permute-start(bf16[3,768,768]{2,1,0:T(8,128)(2,1)} %pad_maximum_fusion.refs_1_.wa0_ref), channel_id=1, source_target_pairs={{0,2},{1,3},{2,0},{3,1},{4,6},{5,7},{6,4},{7,5},{8,10},{9,11},{10,... | collective-permute-start | bytes 10616840 | tf_op jit(solution)/shard_map/ppermute | solution.py:557
  234.6 6.6 collective-permute-start.7
  234.6 55.2 %all-to-all-start.1 = ((bf16[4,2,256,768]{3,2,1,0:T(8,128)(2,1)}), bf16[4,2,256,768]{3,2,1,0:T(8,128)(2,1)}, u32[]{:S(2)}, u32[]{:S(2)}) async-start(bf16[4,2,256,768]{3,2,1,0:T(8,128)(2,1)} %bitcast.139), calls=%async_computation.1 | async-start | bytes 6291456 | tf_op jit(solution)/shard_map/all_to_all | solution.py:510
  289.8 190.4 %all-to-all-start.2 = ((bf16[4,2,256,768]{3,2,1,0:T(8,128)(2,1)}), bf16[4,2,256,768]{3,2,1,0:T(8,128)(2,1)}, u32[]{:S(2)}, u32[]{:S(2)}) async-start(bf16[4,2,256,768]{3,2,1,0:T(8,128)(2,1)} %get-tuple-element.109), calls=%async_computation.2 | async-start | bytes 6291456 | tf_op jit(solution)/shard_map/all_to_all | solution.py:510
  463.2 210.4 %collective-permute-start.12 = (bf16[2,3,768,768]{3,2,1,0:T(8,128)(2,1)}, bf16[2,3,768,768]{3,2,1,0:T(8,128)(2,1)}, u32[]{:S(2)}, u32[]{:S(2)}) collective-permute-start(bf16[2,3,768,768]{3,2,1,0:T(8,128)(2,1)} %get-tuple-element.133), channel_id=1, source_target_pairs={{0,1},{1,0},{2,3},{3,2},{4,5},{5,4},{6,7},{7,6},{8,9},{9,8},{10,11... | collective-permute-start | bytes 21233672 | tf_op jit(solution)/shard_map/ppermute | solution.py:591
  464.6 14.6 %copy-start.6 = (f32[2,64,1]{2,1,0:T(8,128)S(1)}, f32[2,64,1]{2,1,0:T(8,128)}, u32[]{:S(2)}) copy-start(f32[2,64,1]{2,1,0:T(8,128)} %get-tuple-element.126) | copy-start | bytes 1540
  591.6 94.3 %collective-permute-start.8 = (bf16[2,2,768,768]{3,2,1,0:T(8,128)(2,1)}, bf16[2,2,768,768]{3,2,1,0:T(8,128)(2,1)}, u32[]{:S(2)}, u32[]{:S(2)}) collective-permute-start(bf16[2,2,768,768]{3,2,1,0:T(8,128)(2,1)} %get-tuple-element.129), channel_id=1, source_target_pairs={{0,1},{1,0},{2,3},{3,2},{4,5},{5,4},{6,7},{7,6},{8,9},{9,8},{10,11... | collective-permute-start | bytes 14155784 | tf_op jit(solution)/shard_map/ppermute | solution.py:591
  655.0 37.4 %collective-permute-start.10 = (bf16[2,1,768,768]{3,2,1,0:T(8,128)(2,1)}, bf16[2,1,768,768]{3,2,1,0:T(8,128)(2,1)}, u32[]{:S(2)}, u32[]{:S(2)}) collective-permute-start(bf16[2,1,768,768]{3,2,1,0:T(8,128)(2,1)} %get-tuple-element.131), channel_id=1, source_target_pairs={{0,1},{1,0},{2,3},{3,2},{4,5},{5,4},{6,7},{7,6},{8,9},{9,8},{10,11... | collective-permute-start | bytes 7077896 | tf_op jit(solution)/shard_map/ppermute | solution.py:591
  655.5 13.0 %copy-start.5 = (f32[2,64,1]{2,1,0:T(8,128)S(1)}, f32[2,64,1]{2,1,0:T(8,128)}, u32[]{:S(2)}) copy-start(f32[2,64,1]{2,1,0:T(8,128)} %get-tuple-element.121) | copy-start | bytes 1540
  655.5 13.0 %copy-start.7 = (f32[2,64,1]{2,1,0:T(8,128)S(1)}, f32[2,64,1]{2,1,0:T(8,128)}, u32[]{:S(2)}) copy-start(f32[2,64,1]{2,1,0:T(8,128)} %get-tuple-element.122) | copy-start | bytes 1540
  655.5 13.2 %copy-start.11 = (f32[2,2,2,1,448]{4,3,2,1,0:T(1,128)S(1)}, f32[2,2,2,1,448]{4,3,2,1,0:T(1,128)}, u32[]{:S(2)}) copy-start(f32[2,2,2,1,448]{4,3,2,1,0:T(1,128)} %get-tuple-element.123) | copy-start | bytes 43012
  655.5 13.2 %copy-start.14 = (f32[2,2,1,1,448]{4,3,2,1,0:T(1,128)S(1)}, f32[2,2,1,1,448]{4,3,2,1,0:T(1,128)}, u32[]{:S(2)}) copy-start(f32[2,2,1,1,448]{4,3,2,1,0:T(1,128)} %get-tuple-element.124) | copy-start | bytes 21508
  670.1 11.1 %all-to-all-start.4 = ((f32[4,2,10880]{2,1,0:T(2,128)}), f32[4,2,10880]{2,1,0:T(2,128)S(1)}, u32[]{:S(2)}, u32[]{:S(2)}) async-start(f32[4,2,10880]{2,1,0:T(2,128)} %broadcast_in_dim.56), calls=%async_computation.4 | async-start | bytes 696320 | tf_op jit(solution)/shard_map/all_to_all | solution.py:510
  679.3 195.7 %collective-permute-start.13 = (bf16[3,768,768]{2,1,0:T(8,128)(2,1)}, bf16[3,768,768]{2,1,0:T(8,128)(2,1)}, u32[]{:S(2)}, u32[]{:S(2)}) collective-permute-start(bf16[3,768,768]{2,1,0:T(8,128)(2,1)} %fusion.5), channel_id=1, source_target_pairs={{0,2},{1,3},{2,0},{3,1},{4,6},{5,7},{6,4},{7,5},{8,10},{9,11},{10,... | collective-permute-start | bytes 10616840 | tf_op jit(solution)/shard_map/ppermute | solution.py:593
  681.3 111.4 %all-to-all-start.3 = ((bf16[4,2,256,768]{3,2,1,0:T(8,128)(2,1)}), bf16[4,2,256,768]{3,2,1,0:T(8,128)(2,1)}, u32[]{:S(2)}, u32[]{:S(2)}) async-start(bf16[4,2,256,768]{3,2,1,0:T(8,128)(2,1)} %get-tuple-element.118), calls=%async_computation.3 | async-start | bytes 6291456 | tf_op jit(solution)/shard_map/all_to_all | solution.py:510
  685.9 6.5 copy-start.3
  690.4 180.2 %collective-permute-start.9 = (bf16[2,768,768]{2,1,0:T(8,128)(2,1)}, bf16[2,768,768]{2,1,0:T(8,128)(2,1)}, u32[]{:S(2)}, u32[]{:S(2)}) collective-permute-start(bf16[2,768,768]{2,1,0:T(8,128)(2,1)} %fusion.10), channel_id=1, source_target_pairs={{0,2},{1,3},{2,0},{3,1},{4,6},{5,7},{6,4},{7,5},{8,10},{9,11},{10,... | collective-permute-start | bytes 7077896 | tf_op jit(solution)/shard_map/ppermute | solution.py:593
  695.0 173.0 %collective-permute-start.11 = (bf16[1,768,768]{2,1,0:T(8,128)(2,1)}, bf16[1,768,768]{2,1,0:T(8,128)(2,1)}, u32[]{:S(2)}, u32[]{:S(2)}) collective-permute-start(bf16[1,768,768]{2,1,0:T(8,128)(2,1)} %fusion.22), channel_id=1, source_target_pairs={{0,2},{1,3},{2,0},{3,1},{4,6},{5,7},{6,4},{7,5},{8,10},{9,11},{10,... | collective-permute-start | bytes 3538952 | tf_op jit(solution)/shard_map/ppermute | solution.py:593
  868.0 7.0 slice-start
  870.6 4.5 slice-start.1
  878.8 1.8 copy-start.19
  884.6 7.5 copy-start.1
